TPU v7x, 256 devices: a whole 4x4x8 slice. The times are simulated.
256 devices in a mesh: dp: 8 (over z_lo, core), ctx: 32 (over x, y, z_hi).
Axes of the slice: x: 4, y: 4, z: 8 (z_hi: 2, z_lo: 4; z = z_hi * 4 + z_lo), core: 2. Of those that a mesh axis runs over, the one named last changes fastest.
Arguments:
- doc_lengths: int32 [64], P('dp'), parts along dimension 0, may hold values from 1 to 1024, 4096 in all
- assignment: int32 [1024], P('dp'), parts along dimension 0, may hold values from 0 to 127, each once
- queries: bfloat16 [32768, 4096], P(('dp', 'ctx')), parts along dimension 0, may hold values from -6 to 6
- key_state_rows: bfloat16 [32768, 512], P(('dp', 'ctx')), parts along dimension 0, may hold values from -6 to 6
- value_state_rows: bfloat16 [32768, 512], P(('dp', 'ctx')), parts along dimension 0, may hold values from -6 to 6
- out_grad: bfloat16 [32768, 4096], P(('dp', 'ctx')), parts along dimension 0, may hold values from -6 to 6
Outputs:
- attention_out: bfloat16 [32768, 4096], P(('dp', 'ctx')), parts along dimension 0
- query_grad: bfloat16 [32768, 4096], P(('dp', 'ctx')), parts along dimension 0
- key_gradient: bfloat16 [32768, 512], P(('dp', 'ctx')), parts along dimension 0
- value_gradient: bfloat16 [32768, 512], P(('dp', 'ctx')), parts along dimension 0
There are 8 independent parts, one for each index of `dp`. A program takes and returns all parts, laid end to end along the dimension named above; each array names one. Nothing has to cross between parts.
Inputs may be any that keep to these rules, and one draw needn't show every extreme that they name: `assignment`: each of 0 to 127 once.
All inputs are finite; a program needn't handle non-finite values.
Results may differ from a plain program's by a relative error of at most 0.015.
Values may be sent and summed in bfloat16 or wider, within the bound.
No kernel may reach another device: no remote copies, remote signals or barrier semaphores. Data moves between devices by JAX's collectives and lax.ppermute only.
A program may use at most 128 MiB of HBM per device.

v0:
```python
import jax
import jax.numpy as jnp
from jax import lax
from jax.sharding import Mesh
from jax.sharding import PartitionSpec as P

BLK = 32
MOST = 1024
HEAD_SIZE = 128
CTX = ("ctx_0", "ctx_1", "ctx_2")
DP_CTX = ("dp", "ctx_0", "ctx_1", "ctx_2")


def in_one_piece(arrays, axis, dim, along):
    widths = [a.shape[along] for a in arrays]
    both = jnp.concatenate(arrays, axis=along)
    whole = lax.all_gather(both, axis, axis=dim, tiled=True)
    return tuple(jnp.split(whole, [sum(widths[:k]) for k in range(1, len(widths))], axis=along))


def own_rows(terms, axes):
    total = terms.astype(jnp.bfloat16)
    for axis in axes:
        total = lax.psum_scatter(total, axis, scatter_dimension=0, tiled=True)
    return total.astype(jnp.float32)


def body(doc_lengths, assignment, queries, key_state_rows, value_state_rows, out_grad):
    row_count = queries.shape[0]
    head_width = key_state_rows.shape[1]
    kv_heads = head_width // HEAD_SIZE
    group_width = queries.shape[1] // head_width
    block_count = row_count // BLK
    span_rows = MOST + BLK
    blocks_all = assignment.shape[0]
    score_scale = HEAD_SIZE ** (-0.5)
    doc_bounds = jnp.cumsum(doc_lengths)
    slot_of = (
        jnp.zeros((blocks_all,), jnp.int32)
        .at[assignment]
        .set(jnp.arange(blocks_all, dtype=jnp.int32))
    )
    own_blocks = lax.dynamic_slice_in_dim(
        assignment, lax.axis_index(CTX) * block_count, block_count
    )
    query_blocks = queries.reshape(block_count, BLK, kv_heads, group_width, HEAD_SIZE)
    grad_blocks = out_grad.reshape(block_count, BLK, kv_heads, group_width, HEAD_SIZE)

    def arrange(gathered):
        padding = jnp.zeros((span_rows, head_width), jnp.bfloat16)
        ordered = []
        for gathered_rows in gathered:
            blocked = gathered_rows.reshape(blocks_all, BLK, head_width)[slot_of]
            ordered.append(
                jnp.concatenate([padding, blocked.reshape(blocks_all * BLK, head_width)], axis=0)
            )
        return (ordered[0], ordered[1])

    def layout(seq_block):
        block_end = (seq_block + 1) * BLK
        key_place = block_end - span_rows + jnp.arange(span_rows, dtype=jnp.int32)
        query_place = seq_block * BLK + jnp.arange(BLK, dtype=jnp.int32)
        key_doc = jnp.sum((doc_bounds[None, :] <= key_place[:, None]).astype(jnp.int32), axis=1)
        query_doc = jnp.sum((doc_bounds[None, :] <= query_place[:, None]).astype(jnp.int32), axis=1)
        allowed = (
            (key_place[None, :] >= 0)
            & (key_doc[None, :] == query_doc[:, None])
            & (key_place[None, :] <= query_place[:, None])
        )
        return (block_end, allowed)

    def windows(padded_pair, block_end):
        window_keys = lax.dynamic_slice_in_dim(padded_pair[0], block_end, span_rows, 0).reshape(
            span_rows, kv_heads, HEAD_SIZE
        )
        window_values = lax.dynamic_slice_in_dim(padded_pair[1], block_end, span_rows, 0).reshape(
            span_rows, kv_heads, HEAD_SIZE
        )
        return (window_keys, window_values)

    padded_pair = arrange(in_one_piece((key_state_rows, value_state_rows), CTX, 0, 1))

    def forward_block(slices):
        block_query, seq_block = slices
        block_end, allowed = layout(seq_block)
        window_keys, window_values = windows(padded_pair, block_end)
        scores = (
            jnp.einsum(
                "qgjd,kgd->gjqk", block_query, window_keys, preferred_element_type=jnp.float32
            )
            * score_scale
        )
        masked = jnp.where(allowed, scores, -jnp.inf)
        row_top = jnp.max(masked, axis=-1, keepdims=True)
        log_total = row_top + jnp.log(jnp.sum(jnp.exp(masked - row_top), axis=-1, keepdims=True))
        attention = jnp.where(allowed, jnp.exp(scores - log_total), 0.0).astype(jnp.bfloat16)
        output = jnp.einsum(
            "gjqk,kgd->qgjd", attention, window_values, preferred_element_type=jnp.float32
        )
        return (output.astype(jnp.bfloat16), log_total)

    out_blocks, total_blocks = lax.map(forward_block, (query_blocks, own_blocks))
    padded_pair = arrange(in_one_piece((key_state_rows, value_state_rows), CTX, 0, 1))

    def backward_step(buffers, slices):
        block_query, block_grad, block_out, log_total, seq_block = slices
        block_end, allowed = layout(seq_block)
        window_keys, window_values = windows(padded_pair, block_end)
        scores = (
            jnp.einsum(
                "qgjd,kgd->gjqk", block_query, window_keys, preferred_element_type=jnp.float32
            )
            * score_scale
        )
        attention = jnp.where(allowed, jnp.exp(scores - log_total), 0.0)
        attention_b = attention.astype(jnp.bfloat16)
        row_delta = jnp.sum(block_grad.astype(jnp.float32) * block_out.astype(jnp.float32), axis=-1)
        row_delta = jnp.transpose(row_delta, (1, 2, 0))[..., None]
        grad_weights = jnp.einsum(
            "qgjd,kgd->gjqk", block_grad, window_values, preferred_element_type=jnp.float32
        )
        dscore = (attention * (grad_weights - row_delta) * score_scale).astype(jnp.bfloat16)
        query_term = jnp.einsum(
            "gjqk,kgd->qgjd", dscore, window_keys, preferred_element_type=jnp.float32
        ).astype(jnp.bfloat16)
        key_term = jnp.einsum(
            "gjqk,qgjd->kgd", dscore, block_query, preferred_element_type=jnp.float32
        )
        value_term = jnp.einsum(
            "gjqk,qgjd->kgd", attention_b, block_grad, preferred_element_type=jnp.float32
        )
        key_sum, value_sum = buffers
        key_sum = lax.dynamic_update_slice_in_dim(
            key_sum,
            lax.dynamic_slice_in_dim(key_sum, block_end, span_rows, 0) + key_term,
            block_end,
            0,
        )
        value_sum = lax.dynamic_update_slice_in_dim(
            value_sum,
            lax.dynamic_slice_in_dim(value_sum, block_end, span_rows, 0) + value_term,
            block_end,
            0,
        )
        return ((key_sum, value_sum), query_term)

    empty_sums = (
        jnp.zeros((blocks_all * BLK + span_rows, kv_heads, HEAD_SIZE), jnp.float32),
        jnp.zeros((blocks_all * BLK + span_rows, kv_heads, HEAD_SIZE), jnp.float32),
    )
    sums, query_terms = lax.scan(
        backward_step, empty_sums, (query_blocks, grad_blocks, out_blocks, total_blocks, own_blocks)
    )

    def to_slots(buffer):
        trimmed = buffer[span_rows:].reshape(blocks_all, BLK, head_width)
        return trimmed[assignment].reshape(blocks_all * BLK, head_width)

    key_slots = to_slots(sums[0])
    value_slots = to_slots(sums[1])
    both_slots = jnp.concatenate([key_slots, value_slots], axis=1)
    reduced = own_rows(both_slots, CTX)
    key_gradient = reduced[:, :head_width]
    value_gradient = reduced[:, head_width:]
    attention_out = out_blocks.reshape(row_count, -1)
    query_grad = query_terms.reshape(row_count, -1)
    return (
        attention_out,
        query_grad,
        key_gradient.astype(jnp.bfloat16),
        value_gradient.astype(jnp.bfloat16),
    )


def solution(mesh):
    finer = Mesh(mesh.devices.reshape(mesh.shape["dp"], 4, 4, 2), ("dp", "ctx_0", "ctx_1", "ctx_2"))
    return jax.shard_map(
        body,
        mesh=finer,
        in_specs=(
            P("dp"),
            P("dp"),
            P(DP_CTX, None),
            P(DP_CTX, None),
            P(DP_CTX, None),
            P(DP_CTX, None),
        ),
        out_specs=(P(DP_CTX, None), P(DP_CTX, None), P(DP_CTX, None), P(DP_CTX, None)),
        check_vma=False,
    )
```

profile of v0, /device:TPU:32, one launch (start us, length us, event | category | flops | bytes accessed | tf_op | source)
XLA Modules:
  0.0 584.6 jit_solution(1360740804077668440)
XLA Ops:
  14.5 152.6 %all-gather.2.cloned.1.call-done = bf16[4096,1024]{1,0:T(8,128)(2,1)} async-done(((bf16[128,1024]{1,0:T(8,128)(2,1)}), bf16[4096,1024]{1,0:T(8,128)(2,1)}) %all-gather.2.cloned.1.call-update) | async-done | bytes 8388624 | tf_op jit(solution)/shard_map/all_gather | solution.py:17
  167.1 5.7 fusion.47
  172.8 4.9 gather_fusion
  177.8 5.0 gather_fusion.1
  182.7 5.0 concatenate.17
  190.5 55.1 %while.30 = (s32[]{:T(128)}, bf16[4,32,4,8,128]{4,1,3,2,0:T(8,128)(2,1)}, f32[4,4,8,32,1]{3,2,1,4,0:T(8,128)S(1)}, s32[4]{0:T(128)S(1)}, bf16[5152,512]{1,0:T(8,...) while((s32[]{:T(128)}, ...), condition=%wide.region_7.8_spmd, body=%wide.region_2.7_spmd.sunk | while | flops 563673664 | bytes 42250900 | solution.py:102
  200.2 4.0 fusion.72
  214.0 4.0 fusion.72
  227.8 4.0 fusion.72
  241.6 4.0 fusion.72
  245.6 4.7 broadcast.122
  250.3 4.5 broadcast.122.clone
  254.8 96.2 %while.31 = (s32[]{:T(128)}, f32[5152,4,128]{2,0,1:T(8,128)}, f32[5152,4,128]{2,0,1:T(8,128)}, bf16[4,32,4,8,128]{4,3,2,1,0:T(8,128)(2,1)}, s32[4]{0:T(128)S(1)}...) while((s32[]{:T(128)}, f32[5152,4,128]{2,0,1:T(8,128)}, ...), condition=%wide.region_12.13_spmd, body=%wide.region_8.12_spmd.sunk | while | flops 1394670080 | bytes 57162964 | solution.py:151
  259.1 4.3 fusion.81
  269.3 4.1 fusion.84
  283.1 4.3 fusion.81
  293.3 4.1 fusion.84
  307.2 4.3 fusion.81
  317.3 4.1 fusion.84
  321.4 4.0 fusion.85
  331.2 4.3 fusion.81
  341.4 4.2 fusion.84
  355.0 20.5 %copy.34 = bf16[4096,4,128]{2,1,0:T(4,128)(2,1)} copy(bf16[4096,4,128]{2,0,1:T(8,128)(2,1)S(1)} %slice.14) | data formatting | bytes 8388608 | tf_op jit(solution)/shard_map/slice | solution.py:156
  375.4 7.2 %reshape.197 = bf16[128,32,512]{2,1,0:T(8,128)(2,1)} reshape(bf16[4096,4,128]{2,1,0:T(4,128)(2,1)} %copy.34) | data formatting | bytes 8388608 | tf_op jit(solution)/shard_map/reshape | solution.py:156
  386.6 20.4 %copy.35 = bf16[4096,4,128]{2,1,0:T(4,128)(2,1)} copy(bf16[4096,4,128]{2,0,1:T(8,128)(2,1)S(1)} %slice.15) | data formatting | bytes 8388608 | tf_op jit(solution)/shard_map/slice | solution.py:156
  407.0 7.2 %reshape.199 = bf16[128,32,512]{2,1,0:T(8,128)(2,1)} reshape(bf16[4096,4,128]{2,1,0:T(4,128)(2,1)} %copy.35) | data formatting | bytes 8388608 | tf_op jit(solution)/shard_map/reshape | solution.py:156
  414.2 5.0 gather_fusion.2
  419.2 5.0 gather_fusion.3
  424.2 7.9 %pad_maximum_fusion = bf16[4096,1024]{1,0:T(8,128)(2,1)} fusion(bf16[4096,512]{1,0:T(8,128)(2,1)} %bitcast.185, bf16[4096,512]{1,0:T(8,128)(2,1)} %bitcast.183), kind=kLoop, calls=%fused_computation.76 | loop fusion | flops 16777216 | bytes 16777216 | tf_op jit(solution)/shard_map/concatenate | solution.py:161
  432.1 78.9 %reduce-scatter.4.cloned.1.call-done = bf16[1024,1024]{1,0:T(8,128)(2,1)} async-done(((bf16[4096,1024]{1,0:T(8,128)(2,1)}), bf16[1024,1024]{1,0:T(8,128)(2,1)}) %reduce-scatter.4.cloned.1.call-update) | async-done | bytes 2097168 | tf_op jit(solution)/shard_map/reduce_scatter | solution.py:24
  511.0 34.6 %reduce-scatter.6.cloned.1.call-done = bf16[256,1024]{1,0:T(8,128)(2,1)} async-done(((bf16[1024,1024]{1,0:T(8,128)(2,1)}), bf16[256,1024]{1,0:T(8,128)(2,1)}) %reduce-scatter.6.cloned.1.call-update) | async-done | bytes 524304 | tf_op jit(solution)/shard_map/reduce_scatter | solution.py:24
  548.6 27.8 %reduce-scatter.8.cloned.1.call-done = bf16[128,1024]{1,0:T(8,128)(2,1)} async-done(((bf16[256,1024]{1,0:T(8,128)(2,1)}), bf16[128,1024]{1,0:T(8,128)(2,1)}) %reduce-scatter.8.cloned.1.call-update) | async-done | bytes 262160 | tf_op jit(solution)/shard_map/reduce_scatter | solution.py:24
  (189 shorter events, 108.9 us)
Async XLA Ops:
  7.2 4.8 copy-start.5
  7.2 5.0 copy-start.3
  7.2 6.2 %copy-start.6 = (s32[128]{0:T(128)S(1)}, s32[128]{0:T(128)}, u32[]{:S(2)}) copy-start(s32[128]{0:T(128)} %param.11) | copy-start | bytes 1540
  7.2 159.9 %all-gather.2.cloned.1.call-start = ((), (), s32[]{:S(2)}) async-start(), calls=%async_computation.3 | async-start | bytes 8650752 | tf_op jit(solution)/shard_map/all_gather | solution.py:17
  9.0 501.9 %reduce-scatter.4.cloned.1.call-start = ((), (), s32[]{:S(2)}) async-start(), calls=%async_computation.4 | async-start | bytes 10485760 | tf_op jit(solution)/shard_map/reduce_scatter | solution.py:24
  182.7 5.0 copy-start.1
  196.7 2.1 copy-start
  210.5 2.1 copy-start
  224.3 2.1 copy-start
  238.1 2.1 copy-start
  265.9 7.5 %slice-start = ((s8[4718592]{0:T(1024)(128)(4,1)}), s8[4194304]{0:T(1024)(128)(4,1)S(1)}, s32[]{:S(2)}) async-start(s8[4718592]{0:T(1024)(128)(4,1)} %bitcast.173), calls=%async_computation.7 | async-start | bytes 8388608 | tf_op jit(solution)/shard_map/while
  265.9 7.5 %slice-start.1 = ((s8[4718592]{0:T(1024)(128)(4,1)}), s8[524288]{0:T(1024)(128)(4,1)S(1)}, s32[]{:S(2)}) async-start(s8[4718592]{0:T(1024)(128)(4,1)} %bitcast.173), calls=%async_computation.8 | async-start | bytes 1048576 | tf_op jit(solution)/shard_map/while
  289.9 7.5 %slice-start = ((s8[4718592]{0:T(1024)(128)(4,1)}), s8[4194304]{0:T(1024)(128)(4,1)S(1)}, s32[]{:S(2)}) async-start(s8[4718592]{0:T(1024)(128)(4,1)} %bitcast.173), calls=%async_computation.7 | async-start | bytes 8388608 | tf_op jit(solution)/shard_map/while
  289.9 7.4 %slice-start.1 = ((s8[4718592]{0:T(1024)(128)(4,1)}), s8[524288]{0:T(1024)(128)(4,1)S(1)}, s32[]{:S(2)}) async-start(s8[4718592]{0:T(1024)(128)(4,1)} %bitcast.173), calls=%async_computation.8 | async-start | bytes 1048576 | tf_op jit(solution)/shard_map/while
  313.9 7.5 %slice-start = ((s8[4718592]{0:T(1024)(128)(4,1)}), s8[4194304]{0:T(1024)(128)(4,1)S(1)}, s32[]{:S(2)}) async-start(s8[4718592]{0:T(1024)(128)(4,1)} %bitcast.173), calls=%async_computation.7 | async-start | bytes 8388608 | tf_op jit(solution)/shard_map/while
  313.9 7.5 %slice-start.1 = ((s8[4718592]{0:T(1024)(128)(4,1)}), s8[524288]{0:T(1024)(128)(4,1)S(1)}, s32[]{:S(2)}) async-start(s8[4718592]{0:T(1024)(128)(4,1)} %bitcast.173), calls=%async_computation.8 | async-start | bytes 1048576 | tf_op jit(solution)/shard_map/while
  338.0 7.5 %slice-start = ((s8[4718592]{0:T(1024)(128)(4,1)}), s8[4194304]{0:T(1024)(128)(4,1)S(1)}, s32[]{:S(2)}) async-start(s8[4718592]{0:T(1024)(128)(4,1)} %bitcast.173), calls=%async_computation.7 | async-start | bytes 8388608 | tf_op jit(solution)/shard_map/while
  338.0 7.5 %slice-start.1 = ((s8[4718592]{0:T(1024)(128)(4,1)}), s8[524288]{0:T(1024)(128)(4,1)S(1)}, s32[]{:S(2)}) async-start(s8[4718592]{0:T(1024)(128)(4,1)} %bitcast.173), calls=%async_computation.8 | async-start | bytes 1048576 | tf_op jit(solution)/shard_map/while
  432.0 113.6 %copy-start.2 = (bf16[4,32,4,8,128]{4,1,3,2,0:T(8,128)(2,1)S(1)}, bf16[4,32,4,8,128]{4,1,3,2,0:T(8,128)(2,1)}, u32[]{:S(2)}) copy-start(bf16[4,32,4,8,128]{4,1,3,2,0:T(8,128)(2,1)} %get-tuple-element.598) | copy-start | bytes 3145732
  432.0 114.0 %copy-start.4 = (bf16[4,32,4,8,128]{4,3,2,1,0:T(8,128)(2,1)S(1)}, bf16[4,32,4,8,128]{4,3,2,1,0:T(8,128)(2,1)}, u32[]{:S(2)}) copy-start(bf16[4,32,4,8,128]{4,3,2,1,0:T(8,128)(2,1)} %get-tuple-element.259) | copy-start | bytes 3145732
  432.1 113.5 %reduce-scatter.6.cloned.1.call-start = ((), (), s32[]{:S(2)}) async-start(), calls=%async_computation.5 | async-start | bytes 2621440 | tf_op jit(solution)/shard_map/reduce_scatter | solution.py:24
  511.0 65.4 %reduce-scatter.8.cloned.1.call-start = ((), (), s32[]{:S(2)}) async-start(), calls=%async_computation.6 | async-start | bytes 786432 | tf_op jit(solution)/shard_map/reduce_scatter | solution.py:24
Sparse Core Ops, SparseCore 0:
  11.4 155.6 all-gather.1
  432.2 78.7 reduce-scatter.3
  513.5 32.0 reduce-scatter.5
  547.9 28.4 reduce-scatter.7
where the time goes:
time: 589 us; the launch traced here: 585 us
  waiting for transfers between devices  294 us (50%)
  local copies, waits for them, and re-layouts  154 us (26%)
  matrix products  90 us (15%)
  other arithmetic  21.3 us (4%)
  between operations  13.9 us (2%)
  loops' own time  11 us (2%)
    all_gather x1, waiting for transfers between devices, in_one_piece(): whole = lax.all_gather(both, axis, axis=dim, tiled=True)  153 us
    reduce_scatter x3, waiting for transfers between devices, own_rows(): total = lax.psum_scatter(total, axis, scatter_dimension=0, tiled=True)  141 us
    slice x4, local copies, waits for them, and re-layouts, to_slots(): trimmed = buffer[span_rows:].reshape(blocks_all, BLK, head_width)  48.7 us
    dot_general x4, matrix products, backward_step(): jnp.einsum('qgjd,kgd->gjqk', block_query, window_keys, preferred_element_...  17.4 us
    dot_general x4, matrix products, backward_step(): jnp.einsum('gjqk,qgjd->kgd', dscore, block_query, preferred_element_type=...  16.4 us
    dot_general x4, matrix products, forward_block(): jnp.einsum('gjqk,kgd->qgjd', attention, window_values, preferred_element_...  16.2 us
    dot_general x4, matrix products, backward_step(): jnp.einsum('gjqk,qgjd->kgd', attention_b, block_grad, preferred_element_t...  15.8 us
    reshape x2, local copies, waits for them, and re-layouts, to_slots(): trimmed = buffer[span_rows:].reshape(blocks_all, BLK, head_width)  14.4 us
  transfers between devices with their start and end apart: 4, of which 4 were waited for; matrix products, arithmetic and copies ran while one was open for 1% of the time, Pallas kernels for 0%

commit v1 on v0

v1 whole, which is shorter than its diff:
```python
import functools

import jax
import jax.numpy as jnp
from jax import lax
from jax.experimental import pallas as pl
from jax.experimental.pallas import tpu as pltpu
from jax.sharding import Mesh
from jax.sharding import PartitionSpec as P

BLK = 32
HEAD = 128
TILE = 256


def attend(assign_ref, len_ref, coord_ref, qd_ref, kv_ref, od_ref, dkv_ref,
           kp, vp, kt, vt, dk, dv, s_scr, dp_scr, ot, dqt, *, docs, slots, group, xs, ys, zs):
    scale = HEAD ** -0.5
    i = pl.program_id(0)
    per = slots // (xs * ys * zs)
    z = coord_ref[1]
    rows = group * BLK
    tile_blocks = TILE // BLK

    def place(s):
        c = s // per
        zz = jnp.where(c % zs == z, 0, 1)
        return (((c // zs) % ys) * zs + zz) * (xs * per) + (c // (ys * zs)) * per + s % per

    @pl.when(i == 0)
    def _():
        def bring(s, carry):
            b = assign_ref[s]
            at = place(s)
            kp[b] = kv_ref[at, :, :HEAD]
            vp[b] = kv_ref[at, :, HEAD:]
            dk[b] = jnp.zeros((BLK, HEAD), jnp.float32)
            dv[b] = jnp.zeros((BLK, HEAD), jnp.float32)
            return carry
        lax.fori_loop(0, slots, bring, 0, unroll=8)

        def flip(t, carry):
            kt[t] = kp[pl.ds(t * tile_blocks, tile_blocks)].reshape(TILE, HEAD).T
            vt[t] = vp[pl.ds(t * tile_blocks, tile_blocks)].reshape(TILE, HEAD).T
            return carry
        lax.fori_loop(0, slots * BLK // TILE, flip, 0)

    slot = ((i // per) * (ys * zs) + coord_ref[0]) * per + i % per
    first = assign_ref[slot] * BLK
    place_row = first + (lax.broadcasted_iota(jnp.int32, (1, rows), 1) % BLK)
    start_row = jnp.zeros((1, rows), jnp.int32)
    start = jnp.int32(0)
    bound = jnp.int32(0)
    for d in range(docs):
        bound = bound + len_ref[d]
        start_row = jnp.where(place_row >= bound, bound, start_row)
        start = jnp.where(first >= bound, bound, start)
    t0 = start // TILE
    t1 = (first + BLK - 1) // TILE + 1

    q = jnp.concatenate([qd_ref[0, :, h * HEAD:(h + 1) * HEAD] for h in range(group)], axis=0)
    do = jnp.concatenate([qd_ref[0, :, (group + h) * HEAD:(group + h + 1) * HEAD] for h in range(group)], axis=0)
    NT = (((1,), (1,)), ((), ()))
    NN = (((1,), (0,)), ((), ()))
    dot = functools.partial(lax.dot_general, preferred_element_type=jnp.float32)

    def score(t, top):
        k_t = kp[pl.ds(t * tile_blocks, tile_blocks)].reshape(TILE, HEAD)
        v_t = vp[pl.ds(t * tile_blocks, tile_blocks)].reshape(TILE, HEAD)
        s = dot(k_t, q, NT)
        key = t * TILE + lax.broadcasted_iota(jnp.int32, (TILE, rows), 0)
        s = jnp.where((key >= start_row) & (key <= place_row), s, -jnp.inf)
        s_scr[t - t0] = s
        dp_scr[t - t0] = dot(v_t, do, NT)
        return jnp.maximum(top, jnp.max(s.reshape(TILE // 8, 8, rows), axis=0))

    top = lax.fori_loop(t0, t1, score, jnp.full((8, rows), -jnp.inf, jnp.float32))
    top = jnp.max(top, axis=0, keepdims=True)

    def total(t, sums):
        e = jnp.exp((s_scr[t - t0] - top) * scale)
        s_scr[t - t0] = e
        ed = e * dp_scr[t - t0]
        return (sums[0] + jnp.sum(e.reshape(TILE // 8, 8, rows), axis=0),
                sums[1] + jnp.sum(ed.reshape(TILE // 8, 8, rows), axis=0))

    zero = jnp.zeros((8, rows), jnp.float32)
    sums = lax.fori_loop(t0, t1, total, (zero, zero))
    inv = 1.0 / jnp.sum(sums[0], axis=0, keepdims=True)
    delta = jnp.sum(sums[1], axis=0, keepdims=True) * inv
    ot[...] = jnp.zeros_like(ot)
    dqt[...] = jnp.zeros_like(dqt)

    def grads(t, carry):
        p = s_scr[t - t0] * inv
        pb = p.astype(jnp.bfloat16)
        ds = (p * (dp_scr[t - t0] - delta) * scale).astype(jnp.bfloat16)
        ot[...] += dot(vt[t], pb, NN)
        dqt[...] += dot(kt[t], ds, NN)
        at = pl.ds(t * tile_blocks, tile_blocks)
        dv[at] += dot(pb, do, NN).reshape(tile_blocks, BLK, HEAD)
        dk[at] += dot(ds, q, NN).reshape(tile_blocks, BLK, HEAD)
        return carry

    lax.fori_loop(t0, t1, grads, 0)
    o = ot[...].T.astype(jnp.bfloat16)
    dq = dqt[...].T.astype(jnp.bfloat16)
    for h in range(group):
        od_ref[0, :, h * HEAD:(h + 1) * HEAD] = o[h * BLK:(h + 1) * BLK]
        od_ref[0, :, (group + h) * HEAD:(group + h + 1) * HEAD] = dq[h * BLK:(h + 1) * BLK]

    @pl.when(i == pl.num_programs(0) - 1)
    def _():
        def send(s, carry):
            b = assign_ref[s]
            at = place(s)
            dkv_ref[at, :, :HEAD] = dk[b].astype(jnp.bfloat16)
            dkv_ref[at, :, HEAD:] = dv[b].astype(jnp.bfloat16)
            return carry
        lax.fori_loop(0, slots, send, 0, unroll=8)


def attention(assign, lengths, coord, qd, kv, *, xs, ys, zs):
    blocks = qd.shape[0]
    group = qd.shape[2] // (2 * HEAD)
    slots = kv.shape[0]
    span = (1023 + BLK + TILE - 1) // TILE + 1
    rows = group * BLK
    f32, bf = jnp.float32, jnp.bfloat16
    body = functools.partial(attend, docs=lengths.shape[0], slots=slots, group=group, xs=xs, ys=ys, zs=zs)
    return pl.pallas_call(
        body,
        out_shape=(jax.ShapeDtypeStruct(qd.shape, bf), jax.ShapeDtypeStruct(kv.shape, bf)),
        grid_spec=pltpu.PrefetchScalarGridSpec(
            num_scalar_prefetch=3, grid=(blocks,),
            in_specs=[pl.BlockSpec((1, BLK, qd.shape[2]), lambda i, *_: (i, 0, 0)),
                      pl.BlockSpec(kv.shape, lambda i, *_: (0, 0, 0))],
            out_specs=[pl.BlockSpec((1, BLK, qd.shape[2]), lambda i, *_: (i, 0, 0)),
                       pl.BlockSpec(kv.shape, lambda i, *_: (0, 0, 0))],
            scratch_shapes=[
                pltpu.VMEM((slots, BLK, HEAD), bf), pltpu.VMEM((slots, BLK, HEAD), bf),
                pltpu.VMEM((slots * BLK // TILE, HEAD, TILE), bf), pltpu.VMEM((slots * BLK // TILE, HEAD, TILE), bf),
                pltpu.VMEM((slots, BLK, HEAD), f32), pltpu.VMEM((slots, BLK, HEAD), f32),
                pltpu.VMEM((span, TILE, rows), f32), pltpu.VMEM((span, TILE, rows), f32),
                pltpu.VMEM((HEAD, rows), f32), pltpu.VMEM((HEAD, rows), f32),
            ]),
        compiler_params=pltpu.CompilerParams(dimension_semantics=("arbitrary",), vmem_limit_bytes=48 << 20),
        name="attend",
    )(assign, lengths, coord, qd, kv)


X, Y, Z = "ctx_0", "ctx_1", "ctx_2"
DP_CTX = ("dp", X, Y, Z)
SWAP = [(0, 1), (1, 0)]


def by_head(a, heads):
    return a.reshape(a.shape[0], heads, a.shape[1] // heads).transpose(1, 0, 2)


def by_row(a):
    return a.transpose(1, 0, 2).reshape(a.shape[1], a.shape[0] * a.shape[2])


def body(doc_lengths, assignment, queries, key_state_rows, value_state_rows, out_grad):
    xs, ys, zs = (lax.axis_size(name) for name in (X, Y, Z))
    rows = queries.shape[0]
    slots = assignment.shape[0]
    coord = jnp.stack([lax.axis_index((Y, Z)), lax.axis_index(Z)]).astype(jnp.int32)

    kv = jnp.concatenate([by_head(key_state_rows, xs), by_head(value_state_rows, xs)], axis=2)
    qd = jnp.concatenate([by_head(queries, xs), by_head(out_grad, xs)], axis=2)
    kv = lax.all_to_all(kv, X, 0, 0, tiled=True)
    qd, kv = lax.optimization_barrier((qd, kv))
    peer = lax.ppermute(kv, Z, SWAP)
    qd = lax.all_to_all(qd, X, 0, 0, tiled=True)
    pair = jnp.stack([kv, peer])
    pair, qd = lax.optimization_barrier((pair, qd))
    pairs = jnp.broadcast_to(pair[None], (ys,) + pair.shape)
    pairs = lax.all_to_all(pairs, Y, 0, 0, tiled=True)

    od, dkv = attention(
        assignment,
        doc_lengths,
        coord,
        qd.reshape(xs * rows // BLK, BLK, -1),
        pairs.reshape(slots, BLK, -1),
        xs=xs,
        ys=ys,
        zs=zs,
    )

    dkv = dkv.reshape(pairs.shape)
    dkv = lax.all_to_all(dkv, Y, 0, 0, tiled=True)
    dkv = jnp.sum(dkv.astype(jnp.float32), axis=0)
    other = dkv[1].astype(jnp.bfloat16)
    other, od = lax.optimization_barrier((other, od))
    other = lax.ppermute(other, Z, SWAP)
    od = lax.all_to_all(od.reshape(qd.shape), X, 0, 0, tiled=True)
    dkv = (dkv[0] + other.astype(jnp.float32)).astype(jnp.bfloat16)
    dkv, od = lax.optimization_barrier((dkv, od))
    dkv = lax.all_to_all(dkv, X, 0, 0, tiled=True)
    half = od.shape[2] // 2
    return (
        by_row(od[:, :, :half]),
        by_row(od[:, :, half:]),
        by_row(dkv[:, :, :HEAD]),
        by_row(dkv[:, :, HEAD:]),
    )


def solution(mesh):
    finer = Mesh(mesh.devices.reshape(mesh.shape["dp"], 4, 4, 2), DP_CTX)
    rows = P(DP_CTX, None)
    return jax.shard_map(
        body,
        mesh=finer,
        in_specs=(P("dp"), P("dp"), rows, rows, rows, rows),
        out_specs=(rows, rows, rows, rows),
        check_vma=False,
    )
```

time: 589 us -> 182 us (0.31)
  waiting for transfers between devices: 294 us -> 74.8 us
  local copies, waits for them, and re-layouts: 154 us -> 9.32 us
  matrix products: 90 us -> 0 us
  Pallas kernels: 0 us -> 34.4 us
  blocking collectives: 0 us -> 33.2 us
  starting transfers between devices: 0.16 us -> 25.9 us
  other arithmetic: 21.3 us -> 2.78 us
  between operations: 13.9 us -> 0.77 us
  loops' own time: 11 us -> 0 us
    all_gather x1 -> x0, waiting for transfers between devices: 153 us -> none  [in_one_piece(): whole = lax.all_gather(both, axis, axis=dim, tiled=True)]
    reduce_scatter x3 -> x0, waiting for transfers between devices: 141 us -> none  [own_rows(): total = lax.psum_scatter(total, axis, scatter_dimension=0, tiled=True)]
    dot_general x28 -> x0, matrix products: 90 us -> none  [the longest x4 17.4 us: backward_step(): jnp.einsum('qgjd,kgd->gjqk', block_query, window_keys, preferred_element_...]
    all_to_all x0 -> x5, waiting for transfers between devices: none -> 52.6 us  [the longest x1 24.3 us: body(): pairs = lax.all_to_all(pairs, Y, 0, 0, tiled=True)]
    slice x5 -> x1, local copies, waits for them, and re-layouts: 50.4 us -> 0.05 us  [body(): dkv[:, :, HEAD:]]
    pallas_call x0 -> x1, Pallas kernels: none -> 34.4 us  [attention(): pl.pallas_call(body, out_shape=(jax.ShapeDtypeStruct(qd.shape, bf), jax.S...]
    all_to_all x0 -> x1, blocking collectives: none -> 33.2 us  [body(): dkv = lax.all_to_all(dkv, Y, 0, 0, tiled=True)]
    dynamic_slice x21 -> x0, local copies, waits for them, and re-layouts: 22.6 us -> none  [the longest x12 8.83 us: body(): lax.map(forward_block, (query_blocks, own_blocks))]
  transfers between devices with their start and end apart: 4 -> 7, of which waited for: 4 -> 7; matrix products, arithmetic and copies ran while one was open for 1% -> 3% of each run, Pallas kernels for 0% -> 0%
where the time goes in v1:
time: 182 us; the launch traced here: 181 us
  waiting for transfers between devices  74.8 us (41%)
  Pallas kernels  34.4 us (19%)
  blocking collectives  33.2 us (18%)
  starting transfers between devices  25.9 us (14%)
  local copies, waits for them, and re-layouts  9.32 us (5%)
  other arithmetic  2.78 us (2%)
    pallas_call x1, Pallas kernels, attention(): pl.pallas_call(body, out_shape=(jax.ShapeDtypeStruct(qd.shape, bf), jax.S...  34.4 us
    all_to_all x1, blocking collectives, body(): dkv = lax.all_to_all(dkv, Y, 0, 0, tiled=True)  33.2 us
    all_to_all x1, waiting for transfers between devices, body(): pairs = lax.all_to_all(pairs, Y, 0, 0, tiled=True)  24.3 us
    ppermute x1, waiting for transfers between devices, body(): other = lax.ppermute(other, Z, SWAP)  11.6 us
    all_to_all x1, waiting for transfers between devices, body(): od = lax.all_to_all(od.reshape(qd.shape), X, 0, 0, tiled=True)  10.8 us
    ppermute x1, waiting for transfers between devices, body(): peer = lax.ppermute(kv, Z, SWAP)  10.6 us
    all_to_all x1, waiting for transfers between devices, body(): qd = lax.all_to_all(qd, X, 0, 0, tiled=True)  8.13 us
    ppermute x1, starting transfers between devices, body(): peer = lax.ppermute(kv, Z, SWAP)  6.38 us
  transfers between devices with their start and end apart: 7, of which 7 were waited for; matrix products, arithmetic and copies ran while one was open for 3% of the time, Pallas kernels for 0%

profile of v1, /device:TPU:32, one launch (start us, length us, event | category | flops | bytes accessed | tf_op | source)
XLA Modules:
  0.0 181.2 jit_solution(9836293999059382889)
XLA Ops:
  0.7 1.2 copy.21
  1.8 1.0 copy.22
  2.9 0.9 copy.23
  3.7 4.3 %all-to-all-start = ((bf16[4,128,256]{2,1,0:T(8,128)(2,1)}), bf16[4,128,256]{2,1,0:T(8,128)(2,1)S(1)}, u32[]{:S(2)}, u32[]{:S(2)}) async-start(bf16[4,128,256]{2,1,0:T(8,128)(2,1)} %copy.23), calls=%async_computation | async-start | bytes 524288 | tf_op jit(solution)/shard_map/all_to_all | solution.py:173
  8.0 0.2 bitcast_bitcast_fusion
  8.2 1.5 pad_maximum_fusion
  9.8 4.9 %all-to-all-done = bf16[4,128,256]{2,1,0:T(8,128)(2,1)S(1)} async-done(((bf16[4,128,256]{2,1,0:T(8,128)(2,1)}), bf16[4,128,256]{2,1,0:T(8,128)(2,1)S(1)}, u32[]{:S(2)}, u32[]{:S(2)}) %all-to-all-start) | async-done | bytes 262176 | tf_op jit(solution)/shard_map/all_to_all | solution.py:173
  14.7 3.6 %all-to-all-start.1 = ((bf16[4,128,2048]{2,1,0:T(8,128)(2,1)}), bf16[4,128,2048]{2,1,0:T(8,128)(2,1)S(1)}, u32[]{:S(2)}, u32[]{:S(2)}) async-start(bf16[4,128,2048]{2,1,0:T(8,128)(2,1)} %pad_maximum_fusion), calls=%async_computation.1 | async-start | bytes 4194304 | tf_op jit(solution)/shard_map/all_to_all | solution.py:176
  18.3 6.4 %collective-permute-start = (bf16[4,128,256]{2,1,0:T(8,128)(2,1)S(1)}, bf16[4,128,256]{2,1,0:T(8,128)(2,1)S(1)}, u32[]{:S(2)}, u32[]{:S(2)}) collective-permute-start(bf16[4,128,256]{2,1,0:T(8,128)(2,1)S(1)} %all-to-all-done), channel_id=1, source_target_pairs={{0,1},{1,0},{2,3},{3,2},{4,5},{5,4},{6,7},{7,6},{8,9},{9,8},{10,11... | collective-permute-start | bytes 786440 | tf_op jit(solution)/shard_map/ppermute | solution.py:175
  24.7 10.6 %collective-permute-done = bf16[4,128,256]{2,1,0:T(8,128)(2,1)S(1)} collective-permute-done((bf16[4,128,256]{2,1,0:T(8,128)(2,1)S(1)}, bf16[4,128,256]{2,1,0:T(8,128)(2,1)S(1)}, u32[]{:S(2)}, u32[]{:S(2)}) %collective-permute-start) | collective-permute-done | bytes 262176 | tf_op jit(solution)/shard_map/ppermute | solution.py:175
  35.4 8.1 %all-to-all-done.1 = bf16[4,128,2048]{2,1,0:T(8,128)(2,1)S(1)} async-done(((bf16[4,128,2048]{2,1,0:T(8,128)(2,1)}), bf16[4,128,2048]{2,1,0:T(8,128)(2,1)S(1)}, u32[]{:S(2)}, u32[]{:S(2)}) %all-to-all-start.1) | async-done | bytes 2097184 | tf_op jit(solution)/shard_map/all_to_all | solution.py:176
  43.5 1.8 broadcast_in_dim.2
  45.3 0.2 copy-done.2
  45.4 4.5 %all-to-all-start.2 = ((bf16[4,2,4,128,256]{4,3,2,1,0:T(8,128)(2,1)}), bf16[4,2,4,128,256]{4,3,2,1,0:T(8,128)(2,1)}, u32[]{:S(2)}, u32[]{:S(2)}) async-start(bf16[4,2,4,128,256]{4,3,2,1,0:T(8,128)(2,1)} %broadcast_in_dim.2), calls=%async_computation.2 | async-start | bytes 4194304 | tf_op jit(solution)/shard_map/all_to_all | solution.py:180
  50.0 24.3 %all-to-all-done.2 = bf16[4,2,4,128,256]{4,3,2,1,0:T(8,128)(2,1)} async-done(((bf16[4,2,4,128,256]{4,3,2,1,0:T(8,128)(2,1)}), bf16[4,2,4,128,256]{4,3,2,1,0:T(8,128)(2,1)}, u32[]{:S(2)}, u32[]{:S(2)}) %all-to-all-start.2) | async-done | bytes 2097184 | tf_op jit(solution)/shard_map/all_to_all | solution.py:180
  74.3 34.4 %attend.1 = (bf16[16,32,2048]{2,1,0:T(8,128)(2,1)}, bf16[128,32,256]{2,1,0:T(8,128)(2,1)S(1)}) custom-call(s32[128]{0:T(128)S(1)} %copy-done, s32[8]{0:T(128)S(1)} %copy-done.1, s32[2]{0:T(128)S(1)} %pad_add_fusion.coord_ref, bf16[16,32,2048]{2,1,0:T(8,128)(2,1)} %bitcast.47, bf16[128,32,256]{2,1,0:T(8,128)(2,1)} %bitcast.11.kv_ref), custom_call_target="tpu_custom_call" | custom-call | tf_op jit(solution)/shard_map/attend/pallas_call | solution.py:131
  108.7 33.2 %all_to_all.30 = bf16[4,2,4,128,256]{4,3,2,1,0:T(8,128)(2,1)S(1)} all-to-all(bf16[4,2,4,128,256]{4,3,2,1,0:T(8,128)(2,1)S(1)} %bitcast.46), channel_id=1, replica_groups=mesh['dp'=8,'ctx_0'=4,'ctx_1'=4,'ctx_2'=2] {'ctx_1'}, dimensions={0} | all-to-all | bytes 4194304 | tf_op jit(solution)/shard_map/all_to_all | solution.py:194
  141.9 0.3 convert_reduce_fusion
  142.3 3.6 %all-to-all-start.4 = ((bf16[4,128,2048]{2,1,0:T(8,128)(2,1)}), bf16[4,128,2048]{2,1,0:T(8,128)(2,1)S(1)}, u32[]{:S(2)}, u32[]{:S(2)}) async-start(bf16[4,128,2048]{2,1,0:T(8,128)(2,1)} %bitcast.15), calls=%async_computation.4 | async-start | bytes 4194304 | tf_op jit(solution)/shard_map/all_to_all | solution.py:199
  145.9 0.1 collective-permute-start.1
  146.0 11.6 %collective-permute-done.1 = bf16[4,128,256]{2,1,0:T(8,128)(2,1)S(1)} collective-permute-done((bf16[4,128,256]{2,1,0:T(8,128)(2,1)S(1)}, bf16[4,128,256]{2,1,0:T(8,128)(2,1)S(1)}, u32[]{:S(2)}, u32[]{:S(2)}) %collective-permute-start.1) | collective-permute-done | bytes 262176 | tf_op jit(solution)/shard_map/ppermute | solution.py:198
  157.6 0.8 fusion.1
  158.4 10.8 %all-to-all-done.4 = bf16[4,128,2048]{2,1,0:T(8,128)(2,1)S(1)} async-done(((bf16[4,128,2048]{2,1,0:T(8,128)(2,1)}), bf16[4,128,2048]{2,1,0:T(8,128)(2,1)S(1)}, u32[]{:S(2)}, u32[]{:S(2)}) %all-to-all-start.4) | async-done | bytes 2097184 | tf_op jit(solution)/shard_map/all_to_all | solution.py:199
  169.2 3.4 %all-to-all-start.5 = ((bf16[4,128,256]{2,1,0:T(8,128)(2,1)}), bf16[4,128,256]{2,1,0:T(8,128)(2,1)S(1)}, u32[]{:S(2)}, u32[]{:S(2)}) async-start(bf16[4,128,256]{2,1,0:T(8,128)(2,1)} %fusion.1), calls=%async_computation.5 | async-start | bytes 524288 | tf_op jit(solution)/shard_map/all_to_all | solution.py:202
  172.7 0.2 slice_bitcast_fusion
  172.8 1.0 copy.35
  173.9 1.0 copy.34
  174.9 4.4 %all-to-all-done.5 = bf16[4,128,256]{2,1,0:T(8,128)(2,1)S(1)} async-done(((bf16[4,128,256]{2,1,0:T(8,128)(2,1)}), bf16[4,128,256]{2,1,0:T(8,128)(2,1)S(1)}, u32[]{:S(2)}, u32[]{:S(2)}) %all-to-all-start.5) | async-done | bytes 262176 | tf_op jit(solution)/shard_map/all_to_all | solution.py:202
  179.4 0.1 copy.31
  179.5 0.8 copy.29
  180.3 0.1 copy.30
  180.4 0.8 copy.28
  (14 shorter events, 0.2 us)
Async XLA Ops:
  0.6 7.4 %copy-start.3 = (bf16[128,4096]{1,0:T(8,128)(2,1)S(1)}, bf16[128,4096]{1,0:T(8,128)(2,1)}, u32[]{:S(2)}) copy-start(bf16[128,4096]{1,0:T(8,128)(2,1)} %param.11) | copy-start | bytes 3145732
  0.6 7.4 %copy-start.4 = (bf16[128,4096]{1,0:T(8,128)(2,1)S(1)}, bf16[128,4096]{1,0:T(8,128)(2,1)}, u32[]{:S(2)}) copy-start(bf16[128,4096]{1,0:T(8,128)(2,1)} %param.8) | copy-start | bytes 3145732
  3.7 11.0 %all-to-all-start = ((bf16[4,128,256]{2,1,0:T(8,128)(2,1)}), bf16[4,128,256]{2,1,0:T(8,128)(2,1)S(1)}, u32[]{:S(2)}, u32[]{:S(2)}) async-start(bf16[4,128,256]{2,1,0:T(8,128)(2,1)} %copy.23), calls=%async_computation | async-start | bytes 524288 | tf_op jit(solution)/shard_map/all_to_all | solution.py:173
  14.7 28.8 %all-to-all-start.1 = ((bf16[4,128,2048]{2,1,0:T(8,128)(2,1)}), bf16[4,128,2048]{2,1,0:T(8,128)(2,1)S(1)}, u32[]{:S(2)}, u32[]{:S(2)}) async-start(bf16[4,128,2048]{2,1,0:T(8,128)(2,1)} %pad_maximum_fusion), calls=%async_computation.1 | async-start | bytes 4194304 | tf_op jit(solution)/shard_map/all_to_all | solution.py:176
  18.3 17.0 %collective-permute-start = (bf16[4,128,256]{2,1,0:T(8,128)(2,1)S(1)}, bf16[4,128,256]{2,1,0:T(8,128)(2,1)S(1)}, u32[]{:S(2)}, u32[]{:S(2)}) collective-permute-start(bf16[4,128,256]{2,1,0:T(8,128)(2,1)S(1)} %all-to-all-done), channel_id=1, source_target_pairs={{0,1},{1,0},{2,3},{3,2},{4,5},{5,4},{6,7},{7,6},{8,9},{9,8},{10,11... | collective-permute-start | bytes 786440 | tf_op jit(solution)/shard_map/ppermute | solution.py:175
  43.5 1.9 %copy-start.2 = (bf16[4,128,2048]{2,1,0:T(8,128)(2,1)}, bf16[4,128,2048]{2,1,0:T(8,128)(2,1)S(1)}, u32[]{:S(2)}) copy-start(bf16[4,128,2048]{2,1,0:T(8,128)(2,1)S(1)} %all-to-all-done.1) | copy-start | bytes 6291460
  45.2 29.0 %copy-start = (s32[128]{0:T(128)S(1)}, s32[128]{0:T(128)}, u32[]{:S(2)}) copy-start(s32[128]{0:T(128)} %assign_ref.1) | copy-start | bytes 1540
  45.3 29.0 %copy-start.1 = (s32[8]{0:T(128)S(1)}, s32[8]{0:T(128)}, u32[]{:S(2)}) copy-start(s32[8]{0:T(128)} %len_ref.1) | copy-start | bytes 100
  45.4 28.9 %all-to-all-start.2 = ((bf16[4,2,4,128,256]{4,3,2,1,0:T(8,128)(2,1)}), bf16[4,2,4,128,256]{4,3,2,1,0:T(8,128)(2,1)}, u32[]{:S(2)}, u32[]{:S(2)}) async-start(bf16[4,2,4,128,256]{4,3,2,1,0:T(8,128)(2,1)} %broadcast_in_dim.2), calls=%async_computation.2 | async-start | bytes 4194304 | tf_op jit(solution)/shard_map/all_to_all | solution.py:180
  142.3 27.0 %all-to-all-start.4 = ((bf16[4,128,2048]{2,1,0:T(8,128)(2,1)}), bf16[4,128,2048]{2,1,0:T(8,128)(2,1)S(1)}, u32[]{:S(2)}, u32[]{:S(2)}) async-start(bf16[4,128,2048]{2,1,0:T(8,128)(2,1)} %bitcast.15), calls=%async_computation.4 | async-start | bytes 4194304 | tf_op jit(solution)/shard_map/all_to_all | solution.py:199
  145.9 11.7 %collective-permute-start.1 = (bf16[4,128,256]{2,1,0:T(8,128)(2,1)S(1)}, bf16[4,128,256]{2,1,0:T(8,128)(2,1)S(1)}, u32[]{:S(2)}, u32[]{:S(2)}) collective-permute-start(bf16[4,128,256]{2,1,0:T(8,128)(2,1)S(1)} %fusion.2), channel_id=1, source_target_pairs={{0,1},{1,0},{2,3},{3,2},{4,5},{5,4},{6,7},{7,6},{8,9},{9,8},{10,11... | collective-permute-start | bytes 786440 | tf_op jit(solution)/shard_map/ppermute | solution.py:198
  169.2 10.1 %all-to-all-start.5 = ((bf16[4,128,256]{2,1,0:T(8,128)(2,1)}), bf16[4,128,256]{2,1,0:T(8,128)(2,1)S(1)}, u32[]{:S(2)}, u32[]{:S(2)}) async-start(bf16[4,128,256]{2,1,0:T(8,128)(2,1)} %fusion.1), calls=%async_computation.5 | async-start | bytes 524288 | tf_op jit(solution)/shard_map/all_to_all | solution.py:202

commit v2 on v1

v2 whole, which is shorter than its diff:
```python
import functools
import math

import jax
import jax.numpy as jnp
from jax import lax
from jax.experimental import pallas as pl
from jax.experimental.pallas import tpu as pltpu
from jax.sharding import Mesh
from jax.sharding import PartitionSpec as P

BLK = 32
HEAD = 128
TILE = 256
MOST = 1024
LAG = (MOST // BLK + 1 + TILE // BLK - 2) // (TILE // BLK) + 1
RING = LAG + 1
NEG = -1e30


def attend(*refs, docs, slots, group, xs, ys, zs):
    assign_ref, len_ref, coord_ref, qd_in = refs[:4]
    kv_in, od_out, dkv_out = refs[4:4 + ys], refs[4 + ys], refs[5 + ys:5 + 2 * ys]
    (qd, kv, od, dkv, dk, dv, ot, dqt, e_scr, dp_scr, tile_top, top_s, sum_s, del_s, from_s, place_s,
     unit_block, unit_tile, qd_sem, kv_sem, od_sem, dkv_sem) = refs[5 + 2 * ys:]
    scale = HEAD ** -0.5
    steep = scale * math.log2(math.e)
    per = slots // (xs * ys * zs)
    blocks = xs * per
    rows = group * BLK
    tiles = slots * BLK // TILE
    tile_blocks = TILE // BLK
    NT = (((1,), (1,)), ((), ()))
    NN = (((1,), (0,)), ((), ()))
    dot = functools.partial(lax.dot_general, preferred_element_type=jnp.float32)

    y = coord_ref[0] // zs

    def each_block(k, act):
        def one(n, carry):
            c, j = n // per, n % per
            owner = (c // zs * ys + lax.rem(y + k, ys)) * zs + c % zs
            act(assign_ref[owner * per + j], c, j)
            return carry

        lax.fori_loop(0, slots // ys, one, 0, unroll=8)

    for k in range(ys):
        each_block(
            (ys - k) % ys,
            lambda b, c, j: pltpu.make_async_copy(kv_in[k].at[c, :, j], kv.at[b], kv_sem).start(),
        )
    qd_copy = pltpu.make_async_copy(qd_in, qd, qd_sem)
    qd_copy.start()

    for n in range(LAG):
        unit_block[n] = blocks
        unit_tile[n] = 0
    lane = lax.broadcasted_iota(jnp.int32, (1, rows), 1) % BLK

    def plan(i, n):
        slot = ((i // per) * (ys * zs) + coord_ref[0]) * per + i % per
        first = assign_ref[slot] * BLK
        place = first + lane
        from_row = jnp.zeros((1, rows), jnp.int32)
        start = jnp.int32(0)
        bound = jnp.int32(0)
        for d in range(docs):
            bound = bound + len_ref[d]
            from_row = jnp.where(place >= bound, bound, from_row)
            start = jnp.where(first >= bound, bound, start)
        from_s[i] = from_row
        place_s[i] = place
        top_s[i] = jnp.full((1, rows), NEG, jnp.float32)
        sum_s[i] = jnp.zeros((1, rows), jnp.float32)
        del_s[i] = jnp.zeros((1, rows), jnp.float32)
        ot[i] = jnp.zeros((HEAD, rows), jnp.float32)
        dqt[i] = jnp.zeros((HEAD, rows), jnp.float32)

        def unit(t, n):
            unit_block[n] = i
            unit_tile[n] = t
            return n + 1

        return lax.fori_loop(start // TILE, (first + BLK - 1) // TILE + 1, unit, n)

    units = lax.fori_loop(0, blocks, plan, jnp.int32(LAG))
    for n in range(LAG):
        unit_block[units + n] = blocks
        unit_tile[units + n] = 0
    for n in range(RING):
        e_scr[n] = jnp.zeros((TILE, rows), jnp.float32)
        dp_scr[n] = jnp.zeros((TILE, rows), jnp.float32)
        tile_top[n] = jnp.zeros((1, rows), jnp.float32)
    from_s[blocks] = jnp.zeros((1, rows), jnp.int32)
    place_s[blocks] = jnp.zeros((1, rows), jnp.int32)
    top_s[blocks] = jnp.zeros((1, rows), jnp.float32)
    sum_s[blocks] = jnp.ones((1, rows), jnp.float32)
    del_s[blocks] = jnp.zeros((1, rows), jnp.float32)
    ot[blocks] = jnp.zeros((HEAD, rows), jnp.float32)
    dqt[blocks] = jnp.zeros((HEAD, rows), jnp.float32)

    def clear(t, carry):
        dk[t] = jnp.zeros((TILE, HEAD), jnp.float32)
        dv[t] = jnp.zeros((TILE, HEAD), jnp.float32)
        return carry

    lax.fori_loop(0, tiles, clear, 0)
    pltpu.make_async_copy(kv, kv, kv_sem).wait()

    def keys(t):
        return kv[pl.ds(t * tile_blocks, tile_blocks), 0].reshape(TILE, HEAD)

    def values(t):
        return kv[pl.ds(t * tile_blocks, tile_blocks), 1].reshape(TILE, HEAD)

    key = lax.broadcasted_iota(jnp.int32, (TILE, rows), 0)

    def rows_of(i, which):
        i = jnp.minimum(i, blocks - 1)
        return qd[i // per, which, i % per].reshape(rows, HEAD)

    qd_copy.wait()

    def step(u, carry):
        old = unit_block[u]
        t = unit_tile[u]
        spot = lax.rem(u + RING - LAG, RING)
        total = 1.0 / sum_s[old]
        weight = jnp.exp2((tile_top[spot] - top_s[old]) * steep) * total
        delta = del_s[old] * total
        p = e_scr[spot] * weight
        pb = p.astype(jnp.bfloat16)
        ds = (p * (dp_scr[spot] - delta)).astype(jnp.bfloat16)
        ot[old] += dot(values(t).T, pb, NN)
        dqt[old] += dot(keys(t).T, ds, NN)
        dv[t] += dot(pb, rows_of(old, 1), NN)
        dk[t] += dot(ds, rows_of(old, 0), NN)

        i = unit_block[u + LAG]
        t = unit_tile[u + LAG]
        spot = lax.rem(u, RING)
        s = dot(keys(t), rows_of(i, 0), NT)
        dp = dot(values(t), rows_of(i, 1), NT)
        s = jnp.where((key >= from_s[i] - t * TILE) & (key <= place_s[i] - t * TILE), s, NEG)
        top = jnp.max(jnp.max(s.reshape(TILE // 8, 8, rows), axis=0), axis=0, keepdims=True)
        e = jnp.exp2((s - top) * steep)
        e_scr[spot] = e
        dp_scr[spot] = dp
        tile_top[spot] = top
        tile_sum = jnp.sum(jnp.sum(e.reshape(TILE // 8, 8, rows), axis=0), axis=0, keepdims=True)
        tile_del = jnp.sum(jnp.sum((e * dp).reshape(TILE // 8, 8, rows), axis=0), axis=0, keepdims=True)
        was = top_s[i]
        now = jnp.maximum(was, top)
        keep = jnp.exp2((was - now) * steep)
        take = jnp.exp2((top - now) * steep)
        top_s[i] = now
        sum_s[i] = sum_s[i] * keep + tile_sum * take
        del_s[i] = del_s[i] * keep + tile_del * take
        return carry

    lax.fori_loop(0, units, step, 0)

    def gone(t, carry):
        at = pl.ds(t * tile_blocks, tile_blocks)
        dkv[at, 0] = (dk[t] * scale).astype(jnp.bfloat16).reshape(tile_blocks, BLK, HEAD)
        dkv[at, 1] = dv[t].astype(jnp.bfloat16).reshape(tile_blocks, BLK, HEAD)
        return carry

    lax.fori_loop(0, tiles, gone, 0, unroll=2)
    for k in range(ys):
        each_block(
            k, lambda b, c, j: pltpu.make_async_copy(dkv.at[b], dkv_out[k].at[c, :, j], dkv_sem).start()
        )

    def rows_out(i, carry):
        od[i // per, 0, i % per] = ot[i].T.astype(jnp.bfloat16).reshape(group, BLK, HEAD)
        od[i // per, 1, i % per] = (dqt[i].T * scale).astype(jnp.bfloat16).reshape(group, BLK, HEAD)
        return carry

    lax.fori_loop(0, blocks, rows_out, 0, unroll=2)
    od_copy = pltpu.make_async_copy(od, od_out, od_sem)
    od_copy.start()
    pltpu.make_async_copy(dkv, dkv, dkv_sem).wait()
    od_copy.wait()


def attention(assign, lengths, coord, qd, kv, *, xs, ys, zs):
    blocks = qd.shape[0] * qd.shape[2]
    group = qd.shape[3]
    slots = ys * kv[0].shape[0] * kv[0].shape[2]
    tiles = slots * BLK // TILE
    rows = group * BLK
    f32, bf, i32 = jnp.float32, jnp.bfloat16, jnp.int32
    body = functools.partial(attend, docs=lengths.shape[0], slots=slots, group=group, xs=xs, ys=ys, zs=zs)
    smem = pl.BlockSpec(memory_space=pltpu.SMEM)
    anywhere = pl.BlockSpec(memory_space=pl.ANY)
    return pl.pallas_call(
        body,
        out_shape=[jax.ShapeDtypeStruct(a.shape, bf) for a in (qd, *kv)],
        in_specs=[smem] * 3 + [anywhere] * (1 + ys),
        out_specs=[anywhere] * (1 + ys),
        scratch_shapes=[
            pltpu.VMEM(qd.shape, bf), pltpu.VMEM((slots, 2, BLK, HEAD), bf),
            pltpu.VMEM(qd.shape, bf), pltpu.VMEM((slots, 2, BLK, HEAD), bf),
            pltpu.VMEM((tiles, TILE, HEAD), f32), pltpu.VMEM((tiles, TILE, HEAD), f32),
            pltpu.VMEM((blocks + 1, HEAD, rows), f32), pltpu.VMEM((blocks + 1, HEAD, rows), f32),
            pltpu.VMEM((RING, TILE, rows), f32), pltpu.VMEM((RING, TILE, rows), f32),
            pltpu.VMEM((RING, 1, rows), f32),
            pltpu.VMEM((blocks + 1, 1, rows), f32), pltpu.VMEM((blocks + 1, 1, rows), f32),
            pltpu.VMEM((blocks + 1, 1, rows), f32), pltpu.VMEM((blocks + 1, 1, rows), i32),
            pltpu.VMEM((blocks + 1, 1, rows), i32),
            pltpu.SMEM((blocks * LAG + 2 * LAG,), i32), pltpu.SMEM((blocks * LAG + 2 * LAG,), i32),
            pltpu.SemaphoreType.DMA, pltpu.SemaphoreType.DMA, pltpu.SemaphoreType.DMA, pltpu.SemaphoreType.DMA,
        ],
        compiler_params=pltpu.CompilerParams(vmem_limit_bytes=40 << 20),
        cost_estimate=pl.CostEstimate(flops=10 ** 9, bytes_accessed=8 << 20, transcendentals=0),
        name="attend",
    )(assign, lengths, coord, qd, *kv)


def lay_out(a_ref, b_ref, o_ref, *, xs, per, heads, copies):
    for which, ref in enumerate((a_ref, b_ref)):
        for x in range(xs):
            for h in range(heads):
                c = (x * heads + h) * HEAD
                block = ref[:, c:c + HEAD].reshape(per, BLK, HEAD)
                for n in range(copies):
                    if heads == 1:
                        o_ref[x * copies + n, which] = block
                    else:
                        o_ref[x * copies + n, which, :, h] = block


def spread(a, b, xs, copies):
    per = a.shape[0] // BLK
    heads = a.shape[1] // (xs * HEAD)
    shape = (xs * copies, 2, per) + ((heads,) if heads > 1 else ()) + (BLK, HEAD)
    return pl.pallas_call(
        functools.partial(lay_out, xs=xs, per=per, heads=heads, copies=copies),
        out_shape=jax.ShapeDtypeStruct(shape, a.dtype),
        cost_estimate=pl.CostEstimate(flops=10 ** 6, bytes_accessed=4 * a.size, transcendentals=0),
        name="spread",
    )(a, b)


def line_up(a_ref, p_ref, q_ref, *, xs, per, heads, copies):
    for which, ref in enumerate((p_ref, q_ref)):
        for x in range(xs):
            for h in range(heads):
                c = (x * heads + h) * HEAD
                if heads == 1:
                    block = a_ref[x * copies, which].astype(jnp.float32)
                    for n in range(1, copies):
                        block += a_ref[x * copies + n, which].astype(jnp.float32)
                    block = block.astype(jnp.bfloat16)
                else:
                    block = a_ref[x, which, :, h]
                ref[:, c:c + HEAD] = block.reshape(per * BLK, HEAD)


def gather(a, xs):
    copies, per = a.shape[0] // xs, a.shape[2]
    heads = a.shape[3] if a.ndim == 6 else 1
    out = jax.ShapeDtypeStruct((per * BLK, xs * heads * HEAD), a.dtype)
    return pl.pallas_call(
        functools.partial(line_up, xs=xs, per=per, heads=heads, copies=copies),
        out_shape=(out, out),
        cost_estimate=pl.CostEstimate(flops=10 ** 6, bytes_accessed=2 * a.size, transcendentals=0),
        name="gather",
    )(a)


X, Y, Z = "ctx_0", "ctx_1", "ctx_2"
DP_CTX = ("dp", X, Y, Z)


def shift(k, size):
    return [(i, (i + k) % size) for i in range(size)]


def body(doc_lengths, assignment, queries, key_state_rows, value_state_rows, out_grad):
    xs, ys, zs = (lax.axis_size(name) for name in (X, Y, Z))
    coord = lax.axis_index((Y, Z)).reshape(1).astype(jnp.int32)

    kv = spread(key_state_rows, value_state_rows, xs, zs)
    kv = lax.all_to_all(kv, (X, Z), 0, 0, tiled=True)
    qd = spread(queries, out_grad, xs, 1)
    with jax.named_scope("kv_y"):
        kv = [kv] + [lax.ppermute(kv, Y, shift(k, ys)) for k in range(1, ys)]
    with jax.named_scope("qd_x"):
        qd = lax.all_to_all(qd, X, 0, 0, tiled=True)

    od, *dkv = attention(assignment, doc_lengths, coord, qd, kv, xs=xs, ys=ys, zs=zs)

    with jax.named_scope("dkv_y"):
        dkv = dkv[:1] + [lax.ppermute(dkv[k], Y, shift(k, ys)) for k in range(1, ys)]
    with jax.named_scope("od_x"):
        od = lax.all_to_all(od, X, 0, 0, tiled=True)
    dkv = sum(part.astype(jnp.float32) for part in dkv).astype(jnp.bfloat16)
    dkv, od = lax.optimization_barrier((dkv, od))
    dkv = lax.all_to_all(dkv, (X, Z), 0, 0, tiled=True)
    return (*gather(od, xs), *gather(dkv, xs))


def solution(mesh):
    finer = Mesh(mesh.devices.reshape(mesh.shape["dp"], 4, 4, 2), DP_CTX)
    rows = P(DP_CTX, None)
    return jax.shard_map(
        body,
        mesh=finer,
        in_specs=(P("dp"), P("dp"), rows, rows, rows, rows),
        out_specs=(rows, rows, rows, rows),
        check_vma=False,
    )
```

time: 182 us -> 154 us (0.85)
  blocking collectives: 33.2 us -> 0 us
  starting transfers between devices: 25.9 us -> 30.7 us
  Pallas kernels: 34.4 us -> 38.6 us
  local copies, waits for them, and re-layouts: 9.32 us -> 5.36 us
    all_to_all x1 -> x0, blocking collectives: 33.2 us -> none  [body(): dkv = lax.all_to_all(dkv, Y, 0, 0, tiled=True)]
    ppermute x2 -> x6, waiting for transfers between devices: 22.2 us -> 48.1 us  [the longest x3 24.5 us: body(): lax.ppermute(dkv[k], Y, shift(k, ys))]
    all_to_all x4 -> x3, waiting for transfers between devices: 44.5 us -> 26.9 us  [the longest x1 16.4 us: body(): kv = lax.all_to_all(kv, (X, Z), 0, 0, tiled=True)]
    all_to_all x1, waiting for transfers between devices: 8.13 us -> 0.01 us  [body(): qd = lax.all_to_all(qd, X, 0, 0, tiled=True)]
    pallas_call x1 -> x5, Pallas kernels: 34.4 us -> 38.6 us  [the longest x1 28.3 us: attention(): pl.pallas_call(body, out_shape=[jax.ShapeDtypeStruct(a.shape, bf) for a i...]
    all_to_all x4 -> x3, starting transfers between devices: 15.8 us -> 19 us  [the longest x1 10 us: body(): kv = lax.all_to_all(kv, (X, Z), 0, 0, tiled=True)]
    reshape x2 -> x0, local copies, waits for them, and re-layouts: 2.08 us -> none  [by_row(): return a.transpose(1, 0, 2).reshape(a.shape[1], a.shape[0] * a.shape[2])]
    ppermute x2 -> x6, starting transfers between devices: 6.47 us -> 8.06 us  [the longest x3 4.69 us: body(): kv = [kv] + [lax.ppermute(kv, Y, shift(k, ys)) for k in range(1, ys)]]
  transfers between devices with their start and end apart: 7 -> 10, of which waited for: 7 -> 6; matrix products, arithmetic and copies ran while one was open for 3% -> 1% of each run, Pallas kernels for 0% -> 4%
where the time goes in v2:
time: 154 us; the launch traced here: 152 us
  waiting for transfers between devices  75 us (49%)
  Pallas kernels  38.6 us (25%)
  starting transfers between devices  30.7 us (20%)
  local copies, waits for them, and re-layouts  5.36 us (3%)
    pallas_call x1, Pallas kernels, attention(): pl.pallas_call(body, out_shape=[jax.ShapeDtypeStruct(a.shape, bf) for a i...  28.3 us
    ppermute x3, waiting for transfers between devices, body(): lax.ppermute(dkv[k], Y, shift(k, ys))  24.5 us
    ppermute x3, waiting for transfers between devices, body(): kv = [kv] + [lax.ppermute(kv, Y, shift(k, ys)) for k in range(1, ys)]  23.6 us
    all_to_all x1, waiting for transfers between devices, body(): kv = lax.all_to_all(kv, (X, Z), 0, 0, tiled=True)  16.4 us
    all_to_all x1, waiting for transfers between devices, body(): dkv = lax.all_to_all(dkv, (X, Z), 0, 0, tiled=True)  10.6 us
    all_to_all x1, starting transfers between devices, body(): kv = lax.all_to_all(kv, (X, Z), 0, 0, tiled=True)  10 us
    unnamed x24, local copies, waits for them, and re-layouts  5.36 us
    pallas_call x2, Pallas kernels, gather(): pl.pallas_call(functools.partial(line_up, xs=xs, per=per, heads=heads, co...  5.22 us
  transfers between devices with their start and end apart: 10, of which 6 were waited for; matrix products, arithmetic and copies ran while one was open for 1% of the time, Pallas kernels for 4%

profile of v2, /device:TPU:32, one launch (start us, length us, event | category | flops | bytes accessed | tf_op | source)
XLA Modules:
  0.0 151.6 jit_solution(10330645994187301289)
XLA Ops:
  0.6 1.8 %spread.3 = bf16[8,2,4,32,128]{4,3,2,1,0:T(8,128)(2,1)} custom-call(bf16[128,512]{1,0:T(8,128)(2,1)} %a_ref.3, bf16[128,512]{1,0:T(8,128)(2,1)} %b_ref.3), custom_call_target="tpu_custom_call" | custom-call | flops 1000000 | bytes 262144 | tf_op jit(solution)/shard_map/spread/pallas_call | solution.py:239
  2.5 10.0 %all-to-all-start.1 = ((bf16[8,2,4,32,128]{4,3,2,1,0:T(8,128)(2,1)}), bf16[8,2,4,32,128]{4,3,2,1,0:T(8,128)(2,1)S(1)}, u32[]{:S(2)}, u32[]{:S(2)}) async-start(bf16[8,2,4,32,128]{4,3,2,1,0:T(8,128)(2,1)} %spread.3), calls=%async_computation.1 | async-start | bytes 1048576 | tf_op jit(solution)/shard_map/all_to_all | solution.py:287
  12.5 3.2 %spread.2 = bf16[4,2,4,8,32,128]{5,4,3,2,1,0:T(8,128)(2,1)} custom-call(bf16[128,4096]{1,0:T(8,128)(2,1)} %a_ref.2, bf16[128,4096]{1,0:T(8,128)(2,1)} %b_ref.2), custom_call_target="tpu_custom_call" | custom-call | flops 1000000 | bytes 2097152 | tf_op jit(solution)/shard_map/spread/pallas_call | solution.py:239
  15.7 16.4 %all-to-all-done.1.refs_4_ = bf16[8,2,4,32,128]{4,3,2,1,0:T(8,128)(2,1)S(1)} async-done(((bf16[8,2,4,32,128]{4,3,2,1,0:T(8,128)(2,1)}), bf16[8,2,4,32,128]{4,3,2,1,0:T(8,128)(2,1)S(1)}, u32[]{:S(2)}, u32[]{:S(2)}) %all-to-all-start.1) | async-done | bytes 524320 | tf_op jit(solution)/shard_map/all_to_all | solution.py:287
  32.1 3.6 %all-to-all-start = ((bf16[4,2,4,8,32,128]{5,4,3,2,1,0:T(8,128)(2,1)}), bf16[4,2,4,8,32,128]{5,4,3,2,1,0:T(8,128)(2,1)S(1)}, u32[]{:S(2)}, u32[]{:S(2)}) async-start(bf16[4,2,4,8,32,128]{5,4,3,2,1,0:T(8,128)(2,1)} %spread.2), calls=%async_computation | async-start | bytes 4194304 | tf_op jit(solution)/shard_map/qd_x/all_to_all | solution.py:292
  35.7 3.1 %collective-permute-start.2 = (bf16[8,2,4,32,128]{4,3,2,1,0:T(8,128)(2,1)S(1)}, bf16[8,2,4,32,128]{4,3,2,1,0:T(8,128)(2,1)S(1)}, u32[]{:S(2)}, u32[]{:S(2)}) collective-permute-start(bf16[8,2,4,32,128]{4,3,2,1,0:T(8,128)(2,1)S(1)} %all-to-all-done.1.refs_4_), channel_id=1, source_target_pairs={{0,6},{2,0},{4,2},{6,4},{1,7},{3,1},{5,3},{7,5},{8,14},{10,8},{12,... | collective-permute-start | bytes 1572872 | tf_op jit(solution)/shard_map/kv_y/ppermute | solution.py:290
  38.8 0.6 collective-permute-start.1
  39.4 1.0 collective-permute-start
  40.4 19.8 %collective-permute-done.2.refs_7_ = bf16[8,2,4,32,128]{4,3,2,1,0:T(8,128)(2,1)S(1)} collective-permute-done((bf16[8,2,4,32,128]{4,3,2,1,0:T(8,128)(2,1)S(1)}, bf16[8,2,4,32,128]{4,3,2,1,0:T(8,128)(2,1)S(1)}, u32[]{:S(2)}, u32[]{:S(2)}) %collective-permute-start.2) | collective-permute-done | bytes 524320 | tf_op jit(solution)/shard_map/kv_y/ppermute | solution.py:290
  60.2 0.0 collective-permute-done.1.refs_6_
  60.2 3.8 %collective-permute-done.refs_5_ = bf16[8,2,4,32,128]{4,3,2,1,0:T(8,128)(2,1)} collective-permute-done((bf16[8,2,4,32,128]{4,3,2,1,0:T(8,128)(2,1)S(1)}, bf16[8,2,4,32,128]{4,3,2,1,0:T(8,128)(2,1)}, u32[]{:S(2)}, u32[]{:S(2)}) %collective-permute-start) | collective-permute-done | bytes 524320 | tf_op jit(solution)/shard_map/kv_y/ppermute | solution.py:290
  64.0 0.0 all-to-all-done.refs_3_
  64.0 28.3 %attend.1 = (bf16[4,2,4,8,32,128]{5,4,3,2,1,0:T(8,128)(2,1)S(1)}, bf16[8,2,4,32,128]{4,3,2,1,0:T(8,128)(2,1)S(1)}, bf16[8,2,4,32,128]{4,3,2,1,0:T(8,128)(2,1)S(1...) custom-call(s32[128]{0:T(128)S(1)} %copy-done.3, s32[8]{0:T(128)S(1)} %copy-done.4, ...), custom_call_target="tpu_custom_call" | custom-call | flops 1000000000 | bytes 8388608 | tf_op jit(solution)/shard_map/attend/pallas_call | solution.py:198
  92.3 1.3 copy-done
  93.7 0.8 copy-done.1
  94.5 0.8 copy-done.5
  95.3 0.8 copy-done.7
  96.1 0.8 copy-done.9
  96.9 4.6 %all-to-all-start.2 = ((bf16[4,2,4,8,32,128]{5,4,3,2,1,0:T(8,128)(2,1)}), bf16[4,2,4,8,32,128]{5,4,3,2,1,0:T(8,128)(2,1)}, u32[]{:S(2)}, u32[]{:S(2)}) async-start(bf16[4,2,4,8,32,128]{5,4,3,2,1,0:T(8,128)(2,1)} %copy-done), calls=%async_computation.2 | async-start | bytes 4194304 | tf_op jit(solution)/shard_map/od_x/all_to_all | solution.py:299
  101.5 0.1 collective-permute-start.3
  101.6 0.1 collective-permute-start.4
  101.7 3.2 %collective-permute-start.5 = (bf16[8,2,4,32,128]{4,3,2,1,0:T(8,128)(2,1)S(1)}, bf16[8,2,4,32,128]{4,3,2,1,0:T(8,128)(2,1)S(1)}, u32[]{:S(2)}, u32[]{:S(2)}) collective-permute-start(bf16[8,2,4,32,128]{4,3,2,1,0:T(8,128)(2,1)S(1)} %copy-done.6), channel_id=1, source_target_pairs={{0,6},{2,0},{4,2},{6,4},{1,7},{3,1},{5,3},{7,5},{8,14},{10,8},{12,... | collective-permute-start | bytes 1572872 | tf_op jit(solution)/shard_map/dkv_y/ppermute | solution.py:297
  104.9 23.9 %collective-permute-done.3 = bf16[8,2,4,32,128]{4,3,2,1,0:T(8,128)(2,1)S(1)} collective-permute-done((bf16[8,2,4,32,128]{4,3,2,1,0:T(8,128)(2,1)S(1)}, bf16[8,2,4,32,128]{4,3,2,1,0:T(8,128)(2,1)S(1)}, u32[]{:S(2)}, u32[]{:S(2)}) %collective-permute-start.3) | collective-permute-done | bytes 524320 | tf_op jit(solution)/shard_map/dkv_y/ppermute | solution.py:297
  128.8 0.0 collective-permute-done.4
  128.8 0.6 collective-permute-done.5
  129.4 1.2 add_convert_fusion
  130.6 0.0 all-to-all-done.2.a_ref
  130.6 4.4 %all-to-all-start.3 = ((bf16[8,2,4,32,128]{4,3,2,1,0:T(8,128)(2,1)}), bf16[8,2,4,32,128]{4,3,2,1,0:T(8,128)(2,1)S(1)}, u32[]{:S(2)}, u32[]{:S(2)}) async-start(bf16[8,2,4,32,128]{4,3,2,1,0:T(8,128)(2,1)} %add_convert_fusion), calls=%async_computation.3 | async-start | bytes 1048576 | tf_op jit(solution)/shard_map/all_to_all | solution.py:302
  134.9 3.4 %gather.2 = (bf16[128,4096]{1,0:T(8,128)(2,1)}, bf16[128,4096]{1,0:T(8,128)(2,1)}) custom-call(bf16[4,2,4,8,32,128]{5,4,3,2,1,0:T(8,128)(2,1)} %all-to-all-done.2.a_ref), custom_call_target="tpu_custom_call" | custom-call | flops 1000000 | bytes 2097152 | tf_op jit(solution)/shard_map/gather/pallas_call | solution.py:266
  138.4 10.6 %all-to-all-done.3.a_ref = bf16[8,2,4,32,128]{4,3,2,1,0:T(8,128)(2,1)S(1)} async-done(((bf16[8,2,4,32,128]{4,3,2,1,0:T(8,128)(2,1)}), bf16[8,2,4,32,128]{4,3,2,1,0:T(8,128)(2,1)S(1)}, u32[]{:S(2)}, u32[]{:S(2)}) %all-to-all-start.3) | async-done | bytes 524320 | tf_op jit(solution)/shard_map/all_to_all | solution.py:302
  149.0 0.8 copy-done.11
  149.8 1.8 %gather.3 = (bf16[128,512]{1,0:T(8,128)(2,1)}, bf16[128,512]{1,0:T(8,128)(2,1)}) custom-call(bf16[8,2,4,32,128]{4,3,2,1,0:T(8,128)(2,1)} %copy-done.11), custom_call_target="tpu_custom_call" | custom-call | flops 1000000 | bytes 524288 | tf_op jit(solution)/shard_map/gather/pallas_call | solution.py:266
  (18 shorter events, 0.0 us)
Async XLA Ops:
  2.5 29.6 %all-to-all-start.1 = ((bf16[8,2,4,32,128]{4,3,2,1,0:T(8,128)(2,1)}), bf16[8,2,4,32,128]{4,3,2,1,0:T(8,128)(2,1)S(1)}, u32[]{:S(2)}, u32[]{:S(2)}) async-start(bf16[8,2,4,32,128]{4,3,2,1,0:T(8,128)(2,1)} %spread.3), calls=%async_computation.1 | async-start | bytes 1048576 | tf_op jit(solution)/shard_map/all_to_all | solution.py:287
  15.7 48.3 %copy-start.3 = (s32[128]{0:T(128)S(1)}, s32[128]{0:T(128)}, u32[]{:S(2)}) copy-start(s32[128]{0:T(128)} %refs_0_.1) | copy-start | bytes 1540
  15.7 48.3 %copy-start.4 = (s32[8]{0:T(128)S(1)}, s32[8]{0:T(128)}, u32[]{:S(2)}) copy-start(s32[8]{0:T(128)} %refs_1_.1) | copy-start | bytes 100
  32.1 31.9 %all-to-all-start = ((bf16[4,2,4,8,32,128]{5,4,3,2,1,0:T(8,128)(2,1)}), bf16[4,2,4,8,32,128]{5,4,3,2,1,0:T(8,128)(2,1)S(1)}, u32[]{:S(2)}, u32[]{:S(2)}) async-start(bf16[4,2,4,8,32,128]{5,4,3,2,1,0:T(8,128)(2,1)} %spread.2), calls=%async_computation | async-start | bytes 4194304 | tf_op jit(solution)/shard_map/qd_x/all_to_all | solution.py:292
  35.7 24.5 %collective-permute-start.2 = (bf16[8,2,4,32,128]{4,3,2,1,0:T(8,128)(2,1)S(1)}, bf16[8,2,4,32,128]{4,3,2,1,0:T(8,128)(2,1)S(1)}, u32[]{:S(2)}, u32[]{:S(2)}) collective-permute-start(bf16[8,2,4,32,128]{4,3,2,1,0:T(8,128)(2,1)S(1)} %all-to-all-done.1.refs_4_), channel_id=1, source_target_pairs={{0,6},{2,0},{4,2},{6,4},{1,7},{3,1},{5,3},{7,5},{8,14},{10,8},{12,... | collective-permute-start | bytes 1572872 | tf_op jit(solution)/shard_map/kv_y/ppermute | solution.py:290
  38.8 21.4 %collective-permute-start.1 = (bf16[8,2,4,32,128]{4,3,2,1,0:T(8,128)(2,1)S(1)}, bf16[8,2,4,32,128]{4,3,2,1,0:T(8,128)(2,1)}, u32[]{:S(2)}, u32[]{:S(2)}) collective-permute-start(bf16[8,2,4,32,128]{4,3,2,1,0:T(8,128)(2,1)S(1)} %all-to-all-done.1.refs_4_), channel_id=1, source_target_pairs={{0,4},{2,6},{4,0},{6,2},{1,5},{3,7},{5,1},{7,3},{8,12},{10,14},{12... | collective-permute-start | bytes 1572872 | tf_op jit(solution)/shard_map/kv_y/ppermute | solution.py:290
  39.4 24.6 %collective-permute-start = (bf16[8,2,4,32,128]{4,3,2,1,0:T(8,128)(2,1)S(1)}, bf16[8,2,4,32,128]{4,3,2,1,0:T(8,128)(2,1)}, u32[]{:S(2)}, u32[]{:S(2)}) collective-permute-start(bf16[8,2,4,32,128]{4,3,2,1,0:T(8,128)(2,1)S(1)} %all-to-all-done.1.refs_4_), channel_id=1, source_target_pairs={{0,2},{2,4},{4,6},{6,0},{1,3},{3,5},{5,7},{7,1},{8,10},{10,12},{12... | collective-permute-start | bytes 1572872 | tf_op jit(solution)/shard_map/kv_y/ppermute | solution.py:290
  92.3 1.3 copy-start
  93.7 0.8 copy-start.1
  94.5 0.8 copy-start.5
  95.3 0.8 copy-start.7
  96.1 0.8 copy-start.9
  96.9 4.6 %copy-start.10 = (bf16[8,2,4,32,128]{4,3,2,1,0:T(8,128)(2,1)S(1)}, bf16[8,2,4,32,128]{4,3,2,1,0:T(8,128)(2,1)}, u32[]{:S(2)}) copy-start(bf16[8,2,4,32,128]{4,3,2,1,0:T(8,128)(2,1)} %copy-done.9) | copy-start | bytes 1572868
  96.9 4.7 %copy-start.8 = (bf16[8,2,4,32,128]{4,3,2,1,0:T(8,128)(2,1)S(1)}, bf16[8,2,4,32,128]{4,3,2,1,0:T(8,128)(2,1)}, u32[]{:S(2)}) copy-start(bf16[8,2,4,32,128]{4,3,2,1,0:T(8,128)(2,1)} %copy-done.7) | copy-start | bytes 1572868
  96.9 4.8 %copy-start.6 = (bf16[8,2,4,32,128]{4,3,2,1,0:T(8,128)(2,1)S(1)}, bf16[8,2,4,32,128]{4,3,2,1,0:T(8,128)(2,1)}, u32[]{:S(2)}) copy-start(bf16[8,2,4,32,128]{4,3,2,1,0:T(8,128)(2,1)} %copy-done.5) | copy-start | bytes 1572868
  96.9 32.5 %copy-start.2 = (bf16[8,2,4,32,128]{4,3,2,1,0:T(8,128)(2,1)S(1)}, bf16[8,2,4,32,128]{4,3,2,1,0:T(8,128)(2,1)}, u32[]{:S(2)}) copy-start(bf16[8,2,4,32,128]{4,3,2,1,0:T(8,128)(2,1)} %copy-done.1) | copy-start | bytes 1572868
  96.9 33.7 %all-to-all-start.2 = ((bf16[4,2,4,8,32,128]{5,4,3,2,1,0:T(8,128)(2,1)}), bf16[4,2,4,8,32,128]{5,4,3,2,1,0:T(8,128)(2,1)}, u32[]{:S(2)}, u32[]{:S(2)}) async-start(bf16[4,2,4,8,32,128]{5,4,3,2,1,0:T(8,128)(2,1)} %copy-done), calls=%async_computation.2 | async-start | bytes 4194304 | tf_op jit(solution)/shard_map/od_x/all_to_all | solution.py:299
  101.5 27.3 %collective-permute-start.3 = (bf16[8,2,4,32,128]{4,3,2,1,0:T(8,128)(2,1)S(1)}, bf16[8,2,4,32,128]{4,3,2,1,0:T(8,128)(2,1)S(1)}, u32[]{:S(2)}, u32[]{:S(2)}) collective-permute-start(bf16[8,2,4,32,128]{4,3,2,1,0:T(8,128)(2,1)S(1)} %copy-done.10), channel_id=1, source_target_pairs={{0,2},{2,4},{4,6},{6,0},{1,3},{3,5},{5,7},{7,1},{8,10},{10,12},{12... | collective-permute-start | bytes 1572872 | tf_op jit(solution)/shard_map/dkv_y/ppermute | solution.py:297
  101.6 27.2 %collective-permute-start.4 = (bf16[8,2,4,32,128]{4,3,2,1,0:T(8,128)(2,1)S(1)}, bf16[8,2,4,32,128]{4,3,2,1,0:T(8,128)(2,1)S(1)}, u32[]{:S(2)}, u32[]{:S(2)}) collective-permute-start(bf16[8,2,4,32,128]{4,3,2,1,0:T(8,128)(2,1)S(1)} %copy-done.8), channel_id=1, source_target_pairs={{0,4},{2,6},{4,0},{6,2},{1,5},{3,7},{5,1},{7,3},{8,12},{10,14},{12... | collective-permute-start | bytes 1572872 | tf_op jit(solution)/shard_map/dkv_y/ppermute | solution.py:297
  101.7 27.7 %collective-permute-start.5 = (bf16[8,2,4,32,128]{4,3,2,1,0:T(8,128)(2,1)S(1)}, bf16[8,2,4,32,128]{4,3,2,1,0:T(8,128)(2,1)S(1)}, u32[]{:S(2)}, u32[]{:S(2)}) collective-permute-start(bf16[8,2,4,32,128]{4,3,2,1,0:T(8,128)(2,1)S(1)} %copy-done.6), channel_id=1, source_target_pairs={{0,6},{2,0},{4,2},{6,4},{1,7},{3,1},{5,3},{7,5},{8,14},{10,8},{12,... | collective-permute-start | bytes 1572872 | tf_op jit(solution)/shard_map/dkv_y/ppermute | solution.py:297
  130.6 18.4 %all-to-all-start.3 = ((bf16[8,2,4,32,128]{4,3,2,1,0:T(8,128)(2,1)}), bf16[8,2,4,32,128]{4,3,2,1,0:T(8,128)(2,1)S(1)}, u32[]{:S(2)}, u32[]{:S(2)}) async-start(bf16[8,2,4,32,128]{4,3,2,1,0:T(8,128)(2,1)} %add_convert_fusion), calls=%async_computation.3 | async-start | bytes 1048576 | tf_op jit(solution)/shard_map/all_to_all | solution.py:302
  149.0 0.8 copy-start.11

commit v3 on v2

--- a/solution.py
+++ b/solution.py
@@ -14,15 +14,16 @@
 TILE = 256
 MOST = 1024
 LAG = (MOST // BLK + 1 + TILE // BLK - 2) // (TILE // BLK) + 1
-RING = LAG + 1
+RING = LAG
 NEG = -1e30
 
 
 def attend(*refs, docs, slots, group, xs, ys, zs):
     assign_ref, len_ref, coord_ref, qd_in = refs[:4]
-    kv_in, od_out, dkv_out = refs[4:4 + ys], refs[4 + ys], refs[5 + ys:5 + 2 * ys]
+    parts = ys * zs
+    kv_in, od_out, dkv_out = refs[4:4 + parts], refs[4 + parts], refs[5 + parts:5 + 2 * parts]
     (qd, kv, od, dkv, dk, dv, ot, dqt, e_scr, dp_scr, tile_top, top_s, sum_s, del_s, from_s, place_s,
-     unit_block, unit_tile, qd_sem, kv_sem, od_sem, dkv_sem) = refs[5 + 2 * ys:]
+     unit_block, unit_tile, qd_sem, kv_sem, od_sem, dkv_sem) = refs[5 + 2 * parts:]
     scale = HEAD ** -0.5
     steep = scale * math.log2(math.e)
     per = slots // (xs * ys * zs)
@@ -34,22 +35,22 @@
     NN = (((1,), (0,)), ((), ()))
     dot = functools.partial(lax.dot_general, preferred_element_type=jnp.float32)
 
-    y = coord_ref[0] // zs
-
-    def each_block(k, act):
-        def one(n, carry):
-            c, j = n // per, n % per
-            owner = (c // zs * ys + lax.rem(y + k, ys)) * zs + c % zs
-            act(assign_ref[owner * per + j], c, j)
-            return carry
-
-        lax.fori_loop(0, slots // ys, one, 0, unroll=8)
+    y, z = coord_ref[0] // zs, coord_ref[0] % zs
+
+    def each_block(k, w, act):
+        base = (lax.rem(y + k, ys) * zs + lax.rem(z + w, zs)) * per
+        for x in range(xs):
+            for j in range(per):
+                act(assign_ref[base + (x * ys * zs * per + j)], x, j)
 
     for k in range(ys):
-        each_block(
-            (ys - k) % ys,
-            lambda b, c, j: pltpu.make_async_copy(kv_in[k].at[c, :, j], kv.at[b], kv_sem).start(),
-        )
+        for w in range(zs):
+            part = kv_in[k * zs + w]
+            each_block(
+                (ys - k) % ys,
+                w,
+                lambda b, x, j: pltpu.make_async_copy(part.at[x, :, j], kv.at[b], kv_sem).start(),
+            )
     qd_copy = pltpu.make_async_copy(qd_in, qd, qd_sem)
     qd_copy.start()
 
@@ -122,10 +123,30 @@
 
     qd_copy.wait()
 
-    def step(u, carry):
+    def scores(u, spot):
+        i = unit_block[u + LAG]
+        t = unit_tile[u + LAG]
+        s = dot(keys(t), rows_of(i, 0), NT)
+        dp = dot(values(t), rows_of(i, 1), NT)
+        s = jnp.where((key >= from_s[i] - t * TILE) & (key <= place_s[i] - t * TILE), s, NEG)
+        top = jnp.max(jnp.max(s.reshape(TILE // 8, 8, rows), axis=0), axis=0, keepdims=True)
+        e = jnp.exp2((s - top) * steep)
+        tile_sum = jnp.sum(jnp.sum(e.reshape(TILE // 8, 8, rows), axis=0), axis=0, keepdims=True)
+        tile_del = jnp.sum(jnp.sum((e * dp).reshape(TILE // 8, 8, rows), axis=0), axis=0, keepdims=True)
+        e_scr[spot] = e
+        dp_scr[spot] = dp
+        tile_top[spot] = top
+        was = top_s[i]
+        now = jnp.maximum(was, top)
+        keep = jnp.exp2((was - now) * steep)
+        take = jnp.exp2((top - now) * steep)
+        top_s[i] = now
+        sum_s[i] = sum_s[i] * keep + tile_sum * take
+        del_s[i] = del_s[i] * keep + tile_del * take
+
+    def grads(u, spot):
         old = unit_block[u]
         t = unit_tile[u]
-        spot = lax.rem(u + RING - LAG, RING)
         total = 1.0 / sum_s[old]
         weight = jnp.exp2((tile_top[spot] - top_s[old]) * steep) * total
         delta = del_s[old] * total
@@ -137,26 +158,10 @@
         dv[t] += dot(pb, rows_of(old, 1), NN)
         dk[t] += dot(ds, rows_of(old, 0), NN)
 
-        i = unit_block[u + LAG]
-        t = unit_tile[u + LAG]
+    def step(u, carry):
         spot = lax.rem(u, RING)
-        s = dot(keys(t), rows_of(i, 0), NT)
-        dp = dot(values(t), rows_of(i, 1), NT)
-        s = jnp.where((key >= from_s[i] - t * TILE) & (key <= place_s[i] - t * TILE), s, NEG)
-        top = jnp.max(jnp.max(s.reshape(TILE // 8, 8, rows), axis=0), axis=0, keepdims=True)
-        e = jnp.exp2((s - top) * steep)
-        e_scr[spot] = e
-        dp_scr[spot] = dp
-        tile_top[spot] = top
-        tile_sum = jnp.sum(jnp.sum(e.reshape(TILE // 8, 8, rows), axis=0), axis=0, keepdims=True)
-        tile_del = jnp.sum(jnp.sum((e * dp).reshape(TILE // 8, 8, rows), axis=0), axis=0, keepdims=True)
-        was = top_s[i]
-        now = jnp.maximum(was, top)
-        keep = jnp.exp2((was - now) * steep)
-        take = jnp.exp2((top - now) * steep)
-        top_s[i] = now
-        sum_s[i] = sum_s[i] * keep + tile_sum * take
-        del_s[i] = del_s[i] * keep + tile_del * take
+        grads(u, spot)
+        scores(u, spot)
         return carry
 
     lax.fori_loop(0, units, step, 0)
@@ -169,9 +174,11 @@
 
     lax.fori_loop(0, tiles, gone, 0, unroll=2)
     for k in range(ys):
-        each_block(
-            k, lambda b, c, j: pltpu.make_async_copy(dkv.at[b], dkv_out[k].at[c, :, j], dkv_sem).start()
-        )
+        for w in range(zs):
+            part = dkv_out[k * zs + w]
+            each_block(
+                k, w, lambda b, x, j: pltpu.make_async_copy(dkv.at[b], part.at[x, :, j], dkv_sem).start()
+            )
 
     def rows_out(i, carry):
         od[i // per, 0, i % per] = ot[i].T.astype(jnp.bfloat16).reshape(group, BLK, HEAD)
@@ -188,18 +195,18 @@
 def attention(assign, lengths, coord, qd, kv, *, xs, ys, zs):
     blocks = qd.shape[0] * qd.shape[2]
     group = qd.shape[3]
-    slots = ys * kv[0].shape[0] * kv[0].shape[2]
+    slots = len(kv) * kv[0].shape[0] * kv[0].shape[2]
     tiles = slots * BLK // TILE
     rows = group * BLK
     f32, bf, i32 = jnp.float32, jnp.bfloat16, jnp.int32
     body = functools.partial(attend, docs=lengths.shape[0], slots=slots, group=group, xs=xs, ys=ys, zs=zs)
     smem = pl.BlockSpec(memory_space=pltpu.SMEM)
-    anywhere = pl.BlockSpec(memory_space=pl.ANY)
+    far = pl.BlockSpec(memory_space=pltpu.HBM)
     return pl.pallas_call(
         body,
         out_shape=[jax.ShapeDtypeStruct(a.shape, bf) for a in (qd, *kv)],
-        in_specs=[smem] * 3 + [anywhere] * (1 + ys),
-        out_specs=[anywhere] * (1 + ys),
+        in_specs=[smem] * 3 + [far] * (1 + len(kv)),
+        out_specs=[far] * (1 + len(kv)),
         scratch_shapes=[
             pltpu.VMEM(qd.shape, bf), pltpu.VMEM((slots, 2, BLK, HEAD), bf),
             pltpu.VMEM(qd.shape, bf), pltpu.VMEM((slots, 2, BLK, HEAD), bf),
@@ -213,7 +220,7 @@
             pltpu.SMEM((blocks * LAG + 2 * LAG,), i32), pltpu.SMEM((blocks * LAG + 2 * LAG,), i32),
             pltpu.SemaphoreType.DMA, pltpu.SemaphoreType.DMA, pltpu.SemaphoreType.DMA, pltpu.SemaphoreType.DMA,
         ],
-        compiler_params=pltpu.CompilerParams(vmem_limit_bytes=40 << 20),
+        compiler_params=pltpu.CompilerParams(vmem_limit_bytes=63 << 20),
         cost_estimate=pl.CostEstimate(flops=10 ** 9, bytes_accessed=8 << 20, transcendentals=0),
         name="attend",
     )(assign, lengths, coord, qd, *kv)
@@ -267,6 +274,7 @@
         functools.partial(line_up, xs=xs, per=per, heads=heads, copies=copies),
         out_shape=(out, out),
         cost_estimate=pl.CostEstimate(flops=10 ** 6, bytes_accessed=2 * a.size, transcendentals=0),
+        compiler_params=pltpu.CompilerParams(vmem_limit_bytes=16 << 20),
         name="gather",
     )(a)
 
@@ -283,23 +291,24 @@
     xs, ys, zs = (lax.axis_size(name) for name in (X, Y, Z))
     coord = lax.axis_index((Y, Z)).reshape(1).astype(jnp.int32)
 
-    kv = spread(key_state_rows, value_state_rows, xs, zs)
-    kv = lax.all_to_all(kv, (X, Z), 0, 0, tiled=True)
+    kv = spread(key_state_rows, value_state_rows, xs, 1)
+    kv = lax.all_to_all(kv, X, 0, 0, tiled=True)
     qd = spread(queries, out_grad, xs, 1)
-    with jax.named_scope("kv_y"):
-        kv = [kv] + [lax.ppermute(kv, Y, shift(k, ys)) for k in range(1, ys)]
-    with jax.named_scope("qd_x"):
-        qd = lax.all_to_all(qd, X, 0, 0, tiled=True)
+    kv = [kv] + [lax.ppermute(kv, Z, shift(w, zs)) for w in range(1, zs)]
+    kv = [part if k == 0 else lax.ppermute(part, Y, shift(k, ys)) for k in range(ys) for part in kv]
+    qd = lax.all_to_all(qd, X, 0, 0, tiled=True)
 
     od, *dkv = attention(assignment, doc_lengths, coord, qd, kv, xs=xs, ys=ys, zs=zs)
 
-    with jax.named_scope("dkv_y"):
-        dkv = dkv[:1] + [lax.ppermute(dkv[k], Y, shift(k, ys)) for k in range(1, ys)]
-    with jax.named_scope("od_x"):
-        od = lax.all_to_all(od, X, 0, 0, tiled=True)
-    dkv = sum(part.astype(jnp.float32) for part in dkv).astype(jnp.bfloat16)
+    def over_y(w):
+        terms = [dkv[w]] + [lax.ppermute(dkv[k * zs + w], Y, shift(k, ys)) for k in range(1, ys)]
+        return sum(part.astype(jnp.float32) for part in terms)
+
+    other = [lax.ppermute(over_y(w).astype(jnp.bfloat16), Z, shift(w, zs)) for w in range(1, zs)]
+    od = lax.all_to_all(od, X, 0, 0, tiled=True)
+    dkv = sum([part.astype(jnp.float32) for part in other], over_y(0)).astype(jnp.bfloat16)
     dkv, od = lax.optimization_barrier((dkv, od))
-    dkv = lax.all_to_all(dkv, (X, Z), 0, 0, tiled=True)
+    dkv = lax.all_to_all(dkv, X, 0, 0, tiled=True)
     return (*gather(od, xs), *gather(dkv, xs))
 
 

time: 154 us -> 131 us (0.85)
  the two profiles are of different devices: /device:TPU:32 before, /device:TPU:24 now
where the time goes in v3:
time: 131 us; the launch traced here: 130 us
  waiting for transfers between devices  55.7 us (43%)
  starting transfers between devices  37.8 us (29%)
  Pallas kernels  34.5 us (26%)
    pallas_call x1, Pallas kernels, attention(): pl.pallas_call(body, out_shape=[jax.ShapeDtypeStruct(a.shape, bf) for a i...  26.9 us
    ppermute x6, waiting for transfers between devices, over_y(): lax.ppermute(dkv[k * zs + w], Y, shift(k, ys))  21.9 us
    ppermute x6, waiting for transfers between devices, body(): lax.ppermute(part, Y, shift(k, ys))  17.3 us
    ppermute x6, starting transfers between devices, over_y(): lax.ppermute(dkv[k * zs + w], Y, shift(k, ys))  8.16 us
    ppermute x1, starting transfers between devices, body(): kv = [kv] + [lax.ppermute(kv, Z, shift(w, zs)) for w in range(1, zs)]  7.28 us
    ppermute x1, waiting for transfers between devices, body(): lax.ppermute(over_y(w).astype(jnp.bfloat16), Z, shift(w, zs))  6.07 us
    ppermute x6, starting transfers between devices, body(): lax.ppermute(part, Y, shift(k, ys))  5.55 us
    pallas_call x2, Pallas kernels, spread(): pl.pallas_call(functools.partial(lay_out, xs=xs, per=per, heads=heads, co...  4.95 us
  transfers between devices with their start and end apart: 18, of which 12 were waited for; matrix products, arithmetic and copies ran while one was open for 1% of the time, Pallas kernels for 4%

profile of v3, /device:TPU:24, one launch (start us, length us, event | category | flops | bytes accessed | tf_op | source)
XLA Modules:
  0.0 130.4 jit_solution(9720372740550561237)
XLA Ops:
  0.6 1.7 %spread.3 = bf16[4,2,4,32,128]{4,3,2,1,0:T(8,128)(2,1)} custom-call(bf16[128,512]{1,0:T(8,128)(2,1)} %a_ref.3, bf16[128,512]{1,0:T(8,128)(2,1)} %b_ref.3), custom_call_target="tpu_custom_call" | custom-call | flops 1000000 | bytes 262144 | tf_op jit(solution)/shard_map/spread/pallas_call | solution.py:246
  2.3 4.3 %all-to-all-start.1 = ((bf16[4,2,4,32,128]{4,3,2,1,0:T(8,128)(2,1)}), bf16[4,2,4,32,128]{4,3,2,1,0:T(8,128)(2,1)S(1)}, u32[]{:S(2)}, u32[]{:S(2)}) async-start(bf16[4,2,4,32,128]{4,3,2,1,0:T(8,128)(2,1)} %spread.3), calls=%async_computation.1 | async-start | bytes 524288 | tf_op jit(solution)/shard_map/all_to_all | solution.py:295
  6.6 3.2 %spread.2 = bf16[4,2,4,8,32,128]{5,4,3,2,1,0:T(8,128)(2,1)} custom-call(bf16[128,4096]{1,0:T(8,128)(2,1)} %a_ref.2, bf16[128,4096]{1,0:T(8,128)(2,1)} %b_ref.2), custom_call_target="tpu_custom_call" | custom-call | flops 1000000 | bytes 2097152 | tf_op jit(solution)/shard_map/spread/pallas_call | solution.py:246
  9.9 3.4 %all-to-all-done.1.refs_4_ = bf16[4,2,4,32,128]{4,3,2,1,0:T(8,128)(2,1)S(1)} async-done(((bf16[4,2,4,32,128]{4,3,2,1,0:T(8,128)(2,1)}), bf16[4,2,4,32,128]{4,3,2,1,0:T(8,128)(2,1)S(1)}, u32[]{:S(2)}, u32[]{:S(2)}) %all-to-all-start.1) | async-done | bytes 262176 | tf_op jit(solution)/shard_map/all_to_all | solution.py:295
  13.3 4.4 %all-to-all-start = ((bf16[4,2,4,8,32,128]{5,4,3,2,1,0:T(8,128)(2,1)}), bf16[4,2,4,8,32,128]{5,4,3,2,1,0:T(8,128)(2,1)}, u32[]{:S(2)}, u32[]{:S(2)}) async-start(bf16[4,2,4,8,32,128]{5,4,3,2,1,0:T(8,128)(2,1)} %spread.2), calls=%async_computation | async-start | bytes 4194304 | tf_op jit(solution)/shard_map/all_to_all | solution.py:299
  17.8 7.3 %collective-permute-start = (bf16[4,2,4,32,128]{4,3,2,1,0:T(8,128)(2,1)S(1)}, bf16[4,2,4,32,128]{4,3,2,1,0:T(8,128)(2,1)S(1)}, u32[]{:S(2)}, u32[]{:S(2)}) collective-permute-start(bf16[4,2,4,32,128]{4,3,2,1,0:T(8,128)(2,1)S(1)} %all-to-all-done.1.refs_4_), channel_id=1, source_target_pairs={{0,1},{1,0},{2,3},{3,2},{4,5},{5,4},{6,7},{7,6},{8,9},{9,8},{10,11... | collective-permute-start | bytes 786440 | tf_op jit(solution)/shard_map/ppermute | solution.py:297
  25.0 0.7 collective-permute-start.5
  25.8 0.9 collective-permute-start.3
  26.7 2.2 %collective-permute-start.1 = (bf16[4,2,4,32,128]{4,3,2,1,0:T(8,128)(2,1)S(1)}, bf16[4,2,4,32,128]{4,3,2,1,0:T(8,128)(2,1)S(1)}, u32[]{:S(2)}, u32[]{:S(2)}) collective-permute-start(bf16[4,2,4,32,128]{4,3,2,1,0:T(8,128)(2,1)S(1)} %all-to-all-done.1.refs_4_), channel_id=1, source_target_pairs={{0,2},{2,4},{4,6},{6,0},{1,3},{3,5},{5,7},{7,1},{8,10},{10,12},{12... | collective-permute-start | bytes 786440 | tf_op jit(solution)/shard_map/ppermute | solution.py:298
  28.9 2.2 %collective-permute-done.refs_5_ = bf16[4,2,4,32,128]{4,3,2,1,0:T(8,128)(2,1)S(1)} collective-permute-done((bf16[4,2,4,32,128]{4,3,2,1,0:T(8,128)(2,1)S(1)}, bf16[4,2,4,32,128]{4,3,2,1,0:T(8,128)(2,1)S(1)}, u32[]{:S(2)}, u32[]{:S(2)}) %collective-permute-start) | collective-permute-done | bytes 262176 | tf_op jit(solution)/shard_map/ppermute | solution.py:297
  31.1 0.7 collective-permute-start.6
  31.8 0.9 collective-permute-start.4
  32.8 8.3 %collective-permute-done.5.refs_10_ = bf16[4,2,4,32,128]{4,3,2,1,0:T(8,128)(2,1)S(1)} collective-permute-done((bf16[4,2,4,32,128]{4,3,2,1,0:T(8,128)(2,1)S(1)}, bf16[4,2,4,32,128]{4,3,2,1,0:T(8,128)(2,1)S(1)}, u32[]{:S(2)}, u32[]{:S(2)}) %collective-permute-start.5) | collective-permute-done | bytes 262176 | tf_op jit(solution)/shard_map/ppermute | solution.py:298
  41.1 0.8 collective-permute-done.1.refs_6_
  41.9 7.6 %collective-permute-done.6.refs_11_ = bf16[4,2,4,32,128]{4,3,2,1,0:T(8,128)(2,1)S(1)} collective-permute-done((bf16[4,2,4,32,128]{4,3,2,1,0:T(8,128)(2,1)S(1)}, bf16[4,2,4,32,128]{4,3,2,1,0:T(8,128)(2,1)S(1)}, u32[]{:S(2)}, u32[]{:S(2)}) %collective-permute-start.6) | collective-permute-done | bytes 262176 | tf_op jit(solution)/shard_map/ppermute | solution.py:298
  49.5 0.6 collective-permute-done.2.refs_7_
  50.8 26.9 %attend.1 = (bf16[4,2,4,8,32,128]{5,4,3,2,1,0:T(8,128)(2,1)}, bf16[4,2,4,32,128]{4,3,2,1,0:T(8,128)(2,1)}, bf16[4,2,4,32,128]{4,3,2,1,0:T(8,128)(2,1)}, bf16[4,2...) custom-call(s32[128]{0:T(128)} %refs_0_.1, ...), custom_call_target="tpu_custom_call" | custom-call | flops 1000000000 | bytes 8388608 | tf_op jit(solution)/shard_map/attend/pallas_call | solution.py:205
  77.8 4.5 %all-to-all-start.2 = ((bf16[4,2,4,8,32,128]{5,4,3,2,1,0:T(8,128)(2,1)}), bf16[4,2,4,8,32,128]{5,4,3,2,1,0:T(8,128)(2,1)S(1)}, u32[]{:S(2)}, u32[]{:S(2)}) async-start(bf16[4,2,4,8,32,128]{5,4,3,2,1,0:T(8,128)(2,1)} %get-tuple-element.27), calls=%async_computation.2 | async-start | bytes 4194304 | tf_op jit(solution)/shard_map/all_to_all | solution.py:308
  82.3 2.6 %collective-permute-start.10 = (bf16[4,2,4,32,128]{4,3,2,1,0:T(8,128)(2,1)}, bf16[4,2,4,32,128]{4,3,2,1,0:T(8,128)(2,1)S(1)}, u32[]{:S(2)}, u32[]{:S(2)}) collective-permute-start(bf16[4,2,4,32,128]{4,3,2,1,0:T(8,128)(2,1)} %get-tuple-element.24), channel_id=1, source_target_pairs={{0,2},{2,4},{4,6},{6,0},{1,3},{3,5},{5,7},{7,1},{8,10},{10,12},{12... | collective-permute-start | bytes 786440 | tf_op jit(solution)/shard_map/ppermute | solution.py:304
  84.9 0.9 collective-permute-start.12
  85.8 2.4 %collective-permute-start.7 = (bf16[4,2,4,32,128]{4,3,2,1,0:T(8,128)(2,1)S(1)}, bf16[4,2,4,32,128]{4,3,2,1,0:T(8,128)(2,1)S(1)}, u32[]{:S(2)}, u32[]{:S(2)}) collective-permute-start(bf16[4,2,4,32,128]{4,3,2,1,0:T(8,128)(2,1)S(1)} %copy-done.12), channel_id=1, source_target_pairs={{0,2},{2,4},{4,6},{6,0},{1,3},{3,5},{5,7},{7,1},{8,10},{10,12},{12... | collective-permute-start | bytes 786440 | tf_op jit(solution)/shard_map/ppermute | solution.py:304
  88.2 2.3 %collective-permute-start.8 = (bf16[4,2,4,32,128]{4,3,2,1,0:T(8,128)(2,1)S(1)}, bf16[4,2,4,32,128]{4,3,2,1,0:T(8,128)(2,1)S(1)}, u32[]{:S(2)}, u32[]{:S(2)}) collective-permute-start(bf16[4,2,4,32,128]{4,3,2,1,0:T(8,128)(2,1)S(1)} %copy-done.11), channel_id=1, source_target_pairs={{0,4},{2,6},{4,0},{6,2},{1,5},{3,7},{5,1},{7,3},{8,12},{10,14},{12... | collective-permute-start | bytes 786440 | tf_op jit(solution)/shard_map/ppermute | solution.py:304
  90.5 6.7 %collective-permute-done.10 = bf16[4,2,4,32,128]{4,3,2,1,0:T(8,128)(2,1)S(1)} collective-permute-done((bf16[4,2,4,32,128]{4,3,2,1,0:T(8,128)(2,1)}, bf16[4,2,4,32,128]{4,3,2,1,0:T(8,128)(2,1)S(1)}, u32[]{:S(2)}, u32[]{:S(2)}) %collective-permute-start.10) | collective-permute-done | bytes 262176 | tf_op jit(solution)/shard_map/ppermute | solution.py:304
  97.2 3.9 %collective-permute-done.12 = bf16[4,2,4,32,128]{4,3,2,1,0:T(8,128)(2,1)S(1)} collective-permute-done((bf16[4,2,4,32,128]{4,3,2,1,0:T(8,128)(2,1)}, bf16[4,2,4,32,128]{4,3,2,1,0:T(8,128)(2,1)S(1)}, u32[]{:S(2)}, u32[]{:S(2)}) %collective-permute-start.12) | collective-permute-done | bytes 262176 | tf_op jit(solution)/shard_map/ppermute | solution.py:304
  101.4 7.1 %collective-permute-done.7 = bf16[4,2,4,32,128]{4,3,2,1,0:T(8,128)(2,1)S(1)} collective-permute-done((bf16[4,2,4,32,128]{4,3,2,1,0:T(8,128)(2,1)S(1)}, bf16[4,2,4,32,128]{4,3,2,1,0:T(8,128)(2,1)S(1)}, u32[]{:S(2)}, u32[]{:S(2)}) %collective-permute-start.7) | collective-permute-done | bytes 262176 | tf_op jit(solution)/shard_map/ppermute | solution.py:304
  108.5 4.2 %collective-permute-done.9 = bf16[4,2,4,32,128]{4,3,2,1,0:T(8,128)(2,1)S(1)} collective-permute-done((bf16[4,2,4,32,128]{4,3,2,1,0:T(8,128)(2,1)S(1)}, bf16[4,2,4,32,128]{4,3,2,1,0:T(8,128)(2,1)S(1)}, u32[]{:S(2)}, u32[]{:S(2)}) %collective-permute-start.9) | collective-permute-done | bytes 262176 | tf_op jit(solution)/shard_map/ppermute | solution.py:304
  112.7 6.1 %collective-permute-done.13 = bf16[4,2,4,32,128]{4,3,2,1,0:T(8,128)(2,1)S(1)} collective-permute-done((bf16[4,2,4,32,128]{4,3,2,1,0:T(8,128)(2,1)S(1)}, bf16[4,2,4,32,128]{4,3,2,1,0:T(8,128)(2,1)S(1)}, u32[]{:S(2)}, u32[]{:S(2)}) %collective-permute-start.13) | collective-permute-done | bytes 262176 | tf_op jit(solution)/shard_map/ppermute | solution.py:307
  118.7 0.9 add_convert_fusion
  119.6 3.4 %all-to-all-start.3 = ((bf16[4,2,4,32,128]{4,3,2,1,0:T(8,128)(2,1)}), bf16[4,2,4,32,128]{4,3,2,1,0:T(8,128)(2,1)S(1)}, u32[]{:S(2)}, u32[]{:S(2)}) async-start(bf16[4,2,4,32,128]{4,3,2,1,0:T(8,128)(2,1)} %add_convert_fusion), calls=%async_computation.3 | async-start | bytes 524288 | tf_op jit(solution)/shard_map/all_to_all | solution.py:311
  123.0 1.9 %gather.2 = (bf16[128,4096]{1,0:T(8,128)(2,1)}, bf16[128,4096]{1,0:T(8,128)(2,1)}) custom-call(bf16[4,2,4,8,32,128]{5,4,3,2,1,0:T(8,128)(2,1)S(1)} %all-to-all-done.2.a_ref), custom_call_target="tpu_custom_call" | custom-call | flops 1000000 | bytes 2097152 | tf_op jit(solution)/shard_map/gather/pallas_call | solution.py:273
  124.9 4.8 %all-to-all-done.3.a_ref = bf16[4,2,4,32,128]{4,3,2,1,0:T(8,128)(2,1)S(1)} async-done(((bf16[4,2,4,32,128]{4,3,2,1,0:T(8,128)(2,1)}), bf16[4,2,4,32,128]{4,3,2,1,0:T(8,128)(2,1)S(1)}, u32[]{:S(2)}, u32[]{:S(2)}) %all-to-all-start.3) | async-done | bytes 262176 | tf_op jit(solution)/shard_map/all_to_all | solution.py:311
  129.7 0.7 gather.3
  (37 shorter events, 1.0 us)
Async XLA Ops:
  2.3 11.0 %all-to-all-start.1 = ((bf16[4,2,4,32,128]{4,3,2,1,0:T(8,128)(2,1)}), bf16[4,2,4,32,128]{4,3,2,1,0:T(8,128)(2,1)S(1)}, u32[]{:S(2)}, u32[]{:S(2)}) async-start(bf16[4,2,4,32,128]{4,3,2,1,0:T(8,128)(2,1)} %spread.3), calls=%async_computation.1 | async-start | bytes 524288 | tf_op jit(solution)/shard_map/all_to_all | solution.py:295
  13.3 13.4 %copy-start = (bf16[4,2,4,32,128]{4,3,2,1,0:T(8,128)(2,1)}, bf16[4,2,4,32,128]{4,3,2,1,0:T(8,128)(2,1)S(1)}, u32[]{:S(2)}) copy-start(bf16[4,2,4,32,128]{4,3,2,1,0:T(8,128)(2,1)S(1)} %all-to-all-done.1.refs_4_) | copy-start | bytes 786436
  13.3 36.8 %all-to-all-start = ((bf16[4,2,4,8,32,128]{5,4,3,2,1,0:T(8,128)(2,1)}), bf16[4,2,4,8,32,128]{5,4,3,2,1,0:T(8,128)(2,1)}, u32[]{:S(2)}, u32[]{:S(2)}) async-start(bf16[4,2,4,8,32,128]{5,4,3,2,1,0:T(8,128)(2,1)} %spread.2), calls=%async_computation | async-start | bytes 4194304 | tf_op jit(solution)/shard_map/all_to_all | solution.py:299
  17.8 13.3 %collective-permute-start = (bf16[4,2,4,32,128]{4,3,2,1,0:T(8,128)(2,1)S(1)}, bf16[4,2,4,32,128]{4,3,2,1,0:T(8,128)(2,1)S(1)}, u32[]{:S(2)}, u32[]{:S(2)}) collective-permute-start(bf16[4,2,4,32,128]{4,3,2,1,0:T(8,128)(2,1)S(1)} %all-to-all-done.1.refs_4_), channel_id=1, source_target_pairs={{0,1},{1,0},{2,3},{3,2},{4,5},{5,4},{6,7},{7,6},{8,9},{9,8},{10,11... | collective-permute-start | bytes 786440 | tf_op jit(solution)/shard_map/ppermute | solution.py:297
  25.0 16.0 %collective-permute-start.5 = (bf16[4,2,4,32,128]{4,3,2,1,0:T(8,128)(2,1)S(1)}, bf16[4,2,4,32,128]{4,3,2,1,0:T(8,128)(2,1)S(1)}, u32[]{:S(2)}, u32[]{:S(2)}) collective-permute-start(bf16[4,2,4,32,128]{4,3,2,1,0:T(8,128)(2,1)S(1)} %all-to-all-done.1.refs_4_), channel_id=1, source_target_pairs={{0,6},{2,0},{4,2},{6,4},{1,7},{3,1},{5,3},{7,5},{8,14},{10,8},{12,... | collective-permute-start | bytes 786440 | tf_op jit(solution)/shard_map/ppermute | solution.py:298
  25.8 15.3 %collective-permute-start.3 = (bf16[4,2,4,32,128]{4,3,2,1,0:T(8,128)(2,1)S(1)}, bf16[4,2,4,32,128]{4,3,2,1,0:T(8,128)(2,1)S(1)}, u32[]{:S(2)}, u32[]{:S(2)}) collective-permute-start(bf16[4,2,4,32,128]{4,3,2,1,0:T(8,128)(2,1)S(1)} %all-to-all-done.1.refs_4_), channel_id=1, source_target_pairs={{0,4},{2,6},{4,0},{6,2},{1,5},{3,7},{5,1},{7,3},{8,12},{10,14},{12... | collective-permute-start | bytes 786440 | tf_op jit(solution)/shard_map/ppermute | solution.py:298
  26.7 15.2 %collective-permute-start.1 = (bf16[4,2,4,32,128]{4,3,2,1,0:T(8,128)(2,1)S(1)}, bf16[4,2,4,32,128]{4,3,2,1,0:T(8,128)(2,1)S(1)}, u32[]{:S(2)}, u32[]{:S(2)}) collective-permute-start(bf16[4,2,4,32,128]{4,3,2,1,0:T(8,128)(2,1)S(1)} %all-to-all-done.1.refs_4_), channel_id=1, source_target_pairs={{0,2},{2,4},{4,6},{6,0},{1,3},{3,5},{5,7},{7,1},{8,10},{10,12},{12... | collective-permute-start | bytes 786440 | tf_op jit(solution)/shard_map/ppermute | solution.py:298
  31.1 19.7 %copy-start.1 = (bf16[4,2,4,32,128]{4,3,2,1,0:T(8,128)(2,1)}, bf16[4,2,4,32,128]{4,3,2,1,0:T(8,128)(2,1)S(1)}, u32[]{:S(2)}) copy-start(bf16[4,2,4,32,128]{4,3,2,1,0:T(8,128)(2,1)S(1)} %collective-permute-done.refs_5_) | copy-start | bytes 786436
  31.1 18.4 %collective-permute-start.6 = (bf16[4,2,4,32,128]{4,3,2,1,0:T(8,128)(2,1)S(1)}, bf16[4,2,4,32,128]{4,3,2,1,0:T(8,128)(2,1)S(1)}, u32[]{:S(2)}, u32[]{:S(2)}) collective-permute-start(bf16[4,2,4,32,128]{4,3,2,1,0:T(8,128)(2,1)S(1)} %collective-permute-done.refs_5_), channel_id=1, source_target_pairs={{0,6},{2,0},{4,2},{6,4},{1,7},{3,1},{5,3},{7,5},{8,14},{10,8},{12,... | collective-permute-start | bytes 786440 | tf_op jit(solution)/shard_map/ppermute | solution.py:298
  31.8 17.6 %collective-permute-start.4 = (bf16[4,2,4,32,128]{4,3,2,1,0:T(8,128)(2,1)S(1)}, bf16[4,2,4,32,128]{4,3,2,1,0:T(8,128)(2,1)S(1)}, u32[]{:S(2)}, u32[]{:S(2)}) collective-permute-start(bf16[4,2,4,32,128]{4,3,2,1,0:T(8,128)(2,1)S(1)} %collective-permute-done.refs_5_), channel_id=1, source_target_pairs={{0,4},{2,6},{4,0},{6,2},{1,5},{3,7},{5,1},{7,3},{8,12},{10,14},{12... | collective-permute-start | bytes 786440 | tf_op jit(solution)/shard_map/ppermute | solution.py:298
  41.0 9.8 %copy-start.2 = (bf16[4,2,4,32,128]{4,3,2,1,0:T(8,128)(2,1)}, bf16[4,2,4,32,128]{4,3,2,1,0:T(8,128)(2,1)S(1)}, u32[]{:S(2)}) copy-start(bf16[4,2,4,32,128]{4,3,2,1,0:T(8,128)(2,1)S(1)} %collective-permute-done.5.refs_10_) | copy-start | bytes 786436
  41.0 9.1 %collective-permute-start.2 = (bf16[4,2,4,32,128]{4,3,2,1,0:T(8,128)(2,1)S(1)}, bf16[4,2,4,32,128]{4,3,2,1,0:T(8,128)(2,1)S(1)}, u32[]{:S(2)}, u32[]{:S(2)}) collective-permute-start(bf16[4,2,4,32,128]{4,3,2,1,0:T(8,128)(2,1)S(1)} %collective-permute-done.refs_5_), channel_id=1, source_target_pairs={{0,2},{2,4},{4,6},{6,0},{1,3},{3,5},{5,7},{7,1},{8,10},{10,12},{12... | collective-permute-start | bytes 786440 | tf_op jit(solution)/shard_map/ppermute | solution.py:298
  41.1 9.8 %copy-start.3 = (bf16[4,2,4,32,128]{4,3,2,1,0:T(8,128)(2,1)}, bf16[4,2,4,32,128]{4,3,2,1,0:T(8,128)(2,1)S(1)}, u32[]{:S(2)}) copy-start(bf16[4,2,4,32,128]{4,3,2,1,0:T(8,128)(2,1)S(1)} %collective-permute-done.3.refs_8_) | copy-start | bytes 786436
  41.9 8.2 %copy-start.4 = (bf16[4,2,4,32,128]{4,3,2,1,0:T(8,128)(2,1)}, bf16[4,2,4,32,128]{4,3,2,1,0:T(8,128)(2,1)S(1)}, u32[]{:S(2)}) copy-start(bf16[4,2,4,32,128]{4,3,2,1,0:T(8,128)(2,1)S(1)} %collective-permute-done.1.refs_6_) | copy-start | bytes 786436
  49.5 0.7 copy-start.5
  49.5 0.8 copy-start.6
  50.1 0.7 copy-start.8
  77.7 8.1 %copy-start.12 = (bf16[4,2,4,32,128]{4,3,2,1,0:T(8,128)(2,1)S(1)}, bf16[4,2,4,32,128]{4,3,2,1,0:T(8,128)(2,1)}, u32[]{:S(2)}) copy-start(bf16[4,2,4,32,128]{4,3,2,1,0:T(8,128)(2,1)} %get-tuple-element.20) | copy-start | bytes 786436
  77.7 10.4 %copy-start.11 = (bf16[4,2,4,32,128]{4,3,2,1,0:T(8,128)(2,1)S(1)}, bf16[4,2,4,32,128]{4,3,2,1,0:T(8,128)(2,1)}, u32[]{:S(2)}) copy-start(bf16[4,2,4,32,128]{4,3,2,1,0:T(8,128)(2,1)} %get-tuple-element.21) | copy-start | bytes 786436
  77.7 19.4 %copy-start.10 = (bf16[4,2,4,32,128]{4,3,2,1,0:T(8,128)(2,1)S(1)}, bf16[4,2,4,32,128]{4,3,2,1,0:T(8,128)(2,1)}, u32[]{:S(2)}) copy-start(bf16[4,2,4,32,128]{4,3,2,1,0:T(8,128)(2,1)} %get-tuple-element.22) | copy-start | bytes 786436
  77.8 23.4 %copy-start.7 = (bf16[4,2,4,32,128]{4,3,2,1,0:T(8,128)(2,1)S(1)}, bf16[4,2,4,32,128]{4,3,2,1,0:T(8,128)(2,1)}, u32[]{:S(2)}) copy-start(bf16[4,2,4,32,128]{4,3,2,1,0:T(8,128)(2,1)} %get-tuple-element.23) | copy-start | bytes 786436
  77.8 41.0 %copy-start.9 = (bf16[4,2,4,32,128]{4,3,2,1,0:T(8,128)(2,1)S(1)}, bf16[4,2,4,32,128]{4,3,2,1,0:T(8,128)(2,1)}, u32[]{:S(2)}) copy-start(bf16[4,2,4,32,128]{4,3,2,1,0:T(8,128)(2,1)} %get-tuple-element.19) | copy-start | bytes 786436
  77.8 41.8 %all-to-all-start.2 = ((bf16[4,2,4,8,32,128]{5,4,3,2,1,0:T(8,128)(2,1)}), bf16[4,2,4,8,32,128]{5,4,3,2,1,0:T(8,128)(2,1)S(1)}, u32[]{:S(2)}, u32[]{:S(2)}) async-start(bf16[4,2,4,8,32,128]{5,4,3,2,1,0:T(8,128)(2,1)} %get-tuple-element.27), calls=%async_computation.2 | async-start | bytes 4194304 | tf_op jit(solution)/shard_map/all_to_all | solution.py:308
  82.3 14.9 %collective-permute-start.10 = (bf16[4,2,4,32,128]{4,3,2,1,0:T(8,128)(2,1)}, bf16[4,2,4,32,128]{4,3,2,1,0:T(8,128)(2,1)S(1)}, u32[]{:S(2)}, u32[]{:S(2)}) collective-permute-start(bf16[4,2,4,32,128]{4,3,2,1,0:T(8,128)(2,1)} %get-tuple-element.24), channel_id=1, source_target_pairs={{0,2},{2,4},{4,6},{6,0},{1,3},{3,5},{5,7},{7,1},{8,10},{10,12},{12... | collective-permute-start | bytes 786440 | tf_op jit(solution)/shard_map/ppermute | solution.py:304
  84.9 12.3 %collective-permute-start.11 = (bf16[4,2,4,32,128]{4,3,2,1,0:T(8,128)(2,1)}, bf16[4,2,4,32,128]{4,3,2,1,0:T(8,128)(2,1)S(1)}, u32[]{:S(2)}, u32[]{:S(2)}) collective-permute-start(bf16[4,2,4,32,128]{4,3,2,1,0:T(8,128)(2,1)} %get-tuple-element.25), channel_id=1, source_target_pairs={{0,4},{2,6},{4,0},{6,2},{1,5},{3,7},{5,1},{7,3},{8,12},{10,14},{12... | collective-permute-start | bytes 786440 | tf_op jit(solution)/shard_map/ppermute | solution.py:304
  84.9 16.2 %collective-permute-start.12 = (bf16[4,2,4,32,128]{4,3,2,1,0:T(8,128)(2,1)}, bf16[4,2,4,32,128]{4,3,2,1,0:T(8,128)(2,1)S(1)}, u32[]{:S(2)}, u32[]{:S(2)}) collective-permute-start(bf16[4,2,4,32,128]{4,3,2,1,0:T(8,128)(2,1)} %get-tuple-element.26), channel_id=1, source_target_pairs={{0,6},{2,0},{4,2},{6,4},{1,7},{3,1},{5,3},{7,5},{8,14},{10,8},{12,... | collective-permute-start | bytes 786440 | tf_op jit(solution)/shard_map/ppermute | solution.py:304
  85.8 22.7 %collective-permute-start.7 = (bf16[4,2,4,32,128]{4,3,2,1,0:T(8,128)(2,1)S(1)}, bf16[4,2,4,32,128]{4,3,2,1,0:T(8,128)(2,1)S(1)}, u32[]{:S(2)}, u32[]{:S(2)}) collective-permute-start(bf16[4,2,4,32,128]{4,3,2,1,0:T(8,128)(2,1)S(1)} %copy-done.12), channel_id=1, source_target_pairs={{0,2},{2,4},{4,6},{6,0},{1,3},{3,5},{5,7},{7,1},{8,10},{10,12},{12... | collective-permute-start | bytes 786440 | tf_op jit(solution)/shard_map/ppermute | solution.py:304
  88.2 20.3 %collective-permute-start.8 = (bf16[4,2,4,32,128]{4,3,2,1,0:T(8,128)(2,1)S(1)}, bf16[4,2,4,32,128]{4,3,2,1,0:T(8,128)(2,1)S(1)}, u32[]{:S(2)}, u32[]{:S(2)}) collective-permute-start(bf16[4,2,4,32,128]{4,3,2,1,0:T(8,128)(2,1)S(1)} %copy-done.11), channel_id=1, source_target_pairs={{0,4},{2,6},{4,0},{6,2},{1,5},{3,7},{5,1},{7,3},{8,12},{10,14},{12... | collective-permute-start | bytes 786440 | tf_op jit(solution)/shard_map/ppermute | solution.py:304
  97.2 15.5 %collective-permute-start.9 = (bf16[4,2,4,32,128]{4,3,2,1,0:T(8,128)(2,1)S(1)}, bf16[4,2,4,32,128]{4,3,2,1,0:T(8,128)(2,1)S(1)}, u32[]{:S(2)}, u32[]{:S(2)}) collective-permute-start(bf16[4,2,4,32,128]{4,3,2,1,0:T(8,128)(2,1)S(1)} %copy-done.10), channel_id=1, source_target_pairs={{0,6},{2,0},{4,2},{6,4},{1,7},{3,1},{5,3},{7,5},{8,14},{10,8},{12,... | collective-permute-start | bytes 786440 | tf_op jit(solution)/shard_map/ppermute | solution.py:304
  101.3 17.5 %collective-permute-start.13 = (bf16[4,2,4,32,128]{4,3,2,1,0:T(8,128)(2,1)S(1)}, bf16[4,2,4,32,128]{4,3,2,1,0:T(8,128)(2,1)S(1)}, u32[]{:S(2)}, u32[]{:S(2)}) collective-permute-start(bf16[4,2,4,32,128]{4,3,2,1,0:T(8,128)(2,1)S(1)} %add_convert_fusion.1), channel_id=1, source_target_pairs={{0,1},{1,0},{2,3},{3,2},{4,5},{5,4},{6,7},{7,6},{8,9},{9,8},{10,11... | collective-permute-start | bytes 786440 | tf_op jit(solution)/shard_map/ppermute | solution.py:307
  119.6 10.1 %all-to-all-start.3 = ((bf16[4,2,4,32,128]{4,3,2,1,0:T(8,128)(2,1)}), bf16[4,2,4,32,128]{4,3,2,1,0:T(8,128)(2,1)S(1)}, u32[]{:S(2)}, u32[]{:S(2)}) async-start(bf16[4,2,4,32,128]{4,3,2,1,0:T(8,128)(2,1)} %add_convert_fusion), calls=%async_computation.3 | async-start | bytes 524288 | tf_op jit(solution)/shard_map/all_to_all | solution.py:311

commit v4 on v3

--- a/solution.py
+++ b/solution.py
@@ -13,7 +13,9 @@
 HEAD = 128
 TILE = 256
 MOST = 1024
-LAG = (MOST // BLK + 1 + TILE // BLK - 2) // (TILE // BLK) + 1
+SPAN = (MOST // BLK + 1 + TILE // BLK - 2) // (TILE // BLK) + 1
+MANY = 4
+LAG = SPAN + MANY - 1
 RING = LAG
 NEG = -1e30
 
@@ -54,9 +56,6 @@
     qd_copy = pltpu.make_async_copy(qd_in, qd, qd_sem)
     qd_copy.start()
 
-    for n in range(LAG):
-        unit_block[n] = blocks
-        unit_tile[n] = 0
     lane = lax.broadcasted_iota(jnp.int32, (1, rows), 1) % BLK
 
     def plan(i, n):
@@ -85,21 +84,7 @@
 
         return lax.fori_loop(start // TILE, (first + BLK - 1) // TILE + 1, unit, n)
 
-    units = lax.fori_loop(0, blocks, plan, jnp.int32(LAG))
-    for n in range(LAG):
-        unit_block[units + n] = blocks
-        unit_tile[units + n] = 0
-    for n in range(RING):
-        e_scr[n] = jnp.zeros((TILE, rows), jnp.float32)
-        dp_scr[n] = jnp.zeros((TILE, rows), jnp.float32)
-        tile_top[n] = jnp.zeros((1, rows), jnp.float32)
-    from_s[blocks] = jnp.zeros((1, rows), jnp.int32)
-    place_s[blocks] = jnp.zeros((1, rows), jnp.int32)
-    top_s[blocks] = jnp.zeros((1, rows), jnp.float32)
-    sum_s[blocks] = jnp.ones((1, rows), jnp.float32)
-    del_s[blocks] = jnp.zeros((1, rows), jnp.float32)
-    ot[blocks] = jnp.zeros((HEAD, rows), jnp.float32)
-    dqt[blocks] = jnp.zeros((HEAD, rows), jnp.float32)
+    units = lax.fori_loop(0, blocks, plan, jnp.int32(0))
 
     def clear(t, carry):
         dk[t] = jnp.zeros((TILE, HEAD), jnp.float32)
@@ -118,14 +103,13 @@
     key = lax.broadcasted_iota(jnp.int32, (TILE, rows), 0)
 
     def rows_of(i, which):
-        i = jnp.minimum(i, blocks - 1)
         return qd[i // per, which, i % per].reshape(rows, HEAD)
 
     qd_copy.wait()
 
     def scores(u, spot):
-        i = unit_block[u + LAG]
-        t = unit_tile[u + LAG]
+        i = unit_block[u]
+        t = unit_tile[u]
         s = dot(keys(t), rows_of(i, 0), NT)
         dp = dot(values(t), rows_of(i, 1), NT)
         s = jnp.where((key >= from_s[i] - t * TILE) & (key <= place_s[i] - t * TILE), s, NEG)
@@ -158,13 +142,34 @@
         dv[t] += dot(pb, rows_of(old, 1), NN)
         dk[t] += dot(ds, rows_of(old, 0), NN)
 
-    def step(u, carry):
+    def first(u, carry):
+        scores(u, u)
+        return carry
+
+    def both(u, carry):
         spot = lax.rem(u, RING)
-        grads(u, spot)
+        grads(u - LAG, spot)
         scores(u, spot)
         return carry
 
-    lax.fori_loop(0, units, step, 0)
+    def last(n, carry):
+        u = units + n
+        grads(u - LAG, lax.rem(u, RING))
+        return carry
+
+    def several(n, carry):
+        u = LAG + odd + MANY * n
+        for m in range(MANY):
+            grads(u + m - LAG, lax.rem(u + m, RING))
+        for m in range(MANY):
+            scores(u + m, lax.rem(u + m, RING))
+        return carry
+
+    odd = lax.rem(units - LAG, MANY)
+    lax.fori_loop(0, LAG, first, 0, unroll=LAG)
+    lax.fori_loop(LAG, LAG + odd, both, 0)
+    lax.fori_loop(0, (units - LAG) // MANY, several, 0)
+    lax.fori_loop(0, LAG, last, 0, unroll=LAG)
 
     def gone(t, carry):
         at = pl.ds(t * tile_blocks, tile_blocks)
@@ -183,13 +188,12 @@
     def rows_out(i, carry):
         od[i // per, 0, i % per] = ot[i].T.astype(jnp.bfloat16).reshape(group, BLK, HEAD)
         od[i // per, 1, i % per] = (dqt[i].T * scale).astype(jnp.bfloat16).reshape(group, BLK, HEAD)
+        pltpu.make_async_copy(od.at[i // per, :, i % per], od_out.at[i // per, :, i % per], od_sem).start()
         return carry
 
     lax.fori_loop(0, blocks, rows_out, 0, unroll=2)
-    od_copy = pltpu.make_async_copy(od, od_out, od_sem)
-    od_copy.start()
     pltpu.make_async_copy(dkv, dkv, dkv_sem).wait()
-    od_copy.wait()
+    pltpu.make_async_copy(od, od, od_sem).wait()
 
 
 def attention(assign, lengths, coord, qd, kv, *, xs, ys, zs):
@@ -211,13 +215,13 @@
             pltpu.VMEM(qd.shape, bf), pltpu.VMEM((slots, 2, BLK, HEAD), bf),
             pltpu.VMEM(qd.shape, bf), pltpu.VMEM((slots, 2, BLK, HEAD), bf),
             pltpu.VMEM((tiles, TILE, HEAD), f32), pltpu.VMEM((tiles, TILE, HEAD), f32),
-            pltpu.VMEM((blocks + 1, HEAD, rows), f32), pltpu.VMEM((blocks + 1, HEAD, rows), f32),
+            pltpu.VMEM((blocks, HEAD, rows), f32), pltpu.VMEM((blocks, HEAD, rows), f32),
             pltpu.VMEM((RING, TILE, rows), f32), pltpu.VMEM((RING, TILE, rows), f32),
             pltpu.VMEM((RING, 1, rows), f32),
-            pltpu.VMEM((blocks + 1, 1, rows), f32), pltpu.VMEM((blocks + 1, 1, rows), f32),
-            pltpu.VMEM((blocks + 1, 1, rows), f32), pltpu.VMEM((blocks + 1, 1, rows), i32),
-            pltpu.VMEM((blocks + 1, 1, rows), i32),
-            pltpu.SMEM((blocks * LAG + 2 * LAG,), i32), pltpu.SMEM((blocks * LAG + 2 * LAG,), i32),
+            pltpu.VMEM((blocks, 1, rows), f32), pltpu.VMEM((blocks, 1, rows), f32),
+            pltpu.VMEM((blocks, 1, rows), f32), pltpu.VMEM((blocks, 1, rows), i32),
+            pltpu.VMEM((blocks, 1, rows), i32),
+            pltpu.SMEM((blocks * SPAN,), i32), pltpu.SMEM((blocks * SPAN,), i32),
             pltpu.SemaphoreType.DMA, pltpu.SemaphoreType.DMA, pltpu.SemaphoreType.DMA, pltpu.SemaphoreType.DMA,
         ],
         compiler_params=pltpu.CompilerParams(vmem_limit_bytes=63 << 20),
@@ -287,7 +291,7 @@
     return [(i, (i + k) % size) for i in range(size)]
 
 
-def body(doc_lengths, assignment, queries, key_state_rows, value_state_rows, out_grad):
+def work(doc_lengths, assignment, queries, key_state_rows, value_state_rows, out_grad):
     xs, ys, zs = (lax.axis_size(name) for name in (X, Y, Z))
     coord = lax.axis_index((Y, Z)).reshape(1).astype(jnp.int32)
 
@@ -295,13 +299,19 @@
     kv = lax.all_to_all(kv, X, 0, 0, tiled=True)
     qd = spread(queries, out_grad, xs, 1)
     kv = [kv] + [lax.ppermute(kv, Z, shift(w, zs)) for w in range(1, zs)]
-    kv = [part if k == 0 else lax.ppermute(part, Y, shift(k, ys)) for k in range(ys) for part in kv]
+    parts = [kv]
+    for k in range(1, ys):
+        own = lax.ppermute(kv[0], Y, shift(k, ys))
+        parts.append([own] + [lax.ppermute(part, Y, shift(k, ys)) for part in kv[1:]])
+    kv = [part for row in parts for part in row]
     qd = lax.all_to_all(qd, X, 0, 0, tiled=True)
 
     od, *dkv = attention(assignment, doc_lengths, coord, qd, kv, xs=xs, ys=ys, zs=zs)
 
     def over_y(w):
-        terms = [dkv[w]] + [lax.ppermute(dkv[k * zs + w], Y, shift(k, ys)) for k in range(1, ys)]
+        terms = [dkv[w]]
+        for k in range(1, ys):
+            terms.append(lax.ppermute(dkv[k * zs + w], Y, shift(k, ys)))
         return sum(part.astype(jnp.float32) for part in terms)
 
     other = [lax.ppermute(over_y(w).astype(jnp.bfloat16), Z, shift(w, zs)) for w in range(1, zs)]
@@ -316,7 +326,7 @@
     finer = Mesh(mesh.devices.reshape(mesh.shape["dp"], 4, 4, 2), DP_CTX)
     rows = P(DP_CTX, None)
     return jax.shard_map(
-        body,
+        work,
         mesh=finer,
         in_specs=(P("dp"), P("dp"), rows, rows, rows, rows),
         out_specs=(rows, rows, rows, rows),

time: 131 us -> 122 us (0.931)
  Pallas kernels: 34.5 us -> 24.5 us
    pallas_call x1, Pallas kernels: 26.9 us -> 17 us  [attention(): pl.pallas_call(body, out_shape=[jax.ShapeDtypeStruct(a.shape, bf) for a i...]
    all_to_all x4, starting transfers between devices: 16.7 us -> 18.5 us  [the longest x1 5.19 us: work(): dkv = lax.all_to_all(dkv, X, 0, 0, tiled=True)]
  transfers between devices with their start and end apart: 18 -> 18, of which waited for: 12 -> 14; matrix products, arithmetic and copies ran while one was open for 1% -> 1% of each run, Pallas kernels for 4% -> 4%
where the time goes in v4:
time: 122 us; the launch traced here: 121 us
  waiting for transfers between devices  55.1 us (45%)
  starting transfers between devices  39.1 us (32%)
  Pallas kernels  24.5 us (20%)
    ppermute x6, waiting for transfers between devices, over_y(): terms.append(lax.ppermute(dkv[k * zs + w], Y, shift(k, ys)))  19.5 us
    pallas_call x1, Pallas kernels, attention(): pl.pallas_call(body, out_shape=[jax.ShapeDtypeStruct(a.shape, bf) for a i...  17 us
    ppermute x3, waiting for transfers between devices, work(): own = lax.ppermute(kv[0], Y, shift(k, ys))  9.12 us
    ppermute x3, waiting for transfers between devices, work(): lax.ppermute(part, Y, shift(k, ys))  8.18 us
    ppermute x1, waiting for transfers between devices, work(): lax.ppermute(over_y(w).astype(jnp.bfloat16), Z, shift(w, zs))  7.91 us
    ppermute x6, starting transfers between devices, over_y(): terms.append(lax.ppermute(dkv[k * zs + w], Y, shift(k, ys)))  7.76 us
    ppermute x1, starting transfers between devices, work(): kv = [kv] + [lax.ppermute(kv, Z, shift(w, zs)) for w in range(1, zs)]  7.28 us
    all_to_all x1, starting transfers between devices, work(): dkv = lax.all_to_all(dkv, X, 0, 0, tiled=True)  5.19 us
  transfers between devices with their start and end apart: 18, of which 14 were waited for; matrix products, arithmetic and copies ran while one was open for 1% of the time, Pallas kernels for 4%

profile of v4, /device:TPU:24, one launch (start us, length us, event | category | flops | bytes accessed | tf_op | source)
XLA Modules:
  0.0 121.3 jit_solution(1130825475030280715)
XLA Ops:
  0.6 1.7 %spread.3 = bf16[4,2,4,32,128]{4,3,2,1,0:T(8,128)(2,1)} custom-call(bf16[128,512]{1,0:T(8,128)(2,1)} %a_ref.3, bf16[128,512]{1,0:T(8,128)(2,1)} %b_ref.3), custom_call_target="tpu_custom_call" | custom-call | flops 1000000 | bytes 262144 | tf_op jit(solution)/shard_map/spread/pallas_call | solution.py:250
  2.3 4.3 %all-to-all-start.1 = ((bf16[4,2,4,32,128]{4,3,2,1,0:T(8,128)(2,1)}), bf16[4,2,4,32,128]{4,3,2,1,0:T(8,128)(2,1)S(1)}, u32[]{:S(2)}, u32[]{:S(2)}) async-start(bf16[4,2,4,32,128]{4,3,2,1,0:T(8,128)(2,1)} %spread.3), calls=%async_computation.1 | async-start | bytes 524288 | tf_op jit(solution)/shard_map/all_to_all | solution.py:299
  6.6 3.2 %spread.2 = bf16[4,2,4,8,32,128]{5,4,3,2,1,0:T(8,128)(2,1)} custom-call(bf16[128,4096]{1,0:T(8,128)(2,1)} %a_ref.2, bf16[128,4096]{1,0:T(8,128)(2,1)} %b_ref.2), custom_call_target="tpu_custom_call" | custom-call | flops 1000000 | bytes 2097152 | tf_op jit(solution)/shard_map/spread/pallas_call | solution.py:250
  9.9 3.4 %all-to-all-done.1.refs_4_ = bf16[4,2,4,32,128]{4,3,2,1,0:T(8,128)(2,1)S(1)} async-done(((bf16[4,2,4,32,128]{4,3,2,1,0:T(8,128)(2,1)}), bf16[4,2,4,32,128]{4,3,2,1,0:T(8,128)(2,1)S(1)}, u32[]{:S(2)}, u32[]{:S(2)}) %all-to-all-start.1) | async-done | bytes 262176 | tf_op jit(solution)/shard_map/all_to_all | solution.py:299
  13.3 4.4 %all-to-all-start = ((bf16[4,2,4,8,32,128]{5,4,3,2,1,0:T(8,128)(2,1)}), bf16[4,2,4,8,32,128]{5,4,3,2,1,0:T(8,128)(2,1)}, u32[]{:S(2)}, u32[]{:S(2)}) async-start(bf16[4,2,4,8,32,128]{5,4,3,2,1,0:T(8,128)(2,1)} %spread.2), calls=%async_computation | async-start | bytes 4194304 | tf_op jit(solution)/shard_map/all_to_all | solution.py:307
  17.8 7.3 %collective-permute-start = (bf16[4,2,4,32,128]{4,3,2,1,0:T(8,128)(2,1)S(1)}, bf16[4,2,4,32,128]{4,3,2,1,0:T(8,128)(2,1)S(1)}, u32[]{:S(2)}, u32[]{:S(2)}) collective-permute-start(bf16[4,2,4,32,128]{4,3,2,1,0:T(8,128)(2,1)S(1)} %all-to-all-done.1.refs_4_), channel_id=1, source_target_pairs={{0,1},{1,0},{2,3},{3,2},{4,5},{5,4},{6,7},{7,6},{8,9},{9,8},{10,11... | collective-permute-start | bytes 786440 | tf_op jit(solution)/shard_map/ppermute | solution.py:301
  25.0 0.7 collective-permute-start.5
  25.8 0.9 collective-permute-start.3
  26.7 2.2 %collective-permute-start.1 = (bf16[4,2,4,32,128]{4,3,2,1,0:T(8,128)(2,1)S(1)}, bf16[4,2,4,32,128]{4,3,2,1,0:T(8,128)(2,1)S(1)}, u32[]{:S(2)}, u32[]{:S(2)}) collective-permute-start(bf16[4,2,4,32,128]{4,3,2,1,0:T(8,128)(2,1)S(1)} %all-to-all-done.1.refs_4_), channel_id=1, source_target_pairs={{0,2},{2,4},{4,6},{6,0},{1,3},{3,5},{5,7},{7,1},{8,10},{10,12},{12... | collective-permute-start | bytes 786440 | tf_op jit(solution)/shard_map/ppermute | solution.py:304
  28.9 2.2 %collective-permute-done.refs_5_ = bf16[4,2,4,32,128]{4,3,2,1,0:T(8,128)(2,1)S(1)} collective-permute-done((bf16[4,2,4,32,128]{4,3,2,1,0:T(8,128)(2,1)S(1)}, bf16[4,2,4,32,128]{4,3,2,1,0:T(8,128)(2,1)S(1)}, u32[]{:S(2)}, u32[]{:S(2)}) %collective-permute-start) | collective-permute-done | bytes 262176 | tf_op jit(solution)/shard_map/ppermute | solution.py:301
  31.1 0.7 collective-permute-start.6
  31.8 0.9 collective-permute-start.4
  32.8 8.3 %collective-permute-done.5.refs_10_ = bf16[4,2,4,32,128]{4,3,2,1,0:T(8,128)(2,1)S(1)} collective-permute-done((bf16[4,2,4,32,128]{4,3,2,1,0:T(8,128)(2,1)S(1)}, bf16[4,2,4,32,128]{4,3,2,1,0:T(8,128)(2,1)S(1)}, u32[]{:S(2)}, u32[]{:S(2)}) %collective-permute-start.5) | collective-permute-done | bytes 262176 | tf_op jit(solution)/shard_map/ppermute | solution.py:304
  41.1 0.8 collective-permute-done.1.refs_6_
  41.9 7.6 %collective-permute-done.6.refs_11_ = bf16[4,2,4,32,128]{4,3,2,1,0:T(8,128)(2,1)S(1)} collective-permute-done((bf16[4,2,4,32,128]{4,3,2,1,0:T(8,128)(2,1)S(1)}, bf16[4,2,4,32,128]{4,3,2,1,0:T(8,128)(2,1)S(1)}, u32[]{:S(2)}, u32[]{:S(2)}) %collective-permute-start.6) | collective-permute-done | bytes 262176 | tf_op jit(solution)/shard_map/ppermute | solution.py:305
  49.5 0.6 collective-permute-done.2.refs_7_
  50.8 17.0 %attend.1 = (bf16[4,2,4,8,32,128]{5,4,3,2,1,0:T(8,128)(2,1)}, bf16[4,2,4,32,128]{4,3,2,1,0:T(8,128)(2,1)}, bf16[4,2,4,32,128]{4,3,2,1,0:T(8,128)(2,1)}, bf16[4,2...) custom-call(s32[128]{0:T(128)} %refs_0_.1, ...), custom_call_target="tpu_custom_call" | custom-call | flops 1000000000 | bytes 8388608 | tf_op jit(solution)/shard_map/attend/pallas_call | solution.py:209
  67.8 4.5 %all-to-all-start.2 = ((bf16[4,2,4,8,32,128]{5,4,3,2,1,0:T(8,128)(2,1)}), bf16[4,2,4,8,32,128]{5,4,3,2,1,0:T(8,128)(2,1)S(1)}, u32[]{:S(2)}, u32[]{:S(2)}) async-start(bf16[4,2,4,8,32,128]{5,4,3,2,1,0:T(8,128)(2,1)} %get-tuple-element.27), calls=%async_computation.2 | async-start | bytes 4194304 | tf_op jit(solution)/shard_map/all_to_all | solution.py:318
  72.4 2.2 %collective-permute-start.10 = (bf16[4,2,4,32,128]{4,3,2,1,0:T(8,128)(2,1)}, bf16[4,2,4,32,128]{4,3,2,1,0:T(8,128)(2,1)S(1)}, u32[]{:S(2)}, u32[]{:S(2)}) collective-permute-start(bf16[4,2,4,32,128]{4,3,2,1,0:T(8,128)(2,1)} %get-tuple-element.24), channel_id=1, source_target_pairs={{0,2},{2,4},{4,6},{6,0},{1,3},{3,5},{5,7},{7,1},{8,10},{10,12},{12... | collective-permute-start | bytes 786440 | tf_op jit(solution)/shard_map/ppermute | solution.py:314
  74.6 0.9 collective-permute-start.12
  75.4 2.4 %collective-permute-start.7 = (bf16[4,2,4,32,128]{4,3,2,1,0:T(8,128)(2,1)S(1)}, bf16[4,2,4,32,128]{4,3,2,1,0:T(8,128)(2,1)S(1)}, u32[]{:S(2)}, u32[]{:S(2)}) collective-permute-start(bf16[4,2,4,32,128]{4,3,2,1,0:T(8,128)(2,1)S(1)} %copy-done.12), channel_id=1, source_target_pairs={{0,2},{2,4},{4,6},{6,0},{1,3},{3,5},{5,7},{7,1},{8,10},{10,12},{12... | collective-permute-start | bytes 786440 | tf_op jit(solution)/shard_map/ppermute | solution.py:314
  77.8 2.3 %collective-permute-start.8 = (bf16[4,2,4,32,128]{4,3,2,1,0:T(8,128)(2,1)S(1)}, bf16[4,2,4,32,128]{4,3,2,1,0:T(8,128)(2,1)S(1)}, u32[]{:S(2)}, u32[]{:S(2)}) collective-permute-start(bf16[4,2,4,32,128]{4,3,2,1,0:T(8,128)(2,1)S(1)} %copy-done.11), channel_id=1, source_target_pairs={{0,4},{2,6},{4,0},{6,2},{1,5},{3,7},{5,1},{7,3},{8,12},{10,14},{12... | collective-permute-start | bytes 786440 | tf_op jit(solution)/shard_map/ppermute | solution.py:314
  80.1 4.9 %collective-permute-done.10 = bf16[4,2,4,32,128]{4,3,2,1,0:T(8,128)(2,1)S(1)} collective-permute-done((bf16[4,2,4,32,128]{4,3,2,1,0:T(8,128)(2,1)}, bf16[4,2,4,32,128]{4,3,2,1,0:T(8,128)(2,1)S(1)}, u32[]{:S(2)}, u32[]{:S(2)}) %collective-permute-start.10) | collective-permute-done | bytes 262176 | tf_op jit(solution)/shard_map/ppermute | solution.py:314
  85.5 5.7 %collective-permute-done.12 = bf16[4,2,4,32,128]{4,3,2,1,0:T(8,128)(2,1)S(1)} collective-permute-done((bf16[4,2,4,32,128]{4,3,2,1,0:T(8,128)(2,1)}, bf16[4,2,4,32,128]{4,3,2,1,0:T(8,128)(2,1)S(1)}, u32[]{:S(2)}, u32[]{:S(2)}) %collective-permute-start.12) | collective-permute-done | bytes 262176 | tf_op jit(solution)/shard_map/ppermute | solution.py:314
  91.4 5.1 %collective-permute-done.7 = bf16[4,2,4,32,128]{4,3,2,1,0:T(8,128)(2,1)S(1)} collective-permute-done((bf16[4,2,4,32,128]{4,3,2,1,0:T(8,128)(2,1)S(1)}, bf16[4,2,4,32,128]{4,3,2,1,0:T(8,128)(2,1)S(1)}, u32[]{:S(2)}, u32[]{:S(2)}) %collective-permute-start.7) | collective-permute-done | bytes 262176 | tf_op jit(solution)/shard_map/ppermute | solution.py:314
  96.7 3.1 %collective-permute-done.9 = bf16[4,2,4,32,128]{4,3,2,1,0:T(8,128)(2,1)S(1)} collective-permute-done((bf16[4,2,4,32,128]{4,3,2,1,0:T(8,128)(2,1)S(1)}, bf16[4,2,4,32,128]{4,3,2,1,0:T(8,128)(2,1)S(1)}, u32[]{:S(2)}, u32[]{:S(2)}) %collective-permute-start.9) | collective-permute-done | bytes 262176 | tf_op jit(solution)/shard_map/ppermute | solution.py:314
  99.9 7.9 %collective-permute-done.13 = bf16[4,2,4,32,128]{4,3,2,1,0:T(8,128)(2,1)S(1)} collective-permute-done((bf16[4,2,4,32,128]{4,3,2,1,0:T(8,128)(2,1)S(1)}, bf16[4,2,4,32,128]{4,3,2,1,0:T(8,128)(2,1)S(1)}, u32[]{:S(2)}, u32[]{:S(2)}) %collective-permute-start.13) | collective-permute-done | bytes 262176 | tf_op jit(solution)/shard_map/ppermute | solution.py:317
  107.8 0.9 add_convert_fusion
  108.6 5.2 %all-to-all-start.3 = ((bf16[4,2,4,32,128]{4,3,2,1,0:T(8,128)(2,1)}), bf16[4,2,4,32,128]{4,3,2,1,0:T(8,128)(2,1)S(1)}, u32[]{:S(2)}, u32[]{:S(2)}) async-start(bf16[4,2,4,32,128]{4,3,2,1,0:T(8,128)(2,1)} %add_convert_fusion), calls=%async_computation.3 | async-start | bytes 524288 | tf_op jit(solution)/shard_map/all_to_all | solution.py:321
  113.8 1.9 %gather.2 = (bf16[128,4096]{1,0:T(8,128)(2,1)}, bf16[128,4096]{1,0:T(8,128)(2,1)}) custom-call(bf16[4,2,4,8,32,128]{5,4,3,2,1,0:T(8,128)(2,1)S(1)} %all-to-all-done.2.a_ref), custom_call_target="tpu_custom_call" | custom-call | flops 1000000 | bytes 2097152 | tf_op jit(solution)/shard_map/gather/pallas_call | solution.py:277
  115.7 4.8 %all-to-all-done.3.a_ref = bf16[4,2,4,32,128]{4,3,2,1,0:T(8,128)(2,1)S(1)} async-done(((bf16[4,2,4,32,128]{4,3,2,1,0:T(8,128)(2,1)}), bf16[4,2,4,32,128]{4,3,2,1,0:T(8,128)(2,1)S(1)}, u32[]{:S(2)}, u32[]{:S(2)}) %all-to-all-start.3) | async-done | bytes 262176 | tf_op jit(solution)/shard_map/all_to_all | solution.py:321
  120.5 0.7 gather.3
  (37 shorter events, 1.8 us)
Async XLA Ops:
  2.3 11.0 %all-to-all-start.1 = ((bf16[4,2,4,32,128]{4,3,2,1,0:T(8,128)(2,1)}), bf16[4,2,4,32,128]{4,3,2,1,0:T(8,128)(2,1)S(1)}, u32[]{:S(2)}, u32[]{:S(2)}) async-start(bf16[4,2,4,32,128]{4,3,2,1,0:T(8,128)(2,1)} %spread.3), calls=%async_computation.1 | async-start | bytes 524288 | tf_op jit(solution)/shard_map/all_to_all | solution.py:299
  13.3 13.4 %copy-start = (bf16[4,2,4,32,128]{4,3,2,1,0:T(8,128)(2,1)}, bf16[4,2,4,32,128]{4,3,2,1,0:T(8,128)(2,1)S(1)}, u32[]{:S(2)}) copy-start(bf16[4,2,4,32,128]{4,3,2,1,0:T(8,128)(2,1)S(1)} %all-to-all-done.1.refs_4_) | copy-start | bytes 786436
  13.3 36.8 %all-to-all-start = ((bf16[4,2,4,8,32,128]{5,4,3,2,1,0:T(8,128)(2,1)}), bf16[4,2,4,8,32,128]{5,4,3,2,1,0:T(8,128)(2,1)}, u32[]{:S(2)}, u32[]{:S(2)}) async-start(bf16[4,2,4,8,32,128]{5,4,3,2,1,0:T(8,128)(2,1)} %spread.2), calls=%async_computation | async-start | bytes 4194304 | tf_op jit(solution)/shard_map/all_to_all | solution.py:307
  17.8 13.3 %collective-permute-start = (bf16[4,2,4,32,128]{4,3,2,1,0:T(8,128)(2,1)S(1)}, bf16[4,2,4,32,128]{4,3,2,1,0:T(8,128)(2,1)S(1)}, u32[]{:S(2)}, u32[]{:S(2)}) collective-permute-start(bf16[4,2,4,32,128]{4,3,2,1,0:T(8,128)(2,1)S(1)} %all-to-all-done.1.refs_4_), channel_id=1, source_target_pairs={{0,1},{1,0},{2,3},{3,2},{4,5},{5,4},{6,7},{7,6},{8,9},{9,8},{10,11... | collective-permute-start | bytes 786440 | tf_op jit(solution)/shard_map/ppermute | solution.py:301
  25.0 16.0 %collective-permute-start.5 = (bf16[4,2,4,32,128]{4,3,2,1,0:T(8,128)(2,1)S(1)}, bf16[4,2,4,32,128]{4,3,2,1,0:T(8,128)(2,1)S(1)}, u32[]{:S(2)}, u32[]{:S(2)}) collective-permute-start(bf16[4,2,4,32,128]{4,3,2,1,0:T(8,128)(2,1)S(1)} %all-to-all-done.1.refs_4_), channel_id=1, source_target_pairs={{0,6},{2,0},{4,2},{6,4},{1,7},{3,1},{5,3},{7,5},{8,14},{10,8},{12,... | collective-permute-start | bytes 786440 | tf_op jit(solution)/shard_map/ppermute | solution.py:304
  25.8 15.3 %collective-permute-start.3 = (bf16[4,2,4,32,128]{4,3,2,1,0:T(8,128)(2,1)S(1)}, bf16[4,2,4,32,128]{4,3,2,1,0:T(8,128)(2,1)S(1)}, u32[]{:S(2)}, u32[]{:S(2)}) collective-permute-start(bf16[4,2,4,32,128]{4,3,2,1,0:T(8,128)(2,1)S(1)} %all-to-all-done.1.refs_4_), channel_id=1, source_target_pairs={{0,4},{2,6},{4,0},{6,2},{1,5},{3,7},{5,1},{7,3},{8,12},{10,14},{12... | collective-permute-start | bytes 786440 | tf_op jit(solution)/shard_map/ppermute | solution.py:304
  26.7 15.2 %collective-permute-start.1 = (bf16[4,2,4,32,128]{4,3,2,1,0:T(8,128)(2,1)S(1)}, bf16[4,2,4,32,128]{4,3,2,1,0:T(8,128)(2,1)S(1)}, u32[]{:S(2)}, u32[]{:S(2)}) collective-permute-start(bf16[4,2,4,32,128]{4,3,2,1,0:T(8,128)(2,1)S(1)} %all-to-all-done.1.refs_4_), channel_id=1, source_target_pairs={{0,2},{2,4},{4,6},{6,0},{1,3},{3,5},{5,7},{7,1},{8,10},{10,12},{12... | collective-permute-start | bytes 786440 | tf_op jit(solution)/shard_map/ppermute | solution.py:304
  31.1 19.7 %copy-start.1 = (bf16[4,2,4,32,128]{4,3,2,1,0:T(8,128)(2,1)}, bf16[4,2,4,32,128]{4,3,2,1,0:T(8,128)(2,1)S(1)}, u32[]{:S(2)}) copy-start(bf16[4,2,4,32,128]{4,3,2,1,0:T(8,128)(2,1)S(1)} %collective-permute-done.refs_5_) | copy-start | bytes 786436
  31.1 18.4 %collective-permute-start.6 = (bf16[4,2,4,32,128]{4,3,2,1,0:T(8,128)(2,1)S(1)}, bf16[4,2,4,32,128]{4,3,2,1,0:T(8,128)(2,1)S(1)}, u32[]{:S(2)}, u32[]{:S(2)}) collective-permute-start(bf16[4,2,4,32,128]{4,3,2,1,0:T(8,128)(2,1)S(1)} %collective-permute-done.refs_5_), channel_id=1, source_target_pairs={{0,6},{2,0},{4,2},{6,4},{1,7},{3,1},{5,3},{7,5},{8,14},{10,8},{12,... | collective-permute-start | bytes 786440 | tf_op jit(solution)/shard_map/ppermute | solution.py:305
  31.8 17.6 %collective-permute-start.4 = (bf16[4,2,4,32,128]{4,3,2,1,0:T(8,128)(2,1)S(1)}, bf16[4,2,4,32,128]{4,3,2,1,0:T(8,128)(2,1)S(1)}, u32[]{:S(2)}, u32[]{:S(2)}) collective-permute-start(bf16[4,2,4,32,128]{4,3,2,1,0:T(8,128)(2,1)S(1)} %collective-permute-done.refs_5_), channel_id=1, source_target_pairs={{0,4},{2,6},{4,0},{6,2},{1,5},{3,7},{5,1},{7,3},{8,12},{10,14},{12... | collective-permute-start | bytes 786440 | tf_op jit(solution)/shard_map/ppermute | solution.py:305
  41.0 9.8 %copy-start.2 = (bf16[4,2,4,32,128]{4,3,2,1,0:T(8,128)(2,1)}, bf16[4,2,4,32,128]{4,3,2,1,0:T(8,128)(2,1)S(1)}, u32[]{:S(2)}) copy-start(bf16[4,2,4,32,128]{4,3,2,1,0:T(8,128)(2,1)S(1)} %collective-permute-done.5.refs_10_) | copy-start | bytes 786436
  41.0 9.1 %collective-permute-start.2 = (bf16[4,2,4,32,128]{4,3,2,1,0:T(8,128)(2,1)S(1)}, bf16[4,2,4,32,128]{4,3,2,1,0:T(8,128)(2,1)S(1)}, u32[]{:S(2)}, u32[]{:S(2)}) collective-permute-start(bf16[4,2,4,32,128]{4,3,2,1,0:T(8,128)(2,1)S(1)} %collective-permute-done.refs_5_), channel_id=1, source_target_pairs={{0,2},{2,4},{4,6},{6,0},{1,3},{3,5},{5,7},{7,1},{8,10},{10,12},{12... | collective-permute-start | bytes 786440 | tf_op jit(solution)/shard_map/ppermute | solution.py:305
  41.1 9.8 %copy-start.3 = (bf16[4,2,4,32,128]{4,3,2,1,0:T(8,128)(2,1)}, bf16[4,2,4,32,128]{4,3,2,1,0:T(8,128)(2,1)S(1)}, u32[]{:S(2)}) copy-start(bf16[4,2,4,32,128]{4,3,2,1,0:T(8,128)(2,1)S(1)} %collective-permute-done.3.refs_8_) | copy-start | bytes 786436
  41.9 8.2 %copy-start.4 = (bf16[4,2,4,32,128]{4,3,2,1,0:T(8,128)(2,1)}, bf16[4,2,4,32,128]{4,3,2,1,0:T(8,128)(2,1)S(1)}, u32[]{:S(2)}) copy-start(bf16[4,2,4,32,128]{4,3,2,1,0:T(8,128)(2,1)S(1)} %collective-permute-done.1.refs_6_) | copy-start | bytes 786436
  49.5 0.7 copy-start.5
  49.5 0.8 copy-start.6
  50.1 0.7 copy-start.8
  67.8 7.6 %copy-start.12 = (bf16[4,2,4,32,128]{4,3,2,1,0:T(8,128)(2,1)S(1)}, bf16[4,2,4,32,128]{4,3,2,1,0:T(8,128)(2,1)}, u32[]{:S(2)}) copy-start(bf16[4,2,4,32,128]{4,3,2,1,0:T(8,128)(2,1)} %get-tuple-element.20) | copy-start | bytes 786436
  67.8 10.0 %copy-start.11 = (bf16[4,2,4,32,128]{4,3,2,1,0:T(8,128)(2,1)S(1)}, bf16[4,2,4,32,128]{4,3,2,1,0:T(8,128)(2,1)}, u32[]{:S(2)}) copy-start(bf16[4,2,4,32,128]{4,3,2,1,0:T(8,128)(2,1)} %get-tuple-element.21) | copy-start | bytes 786436
  67.8 17.2 %copy-start.10 = (bf16[4,2,4,32,128]{4,3,2,1,0:T(8,128)(2,1)S(1)}, bf16[4,2,4,32,128]{4,3,2,1,0:T(8,128)(2,1)}, u32[]{:S(2)}) copy-start(bf16[4,2,4,32,128]{4,3,2,1,0:T(8,128)(2,1)} %get-tuple-element.22) | copy-start | bytes 786436
  67.8 23.3 %copy-start.7 = (bf16[4,2,4,32,128]{4,3,2,1,0:T(8,128)(2,1)S(1)}, bf16[4,2,4,32,128]{4,3,2,1,0:T(8,128)(2,1)}, u32[]{:S(2)}) copy-start(bf16[4,2,4,32,128]{4,3,2,1,0:T(8,128)(2,1)} %get-tuple-element.23) | copy-start | bytes 786436
  67.8 39.9 %copy-start.9 = (bf16[4,2,4,32,128]{4,3,2,1,0:T(8,128)(2,1)S(1)}, bf16[4,2,4,32,128]{4,3,2,1,0:T(8,128)(2,1)}, u32[]{:S(2)}) copy-start(bf16[4,2,4,32,128]{4,3,2,1,0:T(8,128)(2,1)} %get-tuple-element.19) | copy-start | bytes 786436
  67.8 40.8 %all-to-all-start.2 = ((bf16[4,2,4,8,32,128]{5,4,3,2,1,0:T(8,128)(2,1)}), bf16[4,2,4,8,32,128]{5,4,3,2,1,0:T(8,128)(2,1)S(1)}, u32[]{:S(2)}, u32[]{:S(2)}) async-start(bf16[4,2,4,8,32,128]{5,4,3,2,1,0:T(8,128)(2,1)} %get-tuple-element.27), calls=%async_computation.2 | async-start | bytes 4194304 | tf_op jit(solution)/shard_map/all_to_all | solution.py:318
  72.4 12.6 %collective-permute-start.10 = (bf16[4,2,4,32,128]{4,3,2,1,0:T(8,128)(2,1)}, bf16[4,2,4,32,128]{4,3,2,1,0:T(8,128)(2,1)S(1)}, u32[]{:S(2)}, u32[]{:S(2)}) collective-permute-start(bf16[4,2,4,32,128]{4,3,2,1,0:T(8,128)(2,1)} %get-tuple-element.24), channel_id=1, source_target_pairs={{0,2},{2,4},{4,6},{6,0},{1,3},{3,5},{5,7},{7,1},{8,10},{10,12},{12... | collective-permute-start | bytes 786440 | tf_op jit(solution)/shard_map/ppermute | solution.py:314
  74.6 10.9 %collective-permute-start.11 = (bf16[4,2,4,32,128]{4,3,2,1,0:T(8,128)(2,1)}, bf16[4,2,4,32,128]{4,3,2,1,0:T(8,128)(2,1)S(1)}, u32[]{:S(2)}, u32[]{:S(2)}) collective-permute-start(bf16[4,2,4,32,128]{4,3,2,1,0:T(8,128)(2,1)} %get-tuple-element.25), channel_id=1, source_target_pairs={{0,4},{2,6},{4,0},{6,2},{1,5},{3,7},{5,1},{7,3},{8,12},{10,14},{12... | collective-permute-start | bytes 786440 | tf_op jit(solution)/shard_map/ppermute | solution.py:314
  74.6 16.6 %collective-permute-start.12 = (bf16[4,2,4,32,128]{4,3,2,1,0:T(8,128)(2,1)}, bf16[4,2,4,32,128]{4,3,2,1,0:T(8,128)(2,1)S(1)}, u32[]{:S(2)}, u32[]{:S(2)}) collective-permute-start(bf16[4,2,4,32,128]{4,3,2,1,0:T(8,128)(2,1)} %get-tuple-element.26), channel_id=1, source_target_pairs={{0,6},{2,0},{4,2},{6,4},{1,7},{3,1},{5,3},{7,5},{8,14},{10,8},{12,... | collective-permute-start | bytes 786440 | tf_op jit(solution)/shard_map/ppermute | solution.py:314
  75.4 21.0 %collective-permute-start.7 = (bf16[4,2,4,32,128]{4,3,2,1,0:T(8,128)(2,1)S(1)}, bf16[4,2,4,32,128]{4,3,2,1,0:T(8,128)(2,1)S(1)}, u32[]{:S(2)}, u32[]{:S(2)}) collective-permute-start(bf16[4,2,4,32,128]{4,3,2,1,0:T(8,128)(2,1)S(1)} %copy-done.12), channel_id=1, source_target_pairs={{0,2},{2,4},{4,6},{6,0},{1,3},{3,5},{5,7},{7,1},{8,10},{10,12},{12... | collective-permute-start | bytes 786440 | tf_op jit(solution)/shard_map/ppermute | solution.py:314
  77.8 18.9 %collective-permute-start.8 = (bf16[4,2,4,32,128]{4,3,2,1,0:T(8,128)(2,1)S(1)}, bf16[4,2,4,32,128]{4,3,2,1,0:T(8,128)(2,1)S(1)}, u32[]{:S(2)}, u32[]{:S(2)}) collective-permute-start(bf16[4,2,4,32,128]{4,3,2,1,0:T(8,128)(2,1)S(1)} %copy-done.11), channel_id=1, source_target_pairs={{0,4},{2,6},{4,0},{6,2},{1,5},{3,7},{5,1},{7,3},{8,12},{10,14},{12... | collective-permute-start | bytes 786440 | tf_op jit(solution)/shard_map/ppermute | solution.py:314
  85.0 14.9 %collective-permute-start.9 = (bf16[4,2,4,32,128]{4,3,2,1,0:T(8,128)(2,1)S(1)}, bf16[4,2,4,32,128]{4,3,2,1,0:T(8,128)(2,1)S(1)}, u32[]{:S(2)}, u32[]{:S(2)}) collective-permute-start(bf16[4,2,4,32,128]{4,3,2,1,0:T(8,128)(2,1)S(1)} %copy-done.10), channel_id=1, source_target_pairs={{0,6},{2,0},{4,2},{6,4},{1,7},{3,1},{5,3},{7,5},{8,14},{10,8},{12,... | collective-permute-start | bytes 786440 | tf_op jit(solution)/shard_map/ppermute | solution.py:314
  91.3 16.5 %collective-permute-start.13 = (bf16[4,2,4,32,128]{4,3,2,1,0:T(8,128)(2,1)S(1)}, bf16[4,2,4,32,128]{4,3,2,1,0:T(8,128)(2,1)S(1)}, u32[]{:S(2)}, u32[]{:S(2)}) collective-permute-start(bf16[4,2,4,32,128]{4,3,2,1,0:T(8,128)(2,1)S(1)} %add_convert_fusion.1), channel_id=1, source_target_pairs={{0,1},{1,0},{2,3},{3,2},{4,5},{5,4},{6,7},{7,6},{8,9},{9,8},{10,11... | collective-permute-start | bytes 786440 | tf_op jit(solution)/shard_map/ppermute | solution.py:317
  108.6 11.9 %all-to-all-start.3 = ((bf16[4,2,4,32,128]{4,3,2,1,0:T(8,128)(2,1)}), bf16[4,2,4,32,128]{4,3,2,1,0:T(8,128)(2,1)S(1)}, u32[]{:S(2)}, u32[]{:S(2)}) async-start(bf16[4,2,4,32,128]{4,3,2,1,0:T(8,128)(2,1)} %add_convert_fusion), calls=%async_computation.3 | async-start | bytes 524288 | tf_op jit(solution)/shard_map/all_to_all | solution.py:321

commit v5 on v4

--- a/solution.py
+++ b/solution.py
@@ -13,7 +13,8 @@
 HEAD = 128
 TILE = 256
 MOST = 1024
-SPAN = (MOST // BLK + 1 + TILE // BLK - 2) // (TILE // BLK) + 1
+SPAN = MOST // TILE + 1
+PAD = TILE // BLK
 MANY = 4
 LAG = SPAN + MANY - 1
 RING = LAG
@@ -51,7 +52,7 @@
             each_block(
                 (ys - k) % ys,
                 w,
-                lambda b, x, j: pltpu.make_async_copy(part.at[x, :, j], kv.at[b], kv_sem).start(),
+                lambda b, x, j: pltpu.make_async_copy(part.at[x, :, j], kv.at[PAD + b], kv_sem).start(),
             )
     qd_copy = pltpu.make_async_copy(qd_in, qd, qd_sem)
     qd_copy.start()
@@ -79,26 +80,29 @@
 
         def unit(t, n):
             unit_block[n] = i
-            unit_tile[n] = t
+            unit_tile[n] = first // BLK + 1 - t * tile_blocks
             return n + 1
 
-        return lax.fori_loop(start // TILE, (first + BLK - 1) // TILE + 1, unit, n)
+        return lax.fori_loop(0, (first // BLK - start // BLK) // tile_blocks + 1, unit, n)
 
     units = lax.fori_loop(0, blocks, plan, jnp.int32(0))
 
+    nought = jnp.zeros((tile_blocks, BLK, HEAD), jnp.float32)
+    kv[:PAD] = jnp.zeros((PAD, 2, BLK, HEAD), jnp.bfloat16)
+
     def clear(t, carry):
-        dk[t] = jnp.zeros((TILE, HEAD), jnp.float32)
-        dv[t] = jnp.zeros((TILE, HEAD), jnp.float32)
-        return carry
-
-    lax.fori_loop(0, tiles, clear, 0)
-    pltpu.make_async_copy(kv, kv, kv_sem).wait()
+        dk[pl.ds(t * tile_blocks, tile_blocks)] = nought
+        dv[pl.ds(t * tile_blocks, tile_blocks)] = nought
+        return carry
+
+    lax.fori_loop(0, tiles + 1, clear, 0)
+    pltpu.make_async_copy(kv.at[pl.ds(PAD, slots)], kv.at[pl.ds(PAD, slots)], kv_sem).wait()
 
     def keys(t):
-        return kv[pl.ds(t * tile_blocks, tile_blocks), 0].reshape(TILE, HEAD)
+        return kv[pl.ds(t, tile_blocks), 0].reshape(TILE, HEAD)
 
     def values(t):
-        return kv[pl.ds(t * tile_blocks, tile_blocks), 1].reshape(TILE, HEAD)
+        return kv[pl.ds(t, tile_blocks), 1].reshape(TILE, HEAD)
 
     key = lax.broadcasted_iota(jnp.int32, (TILE, rows), 0)
 
@@ -112,7 +116,8 @@
         t = unit_tile[u]
         s = dot(keys(t), rows_of(i, 0), NT)
         dp = dot(values(t), rows_of(i, 1), NT)
-        s = jnp.where((key >= from_s[i] - t * TILE) & (key <= place_s[i] - t * TILE), s, NEG)
+        ahead = (t - PAD) * BLK
+        s = jnp.where((key >= from_s[i] - ahead) & (key <= place_s[i] - ahead), s, NEG)
         top = jnp.max(jnp.max(s.reshape(TILE // 8, 8, rows), axis=0), axis=0, keepdims=True)
         e = jnp.exp2((s - top) * steep)
         tile_sum = jnp.sum(jnp.sum(e.reshape(TILE // 8, 8, rows), axis=0), axis=0, keepdims=True)
@@ -139,8 +144,9 @@
         ds = (p * (dp_scr[spot] - delta)).astype(jnp.bfloat16)
         ot[old] += dot(values(t).T, pb, NN)
         dqt[old] += dot(keys(t).T, ds, NN)
-        dv[t] += dot(pb, rows_of(old, 1), NN)
-        dk[t] += dot(ds, rows_of(old, 0), NN)
+        at = pl.ds(t, tile_blocks)
+        dv[at] += dot(pb, rows_of(old, 1), NN).reshape(tile_blocks, BLK, HEAD)
+        dk[at] += dot(ds, rows_of(old, 0), NN).reshape(tile_blocks, BLK, HEAD)
 
     def first(u, carry):
         scores(u, u)
@@ -173,8 +179,9 @@
 
     def gone(t, carry):
         at = pl.ds(t * tile_blocks, tile_blocks)
-        dkv[at, 0] = (dk[t] * scale).astype(jnp.bfloat16).reshape(tile_blocks, BLK, HEAD)
-        dkv[at, 1] = dv[t].astype(jnp.bfloat16).reshape(tile_blocks, BLK, HEAD)
+        past = pl.ds(PAD + t * tile_blocks, tile_blocks)
+        dkv[at, 0] = (dk[past] * scale).astype(jnp.bfloat16)
+        dkv[at, 1] = dv[past].astype(jnp.bfloat16)
         return carry
 
     lax.fori_loop(0, tiles, gone, 0, unroll=2)
@@ -200,7 +207,6 @@
     blocks = qd.shape[0] * qd.shape[2]
     group = qd.shape[3]
     slots = len(kv) * kv[0].shape[0] * kv[0].shape[2]
-    tiles = slots * BLK // TILE
     rows = group * BLK
     f32, bf, i32 = jnp.float32, jnp.bfloat16, jnp.int32
     body = functools.partial(attend, docs=lengths.shape[0], slots=slots, group=group, xs=xs, ys=ys, zs=zs)
@@ -212,9 +218,9 @@
         in_specs=[smem] * 3 + [far] * (1 + len(kv)),
         out_specs=[far] * (1 + len(kv)),
         scratch_shapes=[
+            pltpu.VMEM(qd.shape, bf), pltpu.VMEM((PAD + slots, 2, BLK, HEAD), bf),
             pltpu.VMEM(qd.shape, bf), pltpu.VMEM((slots, 2, BLK, HEAD), bf),
-            pltpu.VMEM(qd.shape, bf), pltpu.VMEM((slots, 2, BLK, HEAD), bf),
-            pltpu.VMEM((tiles, TILE, HEAD), f32), pltpu.VMEM((tiles, TILE, HEAD), f32),
+            pltpu.VMEM((PAD + slots, BLK, HEAD), f32), pltpu.VMEM((PAD + slots, BLK, HEAD), f32),
             pltpu.VMEM((blocks, HEAD, rows), f32), pltpu.VMEM((blocks, HEAD, rows), f32),
             pltpu.VMEM((RING, TILE, rows), f32), pltpu.VMEM((RING, TILE, rows), f32),
             pltpu.VMEM((RING, 1, rows), f32),

time: 122 us -> 121 us (level)
  the two profiles are of different devices: /device:TPU:24 before, /device:TPU:8 now
where the time goes in v5:
time: 121 us; the launch traced here: 120 us
  starting transfers between devices  52.4 us (43%)
  waiting for transfers between devices  44.2 us (37%)
  Pallas kernels  21.4 us (18%)
    ppermute x6, starting transfers between devices, over_y(): terms.append(lax.ppermute(dkv[k * zs + w], Y, shift(k, ys)))  19 us
    pallas_call x1, Pallas kernels, attention(): pl.pallas_call(body, out_shape=[jax.ShapeDtypeStruct(a.shape, bf) for a i...  13.9 us
    ppermute x1, waiting for transfers between devices, work(): lax.ppermute(over_y(w).astype(jnp.bfloat16), Z, shift(w, zs))  9.7 us
    ppermute x6, waiting for transfers between devices, over_y(): terms.append(lax.ppermute(dkv[k * zs + w], Y, shift(k, ys)))  9.16 us
    ppermute x3, waiting for transfers between devices, work(): lax.ppermute(part, Y, shift(k, ys))  8.16 us
    ppermute x3, waiting for transfers between devices, work(): own = lax.ppermute(kv[0], Y, shift(k, ys))  7.77 us
    ppermute x1, starting transfers between devices, work(): kv = [kv] + [lax.ppermute(kv, Z, shift(w, zs)) for w in range(1, zs)]  7.28 us
    pallas_call x2, Pallas kernels, spread(): pl.pallas_call(functools.partial(lay_out, xs=xs, per=per, heads=heads, co...  4.95 us
  transfers between devices with their start and end apart: 18, of which 15 were waited for; matrix products, arithmetic and copies ran while one was open for 1% of the time, Pallas kernels for 4%

profile of v5, /device:TPU:8, one launch (start us, length us, event | category | flops | bytes accessed | tf_op | source)
XLA Modules:
  0.0 120.5 jit_solution(11839971226943688692)
XLA Ops:
  0.6 1.7 %spread.3 = bf16[4,2,4,32,128]{4,3,2,1,0:T(8,128)(2,1)} custom-call(bf16[128,512]{1,0:T(8,128)(2,1)} %a_ref.3, bf16[128,512]{1,0:T(8,128)(2,1)} %b_ref.3), custom_call_target="tpu_custom_call" | custom-call | flops 1000000 | bytes 262144 | tf_op jit(solution)/shard_map/spread/pallas_call | solution.py:256
  2.3 4.3 %all-to-all-start.1 = ((bf16[4,2,4,32,128]{4,3,2,1,0:T(8,128)(2,1)}), bf16[4,2,4,32,128]{4,3,2,1,0:T(8,128)(2,1)S(1)}, u32[]{:S(2)}, u32[]{:S(2)}) async-start(bf16[4,2,4,32,128]{4,3,2,1,0:T(8,128)(2,1)} %spread.3), calls=%async_computation.1 | async-start | bytes 524288 | tf_op jit(solution)/shard_map/all_to_all | solution.py:305
  6.6 3.2 %spread.2 = bf16[4,2,4,8,32,128]{5,4,3,2,1,0:T(8,128)(2,1)} custom-call(bf16[128,4096]{1,0:T(8,128)(2,1)} %a_ref.2, bf16[128,4096]{1,0:T(8,128)(2,1)} %b_ref.2), custom_call_target="tpu_custom_call" | custom-call | flops 1000000 | bytes 2097152 | tf_op jit(solution)/shard_map/spread/pallas_call | solution.py:256
  9.9 3.4 %all-to-all-done.1.refs_4_ = bf16[4,2,4,32,128]{4,3,2,1,0:T(8,128)(2,1)S(1)} async-done(((bf16[4,2,4,32,128]{4,3,2,1,0:T(8,128)(2,1)}), bf16[4,2,4,32,128]{4,3,2,1,0:T(8,128)(2,1)S(1)}, u32[]{:S(2)}, u32[]{:S(2)}) %all-to-all-start.1) | async-done | bytes 262176 | tf_op jit(solution)/shard_map/all_to_all | solution.py:305
  13.3 4.4 %all-to-all-start = ((bf16[4,2,4,8,32,128]{5,4,3,2,1,0:T(8,128)(2,1)}), bf16[4,2,4,8,32,128]{5,4,3,2,1,0:T(8,128)(2,1)}, u32[]{:S(2)}, u32[]{:S(2)}) async-start(bf16[4,2,4,8,32,128]{5,4,3,2,1,0:T(8,128)(2,1)} %spread.2), calls=%async_computation | async-start | bytes 4194304 | tf_op jit(solution)/shard_map/all_to_all | solution.py:313
  17.8 7.3 %collective-permute-start = (bf16[4,2,4,32,128]{4,3,2,1,0:T(8,128)(2,1)S(1)}, bf16[4,2,4,32,128]{4,3,2,1,0:T(8,128)(2,1)S(1)}, u32[]{:S(2)}, u32[]{:S(2)}) collective-permute-start(bf16[4,2,4,32,128]{4,3,2,1,0:T(8,128)(2,1)S(1)} %all-to-all-done.1.refs_4_), channel_id=1, source_target_pairs={{0,1},{1,0},{2,3},{3,2},{4,5},{5,4},{6,7},{7,6},{8,9},{9,8},{10,11... | collective-permute-start | bytes 786440 | tf_op jit(solution)/shard_map/ppermute | solution.py:307
  25.5 2.6 %collective-permute-start.3 = (bf16[4,2,4,32,128]{4,3,2,1,0:T(8,128)(2,1)S(1)}, bf16[4,2,4,32,128]{4,3,2,1,0:T(8,128)(2,1)S(1)}, u32[]{:S(2)}, u32[]{:S(2)}) collective-permute-start(bf16[4,2,4,32,128]{4,3,2,1,0:T(8,128)(2,1)S(1)} %all-to-all-done.1.refs_4_), channel_id=1, source_target_pairs={{0,4},{2,6},{4,0},{6,2},{1,5},{3,7},{5,1},{7,3},{8,12},{10,14},{12... | collective-permute-start | bytes 786440 | tf_op jit(solution)/shard_map/ppermute | solution.py:310
  28.1 1.9 %collective-permute-start.1 = (bf16[4,2,4,32,128]{4,3,2,1,0:T(8,128)(2,1)S(1)}, bf16[4,2,4,32,128]{4,3,2,1,0:T(8,128)(2,1)S(1)}, u32[]{:S(2)}, u32[]{:S(2)}) collective-permute-start(bf16[4,2,4,32,128]{4,3,2,1,0:T(8,128)(2,1)S(1)} %all-to-all-done.1.refs_4_), channel_id=1, source_target_pairs={{0,2},{2,4},{4,6},{6,0},{1,3},{3,5},{5,7},{7,1},{8,10},{10,12},{12... | collective-permute-start | bytes 786440 | tf_op jit(solution)/shard_map/ppermute | solution.py:310
  30.0 1.1 collective-permute-done.refs_5_
  31.5 2.6 %collective-permute-start.4 = (bf16[4,2,4,32,128]{4,3,2,1,0:T(8,128)(2,1)S(1)}, bf16[4,2,4,32,128]{4,3,2,1,0:T(8,128)(2,1)S(1)}, u32[]{:S(2)}, u32[]{:S(2)}) collective-permute-start(bf16[4,2,4,32,128]{4,3,2,1,0:T(8,128)(2,1)S(1)} %collective-permute-done.refs_5_), channel_id=1, source_target_pairs={{0,4},{2,6},{4,0},{6,2},{1,5},{3,7},{5,1},{7,3},{8,12},{10,14},{12... | collective-permute-start | bytes 786440 | tf_op jit(solution)/shard_map/ppermute | solution.py:311
  34.1 1.9 %collective-permute-done.5.refs_10_ = bf16[4,2,4,32,128]{4,3,2,1,0:T(8,128)(2,1)S(1)} collective-permute-done((bf16[4,2,4,32,128]{4,3,2,1,0:T(8,128)(2,1)S(1)}, bf16[4,2,4,32,128]{4,3,2,1,0:T(8,128)(2,1)S(1)}, u32[]{:S(2)}, u32[]{:S(2)}) %collective-permute-start.5) | collective-permute-done | bytes 262176 | tf_op jit(solution)/shard_map/ppermute | solution.py:310
  36.0 4.8 %collective-permute-done.3.refs_8_ = bf16[4,2,4,32,128]{4,3,2,1,0:T(8,128)(2,1)S(1)} collective-permute-done((bf16[4,2,4,32,128]{4,3,2,1,0:T(8,128)(2,1)S(1)}, bf16[4,2,4,32,128]{4,3,2,1,0:T(8,128)(2,1)S(1)}, u32[]{:S(2)}, u32[]{:S(2)}) %collective-permute-start.3) | collective-permute-done | bytes 262176 | tf_op jit(solution)/shard_map/ppermute | solution.py:310
  40.9 1.0 collective-permute-done.1.refs_6_
  41.9 2.5 %collective-permute-done.6.refs_11_ = bf16[4,2,4,32,128]{4,3,2,1,0:T(8,128)(2,1)S(1)} collective-permute-done((bf16[4,2,4,32,128]{4,3,2,1,0:T(8,128)(2,1)S(1)}, bf16[4,2,4,32,128]{4,3,2,1,0:T(8,128)(2,1)S(1)}, u32[]{:S(2)}, u32[]{:S(2)}) %collective-permute-start.6) | collective-permute-done | bytes 262176 | tf_op jit(solution)/shard_map/ppermute | solution.py:311
  44.5 4.8 %collective-permute-done.4.refs_9_ = bf16[4,2,4,32,128]{4,3,2,1,0:T(8,128)(2,1)S(1)} collective-permute-done((bf16[4,2,4,32,128]{4,3,2,1,0:T(8,128)(2,1)S(1)}, bf16[4,2,4,32,128]{4,3,2,1,0:T(8,128)(2,1)S(1)}, u32[]{:S(2)}, u32[]{:S(2)}) %collective-permute-start.4) | collective-permute-done | bytes 262176 | tf_op jit(solution)/shard_map/ppermute | solution.py:311
  50.8 13.9 %attend.1 = (bf16[4,2,4,8,32,128]{5,4,3,2,1,0:T(8,128)(2,1)}, bf16[4,2,4,32,128]{4,3,2,1,0:T(8,128)(2,1)}, bf16[4,2,4,32,128]{4,3,2,1,0:T(8,128)(2,1)}, bf16[4,2...) custom-call(s32[128]{0:T(128)} %refs_0_.1, ...), custom_call_target="tpu_custom_call" | custom-call | flops 1000000000 | bytes 8388608 | tf_op jit(solution)/shard_map/attend/pallas_call | solution.py:215
  64.7 4.6 %all-to-all-start.2 = ((bf16[4,2,4,8,32,128]{5,4,3,2,1,0:T(8,128)(2,1)}), bf16[4,2,4,8,32,128]{5,4,3,2,1,0:T(8,128)(2,1)S(1)}, u32[]{:S(2)}, u32[]{:S(2)}) async-start(bf16[4,2,4,8,32,128]{5,4,3,2,1,0:T(8,128)(2,1)} %get-tuple-element.27), calls=%async_computation.2 | async-start | bytes 4194304 | tf_op jit(solution)/shard_map/all_to_all | solution.py:324
  69.3 1.5 %collective-permute-start.10 = (bf16[4,2,4,32,128]{4,3,2,1,0:T(8,128)(2,1)}, bf16[4,2,4,32,128]{4,3,2,1,0:T(8,128)(2,1)S(1)}, u32[]{:S(2)}, u32[]{:S(2)}) collective-permute-start(bf16[4,2,4,32,128]{4,3,2,1,0:T(8,128)(2,1)} %get-tuple-element.24), channel_id=1, source_target_pairs={{0,2},{2,4},{4,6},{6,0},{1,3},{3,5},{5,7},{7,1},{8,10},{10,12},{12... | collective-permute-start | bytes 786440 | tf_op jit(solution)/shard_map/ppermute | solution.py:320
  70.8 5.4 %collective-permute-start.11 = (bf16[4,2,4,32,128]{4,3,2,1,0:T(8,128)(2,1)}, bf16[4,2,4,32,128]{4,3,2,1,0:T(8,128)(2,1)S(1)}, u32[]{:S(2)}, u32[]{:S(2)}) collective-permute-start(bf16[4,2,4,32,128]{4,3,2,1,0:T(8,128)(2,1)} %get-tuple-element.25), channel_id=1, source_target_pairs={{0,4},{2,6},{4,0},{6,2},{1,5},{3,7},{5,1},{7,3},{8,12},{10,14},{12... | collective-permute-start | bytes 786440 | tf_op jit(solution)/shard_map/ppermute | solution.py:320
  76.6 1.6 %collective-permute-start.7 = (bf16[4,2,4,32,128]{4,3,2,1,0:T(8,128)(2,1)S(1)}, bf16[4,2,4,32,128]{4,3,2,1,0:T(8,128)(2,1)S(1)}, u32[]{:S(2)}, u32[]{:S(2)}) collective-permute-start(bf16[4,2,4,32,128]{4,3,2,1,0:T(8,128)(2,1)S(1)} %copy-done.12), channel_id=1, source_target_pairs={{0,2},{2,4},{4,6},{6,0},{1,3},{3,5},{5,7},{7,1},{8,10},{10,12},{12... | collective-permute-start | bytes 786440 | tf_op jit(solution)/shard_map/ppermute | solution.py:320
  78.2 1.2 %collective-permute-start.8 = (bf16[4,2,4,32,128]{4,3,2,1,0:T(8,128)(2,1)S(1)}, bf16[4,2,4,32,128]{4,3,2,1,0:T(8,128)(2,1)S(1)}, u32[]{:S(2)}, u32[]{:S(2)}) collective-permute-start(bf16[4,2,4,32,128]{4,3,2,1,0:T(8,128)(2,1)S(1)} %copy-done.11), channel_id=1, source_target_pairs={{0,4},{2,6},{4,0},{6,2},{1,5},{3,7},{5,1},{7,3},{8,12},{10,14},{12... | collective-permute-start | bytes 786440 | tf_op jit(solution)/shard_map/ppermute | solution.py:320
  79.4 2.0 %collective-permute-done.10 = bf16[4,2,4,32,128]{4,3,2,1,0:T(8,128)(2,1)S(1)} collective-permute-done((bf16[4,2,4,32,128]{4,3,2,1,0:T(8,128)(2,1)}, bf16[4,2,4,32,128]{4,3,2,1,0:T(8,128)(2,1)S(1)}, u32[]{:S(2)}, u32[]{:S(2)}) %collective-permute-start.10) | collective-permute-done | bytes 262176 | tf_op jit(solution)/shard_map/ppermute | solution.py:320
  81.5 8.8 %collective-permute-start.9 = (bf16[4,2,4,32,128]{4,3,2,1,0:T(8,128)(2,1)S(1)}, bf16[4,2,4,32,128]{4,3,2,1,0:T(8,128)(2,1)S(1)}, u32[]{:S(2)}, u32[]{:S(2)}) collective-permute-start(bf16[4,2,4,32,128]{4,3,2,1,0:T(8,128)(2,1)S(1)} %copy-done.10), channel_id=1, source_target_pairs={{0,6},{2,0},{4,2},{6,4},{1,7},{3,1},{5,3},{7,5},{8,14},{10,8},{12,... | collective-permute-start | bytes 786440 | tf_op jit(solution)/shard_map/ppermute | solution.py:320
  90.3 0.9 collective-permute-done.12
  91.4 1.3 %collective-permute-done.7 = bf16[4,2,4,32,128]{4,3,2,1,0:T(8,128)(2,1)S(1)} collective-permute-done((bf16[4,2,4,32,128]{4,3,2,1,0:T(8,128)(2,1)S(1)}, bf16[4,2,4,32,128]{4,3,2,1,0:T(8,128)(2,1)S(1)}, u32[]{:S(2)}, u32[]{:S(2)}) %collective-permute-start.7) | collective-permute-done | bytes 262176 | tf_op jit(solution)/shard_map/ppermute | solution.py:320
  92.7 2.1 %collective-permute-done.8 = bf16[4,2,4,32,128]{4,3,2,1,0:T(8,128)(2,1)S(1)} collective-permute-done((bf16[4,2,4,32,128]{4,3,2,1,0:T(8,128)(2,1)S(1)}, bf16[4,2,4,32,128]{4,3,2,1,0:T(8,128)(2,1)S(1)}, u32[]{:S(2)}, u32[]{:S(2)}) %collective-permute-start.8) | collective-permute-done | bytes 262176 | tf_op jit(solution)/shard_map/ppermute | solution.py:320
  94.8 2.9 %collective-permute-done.9 = bf16[4,2,4,32,128]{4,3,2,1,0:T(8,128)(2,1)S(1)} collective-permute-done((bf16[4,2,4,32,128]{4,3,2,1,0:T(8,128)(2,1)S(1)}, bf16[4,2,4,32,128]{4,3,2,1,0:T(8,128)(2,1)S(1)}, u32[]{:S(2)}, u32[]{:S(2)}) %collective-permute-start.9) | collective-permute-done | bytes 262176 | tf_op jit(solution)/shard_map/ppermute | solution.py:320
  97.7 9.7 %collective-permute-done.13 = bf16[4,2,4,32,128]{4,3,2,1,0:T(8,128)(2,1)S(1)} collective-permute-done((bf16[4,2,4,32,128]{4,3,2,1,0:T(8,128)(2,1)S(1)}, bf16[4,2,4,32,128]{4,3,2,1,0:T(8,128)(2,1)S(1)}, u32[]{:S(2)}, u32[]{:S(2)}) %collective-permute-start.13) | collective-permute-done | bytes 262176 | tf_op jit(solution)/shard_map/ppermute | solution.py:323
  107.4 0.9 add_convert_fusion
  108.2 4.8 %all-to-all-start.3 = ((bf16[4,2,4,32,128]{4,3,2,1,0:T(8,128)(2,1)}), bf16[4,2,4,32,128]{4,3,2,1,0:T(8,128)(2,1)S(1)}, u32[]{:S(2)}, u32[]{:S(2)}) async-start(bf16[4,2,4,32,128]{4,3,2,1,0:T(8,128)(2,1)} %add_convert_fusion), calls=%async_computation.3 | async-start | bytes 524288 | tf_op jit(solution)/shard_map/all_to_all | solution.py:327
  113.0 1.9 %gather.2 = (bf16[128,4096]{1,0:T(8,128)(2,1)}, bf16[128,4096]{1,0:T(8,128)(2,1)}) custom-call(bf16[4,2,4,8,32,128]{5,4,3,2,1,0:T(8,128)(2,1)S(1)} %all-to-all-done.2.a_ref), custom_call_target="tpu_custom_call" | custom-call | flops 1000000 | bytes 2097152 | tf_op jit(solution)/shard_map/gather/pallas_call | solution.py:283
  114.9 4.8 %all-to-all-done.3.a_ref = bf16[4,2,4,32,128]{4,3,2,1,0:T(8,128)(2,1)S(1)} async-done(((bf16[4,2,4,32,128]{4,3,2,1,0:T(8,128)(2,1)}), bf16[4,2,4,32,128]{4,3,2,1,0:T(8,128)(2,1)S(1)}, u32[]{:S(2)}, u32[]{:S(2)}) %all-to-all-start.3) | async-done | bytes 262176 | tf_op jit(solution)/shard_map/all_to_all | solution.py:327
  (37 shorter events, 3.8 us)
Async XLA Ops:
  2.3 11.0 %all-to-all-start.1 = ((bf16[4,2,4,32,128]{4,3,2,1,0:T(8,128)(2,1)}), bf16[4,2,4,32,128]{4,3,2,1,0:T(8,128)(2,1)S(1)}, u32[]{:S(2)}, u32[]{:S(2)}) async-start(bf16[4,2,4,32,128]{4,3,2,1,0:T(8,128)(2,1)} %spread.3), calls=%async_computation.1 | async-start | bytes 524288 | tf_op jit(solution)/shard_map/all_to_all | solution.py:305
  13.3 14.8 %copy-start = (bf16[4,2,4,32,128]{4,3,2,1,0:T(8,128)(2,1)}, bf16[4,2,4,32,128]{4,3,2,1,0:T(8,128)(2,1)S(1)}, u32[]{:S(2)}) copy-start(bf16[4,2,4,32,128]{4,3,2,1,0:T(8,128)(2,1)S(1)} %all-to-all-done.1.refs_4_) | copy-start | bytes 786436
  13.3 36.8 %all-to-all-start = ((bf16[4,2,4,8,32,128]{5,4,3,2,1,0:T(8,128)(2,1)}), bf16[4,2,4,8,32,128]{5,4,3,2,1,0:T(8,128)(2,1)}, u32[]{:S(2)}, u32[]{:S(2)}) async-start(bf16[4,2,4,8,32,128]{5,4,3,2,1,0:T(8,128)(2,1)} %spread.2), calls=%async_computation | async-start | bytes 4194304 | tf_op jit(solution)/shard_map/all_to_all | solution.py:313
  17.8 13.3 %collective-permute-start = (bf16[4,2,4,32,128]{4,3,2,1,0:T(8,128)(2,1)S(1)}, bf16[4,2,4,32,128]{4,3,2,1,0:T(8,128)(2,1)S(1)}, u32[]{:S(2)}, u32[]{:S(2)}) collective-permute-start(bf16[4,2,4,32,128]{4,3,2,1,0:T(8,128)(2,1)S(1)} %all-to-all-done.1.refs_4_), channel_id=1, source_target_pairs={{0,1},{1,0},{2,3},{3,2},{4,5},{5,4},{6,7},{7,6},{8,9},{9,8},{10,11... | collective-permute-start | bytes 786440 | tf_op jit(solution)/shard_map/ppermute | solution.py:307
  25.0 11.0 %collective-permute-start.5 = (bf16[4,2,4,32,128]{4,3,2,1,0:T(8,128)(2,1)S(1)}, bf16[4,2,4,32,128]{4,3,2,1,0:T(8,128)(2,1)S(1)}, u32[]{:S(2)}, u32[]{:S(2)}) collective-permute-start(bf16[4,2,4,32,128]{4,3,2,1,0:T(8,128)(2,1)S(1)} %all-to-all-done.1.refs_4_), channel_id=1, source_target_pairs={{0,6},{2,0},{4,2},{6,4},{1,7},{3,1},{5,3},{7,5},{8,14},{10,8},{12,... | collective-permute-start | bytes 786440 | tf_op jit(solution)/shard_map/ppermute | solution.py:310
  25.5 15.4 %collective-permute-start.3 = (bf16[4,2,4,32,128]{4,3,2,1,0:T(8,128)(2,1)S(1)}, bf16[4,2,4,32,128]{4,3,2,1,0:T(8,128)(2,1)S(1)}, u32[]{:S(2)}, u32[]{:S(2)}) collective-permute-start(bf16[4,2,4,32,128]{4,3,2,1,0:T(8,128)(2,1)S(1)} %all-to-all-done.1.refs_4_), channel_id=1, source_target_pairs={{0,4},{2,6},{4,0},{6,2},{1,5},{3,7},{5,1},{7,3},{8,12},{10,14},{12... | collective-permute-start | bytes 786440 | tf_op jit(solution)/shard_map/ppermute | solution.py:310
  28.1 13.8 %collective-permute-start.1 = (bf16[4,2,4,32,128]{4,3,2,1,0:T(8,128)(2,1)S(1)}, bf16[4,2,4,32,128]{4,3,2,1,0:T(8,128)(2,1)S(1)}, u32[]{:S(2)}, u32[]{:S(2)}) collective-permute-start(bf16[4,2,4,32,128]{4,3,2,1,0:T(8,128)(2,1)S(1)} %all-to-all-done.1.refs_4_), channel_id=1, source_target_pairs={{0,2},{2,4},{4,6},{6,0},{1,3},{3,5},{5,7},{7,1},{8,10},{10,12},{12... | collective-permute-start | bytes 786440 | tf_op jit(solution)/shard_map/ppermute | solution.py:310
  31.1 19.7 %copy-start.1 = (bf16[4,2,4,32,128]{4,3,2,1,0:T(8,128)(2,1)}, bf16[4,2,4,32,128]{4,3,2,1,0:T(8,128)(2,1)S(1)}, u32[]{:S(2)}) copy-start(bf16[4,2,4,32,128]{4,3,2,1,0:T(8,128)(2,1)S(1)} %collective-permute-done.refs_5_) | copy-start | bytes 786436
  31.1 13.4 %collective-permute-start.6 = (bf16[4,2,4,32,128]{4,3,2,1,0:T(8,128)(2,1)S(1)}, bf16[4,2,4,32,128]{4,3,2,1,0:T(8,128)(2,1)S(1)}, u32[]{:S(2)}, u32[]{:S(2)}) collective-permute-start(bf16[4,2,4,32,128]{4,3,2,1,0:T(8,128)(2,1)S(1)} %collective-permute-done.refs_5_), channel_id=1, source_target_pairs={{0,6},{2,0},{4,2},{6,4},{1,7},{3,1},{5,3},{7,5},{8,14},{10,8},{12,... | collective-permute-start | bytes 786440 | tf_op jit(solution)/shard_map/ppermute | solution.py:311
  31.5 17.7 %collective-permute-start.4 = (bf16[4,2,4,32,128]{4,3,2,1,0:T(8,128)(2,1)S(1)}, bf16[4,2,4,32,128]{4,3,2,1,0:T(8,128)(2,1)S(1)}, u32[]{:S(2)}, u32[]{:S(2)}) collective-permute-start(bf16[4,2,4,32,128]{4,3,2,1,0:T(8,128)(2,1)S(1)} %collective-permute-done.refs_5_), channel_id=1, source_target_pairs={{0,4},{2,6},{4,0},{6,2},{1,5},{3,7},{5,1},{7,3},{8,12},{10,14},{12... | collective-permute-start | bytes 786440 | tf_op jit(solution)/shard_map/ppermute | solution.py:311
  36.0 14.8 %copy-start.2 = (bf16[4,2,4,32,128]{4,3,2,1,0:T(8,128)(2,1)}, bf16[4,2,4,32,128]{4,3,2,1,0:T(8,128)(2,1)S(1)}, u32[]{:S(2)}) copy-start(bf16[4,2,4,32,128]{4,3,2,1,0:T(8,128)(2,1)S(1)} %collective-permute-done.5.refs_10_) | copy-start | bytes 786436
  36.0 14.0 %collective-permute-start.2 = (bf16[4,2,4,32,128]{4,3,2,1,0:T(8,128)(2,1)S(1)}, bf16[4,2,4,32,128]{4,3,2,1,0:T(8,128)(2,1)S(1)}, u32[]{:S(2)}, u32[]{:S(2)}) collective-permute-start(bf16[4,2,4,32,128]{4,3,2,1,0:T(8,128)(2,1)S(1)} %collective-permute-done.refs_5_), channel_id=1, source_target_pairs={{0,2},{2,4},{4,6},{6,0},{1,3},{3,5},{5,7},{7,1},{8,10},{10,12},{12... | collective-permute-start | bytes 786440 | tf_op jit(solution)/shard_map/ppermute | solution.py:311
  40.9 9.9 %copy-start.3 = (bf16[4,2,4,32,128]{4,3,2,1,0:T(8,128)(2,1)}, bf16[4,2,4,32,128]{4,3,2,1,0:T(8,128)(2,1)S(1)}, u32[]{:S(2)}) copy-start(bf16[4,2,4,32,128]{4,3,2,1,0:T(8,128)(2,1)S(1)} %collective-permute-done.3.refs_8_) | copy-start | bytes 786436
  41.9 8.2 %copy-start.4 = (bf16[4,2,4,32,128]{4,3,2,1,0:T(8,128)(2,1)}, bf16[4,2,4,32,128]{4,3,2,1,0:T(8,128)(2,1)S(1)}, u32[]{:S(2)}) copy-start(bf16[4,2,4,32,128]{4,3,2,1,0:T(8,128)(2,1)S(1)} %collective-permute-done.1.refs_6_) | copy-start | bytes 786436
  44.5 5.6 %copy-start.5 = (bf16[4,2,4,32,128]{4,3,2,1,0:T(8,128)(2,1)}, bf16[4,2,4,32,128]{4,3,2,1,0:T(8,128)(2,1)S(1)}, u32[]{:S(2)}) copy-start(bf16[4,2,4,32,128]{4,3,2,1,0:T(8,128)(2,1)S(1)} %collective-permute-done.6.refs_11_) | copy-start | bytes 786436
  49.3 0.8 copy-start.6
  50.1 0.7 copy-start.8
  64.7 12.0 %copy-start.12 = (bf16[4,2,4,32,128]{4,3,2,1,0:T(8,128)(2,1)S(1)}, bf16[4,2,4,32,128]{4,3,2,1,0:T(8,128)(2,1)}, u32[]{:S(2)}) copy-start(bf16[4,2,4,32,128]{4,3,2,1,0:T(8,128)(2,1)} %get-tuple-element.20) | copy-start | bytes 786436
  64.7 13.6 %copy-start.11 = (bf16[4,2,4,32,128]{4,3,2,1,0:T(8,128)(2,1)S(1)}, bf16[4,2,4,32,128]{4,3,2,1,0:T(8,128)(2,1)}, u32[]{:S(2)}) copy-start(bf16[4,2,4,32,128]{4,3,2,1,0:T(8,128)(2,1)} %get-tuple-element.21) | copy-start | bytes 786436
  64.7 16.8 %copy-start.10 = (bf16[4,2,4,32,128]{4,3,2,1,0:T(8,128)(2,1)S(1)}, bf16[4,2,4,32,128]{4,3,2,1,0:T(8,128)(2,1)}, u32[]{:S(2)}) copy-start(bf16[4,2,4,32,128]{4,3,2,1,0:T(8,128)(2,1)} %get-tuple-element.22) | copy-start | bytes 786436
  64.7 26.5 %copy-start.7 = (bf16[4,2,4,32,128]{4,3,2,1,0:T(8,128)(2,1)S(1)}, bf16[4,2,4,32,128]{4,3,2,1,0:T(8,128)(2,1)}, u32[]{:S(2)}) copy-start(bf16[4,2,4,32,128]{4,3,2,1,0:T(8,128)(2,1)} %get-tuple-element.23) | copy-start | bytes 786436
  64.7 42.7 %copy-start.9 = (bf16[4,2,4,32,128]{4,3,2,1,0:T(8,128)(2,1)S(1)}, bf16[4,2,4,32,128]{4,3,2,1,0:T(8,128)(2,1)}, u32[]{:S(2)}) copy-start(bf16[4,2,4,32,128]{4,3,2,1,0:T(8,128)(2,1)} %get-tuple-element.19) | copy-start | bytes 786436
  64.7 43.5 %all-to-all-start.2 = ((bf16[4,2,4,8,32,128]{5,4,3,2,1,0:T(8,128)(2,1)}), bf16[4,2,4,8,32,128]{5,4,3,2,1,0:T(8,128)(2,1)S(1)}, u32[]{:S(2)}, u32[]{:S(2)}) async-start(bf16[4,2,4,8,32,128]{5,4,3,2,1,0:T(8,128)(2,1)} %get-tuple-element.27), calls=%async_computation.2 | async-start | bytes 4194304 | tf_op jit(solution)/shard_map/all_to_all | solution.py:324
  69.3 12.2 %collective-permute-start.10 = (bf16[4,2,4,32,128]{4,3,2,1,0:T(8,128)(2,1)}, bf16[4,2,4,32,128]{4,3,2,1,0:T(8,128)(2,1)S(1)}, u32[]{:S(2)}, u32[]{:S(2)}) collective-permute-start(bf16[4,2,4,32,128]{4,3,2,1,0:T(8,128)(2,1)} %get-tuple-element.24), channel_id=1, source_target_pairs={{0,2},{2,4},{4,6},{6,0},{1,3},{3,5},{5,7},{7,1},{8,10},{10,12},{12... | collective-permute-start | bytes 786440 | tf_op jit(solution)/shard_map/ppermute | solution.py:320
  70.8 19.5 %collective-permute-start.11 = (bf16[4,2,4,32,128]{4,3,2,1,0:T(8,128)(2,1)}, bf16[4,2,4,32,128]{4,3,2,1,0:T(8,128)(2,1)S(1)}, u32[]{:S(2)}, u32[]{:S(2)}) collective-permute-start(bf16[4,2,4,32,128]{4,3,2,1,0:T(8,128)(2,1)} %get-tuple-element.25), channel_id=1, source_target_pairs={{0,4},{2,6},{4,0},{6,2},{1,5},{3,7},{5,1},{7,3},{8,12},{10,14},{12... | collective-permute-start | bytes 786440 | tf_op jit(solution)/shard_map/ppermute | solution.py:320
  76.2 15.0 %collective-permute-start.12 = (bf16[4,2,4,32,128]{4,3,2,1,0:T(8,128)(2,1)}, bf16[4,2,4,32,128]{4,3,2,1,0:T(8,128)(2,1)S(1)}, u32[]{:S(2)}, u32[]{:S(2)}) collective-permute-start(bf16[4,2,4,32,128]{4,3,2,1,0:T(8,128)(2,1)} %get-tuple-element.26), channel_id=1, source_target_pairs={{0,6},{2,0},{4,2},{6,4},{1,7},{3,1},{5,3},{7,5},{8,14},{10,8},{12,... | collective-permute-start | bytes 786440 | tf_op jit(solution)/shard_map/ppermute | solution.py:320
  76.6 16.1 %collective-permute-start.7 = (bf16[4,2,4,32,128]{4,3,2,1,0:T(8,128)(2,1)S(1)}, bf16[4,2,4,32,128]{4,3,2,1,0:T(8,128)(2,1)S(1)}, u32[]{:S(2)}, u32[]{:S(2)}) collective-permute-start(bf16[4,2,4,32,128]{4,3,2,1,0:T(8,128)(2,1)S(1)} %copy-done.12), channel_id=1, source_target_pairs={{0,2},{2,4},{4,6},{6,0},{1,3},{3,5},{5,7},{7,1},{8,10},{10,12},{12... | collective-permute-start | bytes 786440 | tf_op jit(solution)/shard_map/ppermute | solution.py:320
  78.2 16.6 %collective-permute-start.8 = (bf16[4,2,4,32,128]{4,3,2,1,0:T(8,128)(2,1)S(1)}, bf16[4,2,4,32,128]{4,3,2,1,0:T(8,128)(2,1)S(1)}, u32[]{:S(2)}, u32[]{:S(2)}) collective-permute-start(bf16[4,2,4,32,128]{4,3,2,1,0:T(8,128)(2,1)S(1)} %copy-done.11), channel_id=1, source_target_pairs={{0,4},{2,6},{4,0},{6,2},{1,5},{3,7},{5,1},{7,3},{8,12},{10,14},{12... | collective-permute-start | bytes 786440 | tf_op jit(solution)/shard_map/ppermute | solution.py:320
  81.5 16.2 %collective-permute-start.9 = (bf16[4,2,4,32,128]{4,3,2,1,0:T(8,128)(2,1)S(1)}, bf16[4,2,4,32,128]{4,3,2,1,0:T(8,128)(2,1)S(1)}, u32[]{:S(2)}, u32[]{:S(2)}) collective-permute-start(bf16[4,2,4,32,128]{4,3,2,1,0:T(8,128)(2,1)S(1)} %copy-done.10), channel_id=1, source_target_pairs={{0,6},{2,0},{4,2},{6,4},{1,7},{3,1},{5,3},{7,5},{8,14},{10,8},{12,... | collective-permute-start | bytes 786440 | tf_op jit(solution)/shard_map/ppermute | solution.py:320
  91.3 16.0 %collective-permute-start.13 = (bf16[4,2,4,32,128]{4,3,2,1,0:T(8,128)(2,1)S(1)}, bf16[4,2,4,32,128]{4,3,2,1,0:T(8,128)(2,1)S(1)}, u32[]{:S(2)}, u32[]{:S(2)}) collective-permute-start(bf16[4,2,4,32,128]{4,3,2,1,0:T(8,128)(2,1)S(1)} %add_convert_fusion.1), channel_id=1, source_target_pairs={{0,1},{1,0},{2,3},{3,2},{4,5},{5,4},{6,7},{7,6},{8,9},{9,8},{10,11... | collective-permute-start | bytes 786440 | tf_op jit(solution)/shard_map/ppermute | solution.py:323
  108.2 11.5 %all-to-all-start.3 = ((bf16[4,2,4,32,128]{4,3,2,1,0:T(8,128)(2,1)}), bf16[4,2,4,32,128]{4,3,2,1,0:T(8,128)(2,1)S(1)}, u32[]{:S(2)}, u32[]{:S(2)}) async-start(bf16[4,2,4,32,128]{4,3,2,1,0:T(8,128)(2,1)} %add_convert_fusion), calls=%async_computation.3 | async-start | bytes 524288 | tf_op jit(solution)/shard_map/all_to_all | solution.py:327
